TPU v7x, 32 devices: a whole 2x2x4 slice. The times are simulated.
32 devices in a mesh: tp: 32 (over z, y, x, core).
Axes of the slice: x: 2, y: 2, z: 4, core: 2. Of those that a mesh axis runs over, the one named last changes fastest.
Arguments:
- x_input: bfloat16 [1, 3072, 4096], P(None, 'tp')
- w_query: bfloat16 [4096, 4096], P(None, 'tp')
- w_key: bfloat16 [4096, 4096], P(None, 'tp')
- w_value: bfloat16 [4096, 4096], P(None, 'tp')
- w_out: bfloat16 [4096, 4096], P('tp')
- g_query: bfloat16 [4096], P('tp')
- g_key: bfloat16 [4096], P('tp')
- g_attn: bfloat16 [4096], replicated
- grad_y: bfloat16 [1, 3072, 4096], P(None, 'tp')
Outputs:
- output 1: bfloat16 [1, 3072, 4096], P(None, 'tp')
- output 2: bfloat16 [1, 3072, 4096], P(None, 'tp')
- output 3: bfloat16 [4096, 4096], P(None, 'tp')
- output 4: bfloat16 [4096, 4096], P(None, 'tp')
- output 5: bfloat16 [4096, 4096], P(None, 'tp')
- output 6: bfloat16 [4096, 4096], P('tp')
- output 7: bfloat16 [4096], P('tp')
- output 8: bfloat16 [4096], P('tp')
- output 9: bfloat16 [4096], replicated
All inputs are finite; a program needn't handle non-finite values.
Results may differ from a plain program's by a relative error of at most 0.0172326.
Values are sent between devices in bfloat16 or wider.
A program may use at most 1 GiB of HBM per device.

v0:
```python
import jax
import jax.numpy as jnp
from jax import lax
from jax.sharding import PartitionSpec as P

HEAD_SIZE = 128
ROPE_THETA = 500000.0
NORM_EPS = 1e-6


def rope_tables(seq_len):
    half_dim = HEAD_SIZE // 2
    inv_freq = 1.0 / (ROPE_THETA ** (jnp.arange(half_dim, dtype=jnp.float32) / half_dim))
    angles = jnp.arange(seq_len, dtype=jnp.float32)[:, None] * inv_freq[None, :]
    return jnp.cos(angles)[:, None, :], jnp.sin(angles)[:, None, :]


def rotate(values, cos_t, sin_t):
    lower_half, upper_half = jnp.split(values, 2, axis=-1)
    return jnp.concatenate([lower_half * cos_t - upper_half * sin_t, upper_half * cos_t + lower_half * sin_t], axis=-1)


def rotate_back(values, cos_t, sin_t):
    lower_half, upper_half = jnp.split(values, 2, axis=-1)
    return jnp.concatenate([lower_half * cos_t + upper_half * sin_t, upper_half * cos_t - lower_half * sin_t], axis=-1)


def local_block(x_loc, wq_loc, wk_loc, wv_loc, wo_loc, gq_loc, gk_loc, g_attn, dy_loc):
    batch_size, seq_loc, model_dim = x_loc.shape
    local_dim = wq_loc.shape[1]
    x_full = lax.all_gather(x_loc, 'tp', axis=1, tiled=True)
    seq_len = x_full.shape[1]
    head_shape = (batch_size, seq_len, local_dim // HEAD_SIZE, HEAD_SIZE)
    flat_shape = (batch_size, seq_len, local_dim)
    cos_t, sin_t = rope_tables(seq_len)
    causal = jnp.arange(seq_len)[:, None] >= jnp.arange(seq_len)[None, :]
    attn_scale = HEAD_SIZE ** -0.5
    q_raw = jnp.einsum('bsd,de->bse', x_full, wq_loc, preferred_element_type=jnp.float32)
    k_raw = jnp.einsum('bsd,de->bse', x_full, wk_loc, preferred_element_type=jnp.float32)
    v_heads = jnp.einsum('bsd,de->bse', x_full, wv_loc, preferred_element_type=jnp.float32).astype(jnp.bfloat16).reshape(head_shape)
    sq_sums = lax.psum(jnp.stack([jnp.sum(q_raw * q_raw, axis=-1), jnp.sum(k_raw * k_raw, axis=-1)]), 'tp')
    inv_rms = lax.rsqrt(sq_sums / model_dim + NORM_EPS)[..., None]
    q_unit = q_raw * inv_rms[0]
    k_unit = k_raw * inv_rms[1]
    gq_f = gq_loc.astype(jnp.float32)
    gk_f = gk_loc.astype(jnp.float32)
    q_rot = rotate((q_unit * gq_f).reshape(head_shape), cos_t, sin_t).astype(jnp.bfloat16)
    k_rot = rotate((k_unit * gk_f).reshape(head_shape), cos_t, sin_t).astype(jnp.bfloat16)
    scores = jnp.einsum('bqhd,bkhd->bhqk', q_rot, k_rot, preferred_element_type=jnp.float32) * attn_scale
    attn_probs = jax.nn.softmax(jnp.where(causal, scores, -1e30), axis=-1)
    probs_low = attn_probs.astype(jnp.bfloat16)
    attn_heads = jnp.einsum('bhqk,bkhd->bqhd', probs_low, v_heads, preferred_element_type=jnp.float32).astype(jnp.bfloat16).reshape(flat_shape)
    attn_part = jnp.einsum('bse,ed->bsd', attn_heads, wo_loc, preferred_element_type=jnp.float32)
    attn_loc = lax.psum_scatter(attn_part, 'tp', scatter_dimension=1, tiled=True)
    post_rms = lax.rsqrt(jnp.mean(attn_loc * attn_loc, axis=-1, keepdims=True) + NORM_EPS)
    normed = attn_loc * post_rms
    ga_f = g_attn.astype(jnp.float32)
    dy_f = dy_loc.astype(jnp.float32)
    y_loc = (x_loc.astype(jnp.float32) + normed * ga_f).astype(jnp.bfloat16)

    grad_ga = lax.psum(jnp.sum(dy_f * normed, axis=(0, 1)), 'tp')
    g_normed = dy_f * ga_f
    d_attn = post_rms * (g_normed - normed * jnp.mean(g_normed * normed, axis=-1, keepdims=True))
    d_attn_full = lax.all_gather(d_attn.astype(jnp.bfloat16), 'tp', axis=1, tiled=True)
    grad_wo = jnp.einsum('bse,bsd->ed', attn_heads, d_attn_full, preferred_element_type=jnp.float32)
    d_heads = jnp.einsum('bsd,ed->bse', d_attn_full, wo_loc, preferred_element_type=jnp.float32).astype(jnp.bfloat16).reshape(head_shape)
    d_probs = jnp.einsum('bqhd,bkhd->bhqk', d_heads, v_heads, preferred_element_type=jnp.float32)
    d_value = jnp.einsum('bhqk,bqhd->bkhd', probs_low, d_heads, preferred_element_type=jnp.float32).astype(jnp.bfloat16).reshape(flat_shape)
    d_scores = (attn_probs * (d_probs - jnp.sum(attn_probs * d_probs, axis=-1, keepdims=True)) * attn_scale).astype(jnp.bfloat16)
    dq_rot = jnp.einsum('bhqk,bkhd->bqhd', d_scores, k_rot, preferred_element_type=jnp.float32)
    dk_rot = jnp.einsum('bhqk,bqhd->bkhd', d_scores, q_rot, preferred_element_type=jnp.float32)
    dq_hat = rotate_back(dq_rot, cos_t, sin_t).reshape(flat_shape)
    dk_hat = rotate_back(dk_rot, cos_t, sin_t).reshape(flat_shape)
    grad_gq = jnp.sum(dq_hat * q_unit, axis=(0, 1))
    grad_gk = jnp.sum(dk_hat * k_unit, axis=(0, 1))
    dq_unit = dq_hat * gq_f
    dk_unit = dk_hat * gk_f
    unit_dots = lax.psum(jnp.stack([jnp.sum(dq_unit * q_unit, axis=-1), jnp.sum(dk_unit * k_unit, axis=-1)]), 'tp')[..., None] / model_dim
    dq_raw = (inv_rms[0] * (dq_unit - q_unit * unit_dots[0])).astype(jnp.bfloat16)
    dk_raw = (inv_rms[1] * (dk_unit - k_unit * unit_dots[1])).astype(jnp.bfloat16)
    grad_wq = jnp.einsum('bsd,bse->de', x_full, dq_raw, preferred_element_type=jnp.float32)
    grad_wk = jnp.einsum('bsd,bse->de', x_full, dk_raw, preferred_element_type=jnp.float32)
    grad_wv = jnp.einsum('bsd,bse->de', x_full, d_value, preferred_element_type=jnp.float32)
    dx_part = (jnp.einsum('bse,de->bsd', dq_raw, wq_loc, preferred_element_type=jnp.float32)
               + jnp.einsum('bse,de->bsd', dk_raw, wk_loc, preferred_element_type=jnp.float32)
               + jnp.einsum('bse,de->bsd', d_value, wv_loc, preferred_element_type=jnp.float32))
    grad_x = lax.psum_scatter(dx_part, 'tp', scatter_dimension=1, tiled=True) + dy_f
    return (y_loc, grad_x.astype(jnp.bfloat16), grad_wq.astype(jnp.bfloat16), grad_wk.astype(jnp.bfloat16),
            grad_wv.astype(jnp.bfloat16), grad_wo.astype(jnp.bfloat16), grad_gq.astype(jnp.bfloat16),
            grad_gk.astype(jnp.bfloat16), grad_ga.astype(jnp.bfloat16))


def solution(mesh):
    act_spec = P(None, 'tp', None)
    col_spec = P(None, 'tp')
    row_spec = P('tp', None)
    vec_spec = P('tp')
    in_specs = (act_spec, col_spec, col_spec, col_spec, row_spec, vec_spec, vec_spec, P(), act_spec)
    out_specs = (act_spec, act_spec, col_spec, col_spec, col_spec, row_spec, vec_spec, vec_spec, P())
    return jax.shard_map(local_block, mesh=mesh, in_specs=in_specs, out_specs=out_specs, check_vma=False)
```

profile of v0, /device:TPU:0, one launch (start us, length us, event | category | flops | bytes accessed | tf_op | source)
XLA Modules:
  0.0 1595.4 jit_solution(6279381490521560726)
XLA Ops:
  7.2 0.0 copy-start
  7.2 0.0 all-gather.3.cloned.1.call-start
  7.2 0.7 all-gather.3.cloned.1.call-update
  7.9 0.0 reduce-scatter.3.cloned.1.call-start
  8.0 0.7 convert_element_type.108
  8.6 0.7 convert_element_type.109
  9.3 157.7 %all-gather.3.cloned.1.call-done = bf16[1,3072,4096]{2,1,0:T(8,128)(2,1)} async-done(((bf16[1,96,4096]{2,1,0:T(8,128)(2,1)}), bf16[1,3072,4096]{2,1,0:T(8,128)(2,1)}) %all-gather.3.cloned.1.call-update) | async-done | bytes 25165840 | tf_op jit(solution)/shard_map/all_gather | solution.py:31
  167.0 13.5 multiply_reduce_fusion.7
  180.5 15.1 multiply_reduce_fusion.6
  195.6 38.9 %psum.21 = f32[2,1,3072]{2,1,0:T(1,128)S(1)} all-reduce(f32[2,1,3072]{2,1,0:T(1,128)S(1)} %pad_maximum_fusion.6), channel_id=1, replica_groups=mesh['tp'=32] {'tp'}, use_global_device_ids=true, to_apply=%region_2.0 | all-reduce | flops 6144 | bytes 49152 | tf_op jit(solution)/shard_map/psum | solution.py:41
  234.6 1.9 multiply_bitcast_fusion
  236.5 3.5 fusion.72
  240.1 0.0 copy-start.20
  240.1 0.0 copy-start.22
  240.1 14.6 fusion.18
  254.7 0.0 copy-start.24
  254.7 17.0 %fusion.1 = f32[3072]{0:T(1024)S(1)} fusion(f32[3072,3072]{0,1:T(8,128)} %get-tuple-element.49, f32[3072]{0:T(1024)S(1)} %get-tuple-element.48), kind=kLoop, calls=%fused_computation.7 | loop fusion | flops 47182848 | bytes 37773312 | tf_op jit(solution)/shard_map/reduce_sum | solution.py:50
  271.8 11.7 fusion.50
  283.5 0.0 copy-start.38
  283.5 0.9 copy-done.38
  284.4 17.6 %fusion.59 = bf16[3072,128]{0,1:T(8,128)(2,1)S(1)} fusion(bf16[3072,128]{1,0:T(8,128)(2,1)S(1)} %fusion.50, f32[3072,3072]{0,1:T(8,128)} %get-tuple-element.49, f32[3072]{0:T(1024)S(1)} %fusion.1, f32[3072]{0:T(1024)S(1)} %get-tuple-element.48), kind=kOutput, calls=%fused_computation.44 | convolution fusion | flops 2472935424 | bytes 39346176 | tf_op jit(solution)/shard_map/bhqk,bkhd->bqhd/dot_general | solution.py:52
  302.0 19.4 %convolution_bitcast_fusion = f32[1,3072,4096]{2,1,0:T(8,128)} fusion(bf16[3072,128]{0,1:T(8,128)(2,1)S(1)} %fusion.59, bf16[128,4096]{1,0:T(8,128)(2,1)S(1)} %copy-done.25), kind=kOutput, calls=%fused_computation.8 | convolution fusion | flops 3221225472 | bytes 52166656 | tf_op jit(solution)/shard_map/bse,ed->bsd/dot_general | solution.py:53
  321.3 0.0 reduce-scatter.3.cloned.1.call-update
  321.4 0.0 all-gather.5.cloned.1.call-start
  321.4 0.6 copy-done.31
  322.0 424.9 %reduce-scatter.3.cloned.1.call-done = f32[1,96,4096]{2,1,0:T(8,128)} async-done(((f32[1,3072,4096]{2,1,0:T(8,128)}), f32[1,96,4096]{2,1,0:T(8,128)}) %reduce-scatter.3.cloned.1.call-update) | async-done | bytes 1572880 | tf_op jit(solution)/shard_map/reduce_scatter | solution.py:54
  747.0 1.6 multiply_reduce_fusion.5
  748.6 2.4 fusion.68
  751.1 3.1 fusion.66
  754.2 0.0 all-gather.5.cloned.1.call-update
  754.2 0.0 reduce-scatter.5.cloned.1.call-start
  754.2 153.0 %all-gather.5.cloned.1.call-done = bf16[1,3072,4096]{2,1,0:T(8,128)(2,1)} async-done(((bf16[1,96,4096]{2,1,0:T(8,128)(2,1)}), bf16[1,3072,4096]{2,1,0:T(8,128)(2,1)}) %all-gather.5.cloned.1.call-update) | async-done | bytes 25165840 | tf_op jit(solution)/shard_map/all_gather | solution.py:64
  907.2 12.4 fusion.53
  919.6 0.0 copy-start.39
  919.6 18.3 %fusion.56 = bf16[3072,128]{0,1:T(8,128)(2,1)} fusion(bf16[3072,128]{1,0:T(8,128)(2,1)S(1)} %fusion.53, f32[3072,3072]{0,1:T(8,128)} %get-tuple-element.49, f32[3072]{0:T(1024)S(1)} %fusion.1, f32[3072]{0:T(1024)S(1)} %get-tuple-element.48), kind=kOutput, calls=%fused_computation.43 | convolution fusion | flops 2472935424 | bytes 39346176 | tf_op jit(solution)/shard_map/bhqk,bqhd->bkhd/dot_general | solution.py:68
  937.9 27.6 %multiply_reduce_fusion = (f32[3072]{0:T(1024)S(1)}, f32[3072,3072]{0,1:T(8,128)}) fusion(f32[3072]{0:T(1024)S(1)} %fusion.1, f32[3072]{0:T(1024)S(1)} %get-tuple-element.48, f32[3072,3072]{0,1:T(8,128)} %get-tuple-element.49, bf16[3072,128]{1,0:T(8,128)(2,1)S(1)} %fusion.53, bf16[3072,128]{1,0:T(8,128)(2,1)S(1)} %copy-done.39), kind=kOutput, calls=%fused_computation.2 | convolution fusion | flops 2481976320 | bytes 77107200 | tf_op jit(solution)/shard_map/bqhd,bkhd->bhqk/dot_general | solution.py:67
  965.6 32.2 %multiply_convert_fusion = bf16[3072,3072]{0,1:T(8,128)(2,1)} fusion(f32[3072,3072]{0,1:T(8,128)} %get-tuple-element.51, f32[3072]{0:T(1024)S(1)} %get-tuple-element.50, f32[3072]{0:T(1024)S(1)} %fusion.1, f32[3072]{0:T(1024)S(1)} %get-tuple-element.48, f32[3072,3072]{0,1:T(8,128)} %get-tuple-element.49), kind=kLoop, calls=%fused_computation.1 | loop fusion | flops 84934656 | bytes 94408704 | tf_op jit(solution)/shard_map/convert_element_type | solution.py:69
  997.8 13.9 convolution_bitcast_fusion.1
  1011.8 0.0 copy-start.35
  1011.8 0.0 copy-start.33
  1011.8 7.9 convolution_bitcast_fusion.2
  1019.8 3.5 multiply_add_fusion
  1023.3 0.0 copy-start.5
  1023.3 0.0 copy-start.6
  1023.3 0.0 copy-start.7
  1023.3 0.0 copy-start.8
  1023.4 1.5 multiply_reduce_fusion.1
  1024.8 1.2 multiply_reduce_fusion.2
  1026.1 39.8 %all-reduce = (f32[2,1,3072]{2,1,0:T(1,128)S(1)}, bf16[4096]{0:T(1024)(128)(2,1)}) all-reduce(f32[2,1,3072]{2,1,0:T(1,128)S(1)} %pad_maximum_fusion.7, f32[4096]{0:T(1024)S(1)} %copy-done.30), channel_id=1, replica_groups=mesh['tp'=32] {'tp'}, use_global_device_ids=true, to_apply=%region_11.12 | all-reduce | flops 10240 | bytes 73728 | tf_op jit(solution)/shard_map/psum | solution.py:78
  1065.9 2.2 multiply_convert_fusion.1
  1068.1 2.6 multiply_convert_fusion.2
  1070.7 19.3 %fusion.84 = f32[3072,4096]{1,0:T(8,128)} fusion(bf16[3072,128]{0,1:T(8,128)(2,1)S(1)} %multiply_convert_fusion.1, bf16[4096,128]{1,0:T(8,128)(2,1)S(1)} %copy-done), kind=kOutput, calls=%fused_computation.100 | convolution fusion | flops 3221225472 | bytes 52166656 | tf_op jit(solution)/shard_map/bse,de->bsd/dot_general | solution.py:85
  1090.1 20.6 %fusion.83 = f32[3072,4096]{1,0:T(8,128)} fusion(bf16[3072,128]{0,1:T(8,128)(2,1)S(1)} %copy-done.4, bf16[4096,128]{1,0:T(8,128)(2,1)} %param.10), kind=kOutput, calls=%fused_computation.99 | convolution fusion | flops 3221225472 | bytes 52166656 | tf_op jit(solution)/shard_map/bse,de->bsd/dot_general | solution.py:84
  1110.7 50.1 %add_bitcast_fusion = f32[1,3072,4096]{2,1,0:T(8,128)} fusion(f32[3072,4096]{1,0:T(8,128)} %fusion.83, f32[3072,4096]{1,0:T(8,128)} %fusion.84, bf16[3072,128]{0,1:T(8,128)(2,1)S(1)} %copy-done.12, bf16[4096,128]{1,0:T(8,128)(2,1)} %param.12), kind=kOutput, calls=%fused_computation | convolution fusion | flops 3246391296 | bytes 152829952 | tf_op jit(solution)/shard_map/bse,de->bsd/dot_general | solution.py:86
  1160.8 0.0 reduce-scatter.5.cloned.1.call-update
  1160.8 12.5 fusion.35
  1173.4 2.3 copy.20
  1175.6 12.5 fusion.38
  1188.2 2.3 copy.19
  1190.5 12.5 fusion.41
  1203.1 2.6 copy.18
  1205.7 12.6 fusion.32
  1218.2 367.7 %reduce-scatter.5.cloned.1.call-done = f32[1,96,4096]{2,1,0:T(8,128)} async-done(((f32[1,3072,4096]{2,1,0:T(8,128)}), f32[1,96,4096]{2,1,0:T(8,128)}) %reduce-scatter.5.cloned.1.call-update) | async-done | bytes 1572880 | tf_op jit(solution)/shard_map/reduce_scatter | solution.py:87
  1586.0 2.4 fusion.67
  (76 shorter events, 0.3 us)
Async XLA Ops:
  7.2 173.3 %copy-start = (bf16[4096,128]{1,0:T(8,128)(2,1)S(1)}, bf16[4096,128]{1,0:T(8,128)(2,1)}, u32[]{:S(2)}) copy-start(bf16[4096,128]{1,0:T(8,128)(2,1)} %param.11) | copy-start | bytes 3145732
  7.2 159.8 %all-gather.3.cloned.1.call-start = ((), (), s32[]{:S(2)}) async-start(), calls=%async_computation.2 | async-start | bytes 25952256 | tf_op jit(solution)/shard_map/all_gather | solution.py:31
  7.9 739.0 %reduce-scatter.3.cloned.1.call-start = ((), (), s32[]{:S(2)}) async-start(), calls=%async_computation.3 | async-start | bytes 51904512 | tf_op jit(solution)/shard_map/reduce_scatter | solution.py:54
  8.6 226.0 %copy-start.32 = (f32[128]{0:T(128)}, f32[128]{0:T(128)S(1)}, u32[]{:S(2)}) copy-start(f32[128]{0:T(128)S(1)} %convert_element_type.108) | copy-start | bytes 1540
  9.3 225.3 %copy-start.34 = (f32[128]{0:T(128)}, f32[128]{0:T(128)S(1)}, u32[]{:S(2)}) copy-start(f32[128]{0:T(128)S(1)} %convert_element_type.109) | copy-start | bytes 1540
  9.3 227.2 %copy-start.36 = (f32[64]{0:T(128)}, f32[64]{0:T(128)S(1)}, u32[]{:S(2)}) copy-start(f32[64]{0:T(128)S(1)} %negate_power_fusion) | copy-start | bytes 772
  180.5 56.0 %copy-start.1 = (f32[3072,128]{0,1:T(8,128)}, f32[3072,128]{0,1:T(8,128)S(1)}, u32[]{:S(2)}) copy-start(f32[3072,128]{0,1:T(8,128)S(1)} %get-tuple-element.47) | copy-start | bytes 4718596
  234.6 5.4 copy-start.26
  234.6 5.5 copy-start.28
  240.0 14.7 copy-start.16
  240.0 14.6 copy-start.18
  240.1 14.6 copy-start.20
  240.1 14.6 copy-start.22
  254.7 17.1 %copy-start.24 = (bf16[4096,128]{1,0:T(8,128)(2,1)S(1)}, bf16[4096,128]{1,0:T(8,128)(2,1)}, u32[]{:S(2)}) copy-start(bf16[4096,128]{1,0:T(8,128)(2,1)} %param.12) | copy-start | bytes 3145732
  283.5 0.9 copy-start.38
  284.4 17.6 %copy-start.25 = (bf16[128,4096]{1,0:T(8,128)(2,1)S(1)}, bf16[128,4096]{1,0:T(8,128)(2,1)}, u32[]{:S(2)}) copy-start(bf16[128,4096]{1,0:T(8,128)(2,1)} %param.13) | copy-start | bytes 3145732
  302.0 19.4 %copy-start.13 = (bf16[3072,128]{0,1:T(8,128)(2,1)}, bf16[3072,128]{0,1:T(8,128)(2,1)S(1)}, u32[]{:S(2)}) copy-start(bf16[3072,128]{0,1:T(8,128)(2,1)S(1)} %fusion.59) | copy-start | bytes 2359300
  321.3 0.7 copy-start.31
  321.3 427.3 %copy-start.9 = (bf16[1,96,4096]{2,1,0:T(8,128)(2,1)S(1)}, bf16[1,96,4096]{2,1,0:T(8,128)(2,1)}, u32[]{:S(2)}) copy-start(bf16[1,96,4096]{2,1,0:T(8,128)(2,1)} %param.17) | copy-start | bytes 2359300
  321.3 429.7 %copy-start.15 = (bf16[1,96,4096]{2,1,0:T(8,128)(2,1)S(1)}, bf16[1,96,4096]{2,1,0:T(8,128)(2,1)}, u32[]{:S(2)}) copy-start(bf16[1,96,4096]{2,1,0:T(8,128)(2,1)} %param.9) | copy-start | bytes 2359300
  321.4 585.9 %all-gather.5.cloned.1.call-start = ((), (), s32[]{:S(2)}) async-start(), calls=%async_computation.4 | async-start | bytes 25952256 | tf_op jit(solution)/shard_map/all_gather | solution.py:64
  754.2 831.8 %reduce-scatter.5.cloned.1.call-start = ((), (), s32[]{:S(2)}) async-start(), calls=%async_computation.5 | async-start | bytes 51904512 | tf_op jit(solution)/shard_map/reduce_scatter | solution.py:87
  919.6 18.3 %copy-start.39 = (bf16[3072,128]{1,0:T(8,128)(2,1)S(1)}, bf16[3072,128]{1,0:T(8,128)(2,1)}, u32[]{:S(2)}) copy-start(bf16[3072,128]{1,0:T(8,128)(2,1)} %copy-done.38) | copy-start | bytes 2359300
  965.6 32.2 %copy-start.21 = (bf16[3072,64]{0,1:T(8,128)(2,1)S(1)}, bf16[3072,64]{0,1:T(8,128)(2,1)}, u32[]{:S(2)}) copy-start(bf16[3072,64]{0,1:T(8,128)(2,1)} %copy-done.20) | copy-start | bytes 1179652
  965.6 32.2 %copy-start.23 = (bf16[3072,64]{0,1:T(8,128)(2,1)S(1)}, bf16[3072,64]{0,1:T(8,128)(2,1)}, u32[]{:S(2)}) copy-start(bf16[3072,64]{0,1:T(8,128)(2,1)} %copy-done.22) | copy-start | bytes 1179652
  997.8 13.9 copy-start.17
  997.8 13.9 copy-start.19
  1011.7 8.0 copy-start.11
  1011.7 8.0 copy-start.37
  1011.7 11.6 copy-start.3
  1011.7 11.6 copy-start.29
  1011.8 11.6 copy-start.35
  1011.8 13.1 copy-start.2
  1011.8 13.1 copy-start.27
  1011.8 13.1 copy-start.33
  1011.8 14.3 copy-start.30
  1023.3 1.5 copy-start.5
  1023.3 2.8 copy-start.6
  1023.3 2.8 copy-start.7
  1023.3 2.8 copy-start.8
  1070.7 19.3 %copy-start.4 = (bf16[3072,128]{0,1:T(8,128)(2,1)S(1)}, bf16[3072,128]{0,1:T(8,128)(2,1)}, u32[]{:S(2)}) copy-start(bf16[3072,128]{0,1:T(8,128)(2,1)} %multiply_convert_fusion.2) | copy-start | bytes 2359300
  1090.1 20.6 %copy-start.12 = (bf16[3072,128]{0,1:T(8,128)(2,1)S(1)}, bf16[3072,128]{0,1:T(8,128)(2,1)}, u32[]{:S(2)}) copy-start(bf16[3072,128]{0,1:T(8,128)(2,1)} %fusion.56) | copy-start | bytes 2359300
  1188.2 17.5 %copy-start.14 = (bf16[3072,128]{0,1:T(8,128)(2,1)S(1)}, bf16[3072,128]{0,1:T(8,128)(2,1)}, u32[]{:S(2)}) copy-start(bf16[3072,128]{0,1:T(8,128)(2,1)} %copy-done.13) | copy-start | bytes 2359300
  1203.1 382.9 %copy-start.10 = (bf16[1,96,4096]{2,1,0:T(8,128)(2,1)S(1)}, bf16[1,96,4096]{2,1,0:T(8,128)(2,1)}, u32[]{:S(2)}) copy-start(bf16[1,96,4096]{2,1,0:T(8,128)(2,1)} %param.17) | copy-start | bytes 2359300
Sparse Core Ops, SparseCore 0:
  10.9 156.0 all-gather.2
  321.5 425.4 reduce-scatter.2
  754.3 152.8 all-gather.4
  1160.9 424.9 reduce-scatter.4
where the time goes:
time: 1600 us
  waiting for transfers between devices  1100 us (69%)
  matrix products  312 us (20%)
  blocking collectives  78.7 us (5%)
  other arithmetic  76.6 us (5%)
    reduce_scatter x1, waiting for transfers between devices, local_block(): lax.psum_scatter(attn_part, 'tp', scatter_dimension=1, tiled=True)  425 us
    reduce_scatter x1, waiting for transfers between devices, local_block(): lax.psum_scatter(dx_part, 'tp', scatter_dimension=1, tiled=True) + dy_f  368 us
    all_gather x1, waiting for transfers between devices, local_block(): x_full = lax.all_gather(x_loc, 'tp', axis=1, tiled=True)  158 us
    all_gather x1, waiting for transfers between devices, local_block(): lax.all_gather(d_attn.astype(jnp.bfloat16), 'tp', axis=1, tiled=True)  153 us
    dot_general x1, matrix products, local_block(): jnp.einsum('bse,de->bsd', d_value, wv_loc, preferred_element_type=jnp.flo...  50.1 us
    psum x1, blocking collectives, local_block(): lax.psum(jnp.stack([jnp.sum(dq_unit * q_unit, axis=-1), jnp.sum(dk_unit *...  39.8 us
    psum x1, blocking collectives, local_block(): lax.psum(jnp.stack([jnp.sum(q_raw * q_raw, axis=-1), jnp.sum(k_raw * k_ra...  38.9 us
    convert_element_type x1, other arithmetic, local_block(): (attn_probs * (d_probs - jnp.sum(attn_probs * d_probs, axis=-1, keepdims=...  32.2 us
  transfers between devices with their start and end apart: 4, of which 4 were waited for; matrix products, arithmetic and copies ran while one was open for 4% of the time, Pallas kernels for 0%

commit v1 on v0

v1 whole, which is shorter than its diff:
```python
import functools

import jax
import jax.numpy as jnp
from jax import lax
from jax.experimental import pallas as pl
from jax.experimental.pallas import tpu as pltpu
from jax.sharding import PartitionSpec as P

HEAD_SIZE = 128
ROPE_THETA = 500000.0
NORM_EPS = 1e-6
LOG2E = 1.4426950408889634
ATTN_SCALE = HEAD_SIZE ** -0.5
MESH = pl.DeviceIdType.MESH
VMEM = pl.BlockSpec(memory_space=pltpu.VMEM)
BLOCK = 512


def rope_tables(seq_len):
    half_dim = HEAD_SIZE // 2
    inv_freq = 1.0 / (ROPE_THETA ** (jnp.arange(half_dim, dtype=jnp.float32) / half_dim))
    angles = jnp.arange(seq_len, dtype=jnp.float32)[:, None] * inv_freq[None, :]
    return jnp.cos(angles), jnp.sin(angles)


def rotate(values, cos_t, sin_t):
    lower_half, upper_half = jnp.split(values, 2, axis=-1)
    return jnp.concatenate([lower_half * cos_t - upper_half * sin_t, upper_half * cos_t + lower_half * sin_t], axis=-1)


def rotate_back(values, cos_t, sin_t):
    lower_half, upper_half = jnp.split(values, 2, axis=-1)
    return jnp.concatenate([lower_half * cos_t + upper_half * sin_t, upper_half * cos_t - lower_half * sin_t], axis=-1)


def column_of(me):
    z, c, core = me // 8, lax.rem(me // 2, 4), lax.rem(me, 2)
    return z * 2 + core, c


def column_peer(me, k):
    m, c = column_of(me)
    m2 = lax.rem(m + k, 8)
    return (m2 // 2) * 8 + c * 2 + lax.rem(m2, 2)


def plane_peer(me, k):
    return (me // 8) * 8 + lax.rem(lax.rem(me, 8) + k, 8)


def ring_peer(me, k):
    c = lax.rem(lax.rem(me // 2, 4) + k, 4)
    return (me // 8) * 8 + c * 2 + lax.rem(me, 2)


def line_peer(me, k):
    return lax.rem(me // 8 + k, 4) * 8 + lax.rem(me, 8)


def entry_barrier(me, peer_of, count):
    barrier = pltpu.get_barrier_semaphore()
    for k in range(1, count):
        pl.semaphore_signal(barrier, inc=1, device_id=(peer_of(me, k),), device_id_type=MESH)
    pl.semaphore_wait(barrier, count - 1)


def exchange_kernel(peer_of, count, source, target, x_ref, out_ref, send_sem, recv_sem):
    me = lax.axis_index('tp')
    entry_barrier(me, peer_of, count)
    copies = []
    for k in range(1, count):
        peer = peer_of(me, k)
        copy = pltpu.make_async_remote_copy(
            src_ref=source(x_ref, peer), dst_ref=target(out_ref, me),
            send_sem=send_sem.at[k], recv_sem=recv_sem.at[k], device_id=(peer,), device_id_type=MESH)
        copy.start()
        copies.append(copy)
    target(out_ref, me)[...] = source(x_ref, me)[...]
    for copy in copies:
        copy.wait()


def exchange(x, out_shape, peer_of, count, source, target, collective_id):
    return pl.pallas_call(
        functools.partial(exchange_kernel, peer_of, count, source, target),
        out_shape=jax.ShapeDtypeStruct(out_shape, x.dtype),
        in_specs=[VMEM], out_specs=VMEM,
        scratch_shapes=[pltpu.SemaphoreType.DMA((count,)), pltpu.SemaphoreType.DMA((count,))],
        compiler_params=pltpu.CompilerParams(collective_id=collective_id, has_side_effects=True, vmem_limit_bytes=24 << 20),
    )(x)


def reduce_kernel(peer_of, count, rank_of, x_ref, out_ref, parts, send_sem, recv_sem):
    me = lax.axis_index('tp')
    entry_barrier(me, peer_of, count)
    copies = []
    for k in range(1, count):
        peer = peer_of(me, k)
        copy = pltpu.make_async_remote_copy(
            src_ref=x_ref.at[rank_of(peer)], dst_ref=parts.at[k - 1],
            send_sem=send_sem.at[k], recv_sem=recv_sem.at[k], device_id=(peer,), device_id_type=MESH)
        copy.start()
        copies.append(copy)
    mine = rank_of(me)
    for copy in copies:
        copy.wait()

    def add(i, carry):
        rows = pl.ds(pl.multiple_of(i * 8, 8), 8)
        total = x_ref[mine, rows, :]
        for k in range(count - 1):
            total = total + parts[k, rows, :]
        out_ref[rows, :] = total
        return carry

    lax.fori_loop(0, out_ref.shape[0] // 8, add, 0)


def reduce_scatter(x, peer_of, rank_of, collective_id):
    count, rows, cols = x.shape
    return pl.pallas_call(
        functools.partial(reduce_kernel, peer_of, count, rank_of),
        out_shape=jax.ShapeDtypeStruct((rows, cols), x.dtype),
        in_specs=[VMEM], out_specs=VMEM,
        scratch_shapes=[pltpu.VMEM((count - 1, rows, cols), x.dtype),
                        pltpu.SemaphoreType.DMA((count,)), pltpu.SemaphoreType.DMA((count,))],
        compiler_params=pltpu.CompilerParams(collective_id=collective_id, has_side_effects=True, vmem_limit_bytes=32 << 20),
    )(x)


def all_sum_kernel(x_ref, out_ref, plane, middle, line, send_sem, recv_sem):
    me = lax.axis_index('tp')
    barrier = pltpu.get_barrier_semaphore()
    for k in range(1, 8):
        pl.semaphore_signal(barrier, inc=1, device_id=(plane_peer(me, k),), device_id_type=MESH)
    for k in range(1, 4):
        pl.semaphore_signal(barrier, inc=1, device_id=(line_peer(me, k),), device_id_type=MESH)
    pl.semaphore_wait(barrier, 10)
    mine = lax.rem(me, 8)
    copies = []
    for k in range(1, 8):
        copy = pltpu.make_async_remote_copy(
            src_ref=x_ref, dst_ref=plane.at[mine], send_sem=send_sem.at[k], recv_sem=recv_sem.at[k],
            device_id=(plane_peer(me, k),), device_id_type=MESH)
        copy.start()
        copies.append(copy)
    plane[mine] = x_ref[...]
    for copy in copies:
        copy.wait()
    total = plane[0]
    for k in range(1, 8):
        total = total + plane[k]
    middle[...] = total
    z = me // 8
    line[z] = total
    copies = []
    for k in range(1, 4):
        copy = pltpu.make_async_remote_copy(
            src_ref=middle, dst_ref=line.at[z], send_sem=send_sem.at[7 + k], recv_sem=recv_sem.at[7 + k],
            device_id=(line_peer(me, k),), device_id_type=MESH)
        copy.start()
        copies.append(copy)
    for copy in copies:
        copy.wait()
    out_ref[...] = (line[0] + line[1]) + (line[2] + line[3])


def all_sum(x, collective_id):
    return pl.pallas_call(
        all_sum_kernel,
        out_shape=jax.ShapeDtypeStruct(x.shape, x.dtype),
        in_specs=[VMEM], out_specs=VMEM,
        scratch_shapes=[pltpu.VMEM((8,) + x.shape, x.dtype), pltpu.VMEM(x.shape, x.dtype), pltpu.VMEM((4,) + x.shape, x.dtype),
                        pltpu.SemaphoreType.DMA((11,)), pltpu.SemaphoreType.DMA((11,))],
        compiler_params=pltpu.CompilerParams(collective_id=collective_id, has_side_effects=True, vmem_limit_bytes=8 << 20),
    )(x)


def greet(peers):
    barrier = pltpu.get_barrier_semaphore()
    for peer in peers:
        pl.semaphore_signal(barrier, inc=1, device_id=(peer,), device_id_type=MESH)
    pl.semaphore_wait(barrier, len(peers))


def send(src, dst, sems, slot, peer):
    copy = pltpu.make_async_remote_copy(
        src_ref=src, dst_ref=dst, send_sem=sems[0].at[slot], recv_sem=sems[1].at[slot], device_id=(peer,), device_id_type=MESH)
    copy.start()
    return copy


def semaphores(count):
    return [pltpu.SemaphoreType.DMA((count,)), pltpu.SemaphoreType.DMA((count,))]


def spread_kernel(x_ref, ring_ref, near_ref, *sems):
    me = lax.axis_index('tp')
    greet([ring_peer(me, k) for k in range(1, 4)] + [line_peer(me, 1), line_peer(me, 3)])
    mine = lax.rem(me // 2, 4)
    copies = [send(x_ref, ring_ref.at[mine], sems, k, ring_peer(me, k)) for k in range(1, 4)]
    copies += [send(x_ref, near_ref.at[0], sems, 4, line_peer(me, 1)), send(x_ref, near_ref.at[1], sems, 5, line_peer(me, 3))]
    ring_ref[mine] = x_ref[...]
    for copy in copies:
        copy.wait()


def spread(x, collective_id):
    return pl.pallas_call(
        spread_kernel,
        out_shape=(jax.ShapeDtypeStruct((4,) + x.shape, x.dtype), jax.ShapeDtypeStruct((2,) + x.shape, x.dtype)),
        in_specs=[VMEM], out_specs=(VMEM, VMEM), scratch_shapes=semaphores(6),
        compiler_params=pltpu.CompilerParams(collective_id=collective_id, has_side_effects=True, vmem_limit_bytes=24 << 20),
    )(x)


def plane_kernel(width, x_ref, d_ref, out_ref, far_ref, *sems):
    me = lax.axis_index('tp')
    greet([plane_peer(me, k) for k in range(1, 8)] + [line_peer(me, 2)])
    mine = lax.rem(me, 8)
    columns = pl.ds(pl.multiple_of(mine * width, width), width)
    copies = [send(d_ref, far_ref, sems, 0, line_peer(me, 2))]
    for k in range(1, 8):
        peer = plane_peer(me, k)
        copies.append(send(x_ref.at[:, lax.rem(peer, 8)], out_ref.at[:, :, columns], sems, k, peer))
    out_ref[:, :, columns] = x_ref[:, mine]
    for copy in copies:
        copy.wait()


def plane_exchange(x, d, collective_id):
    width = x.shape[-1]
    return pl.pallas_call(
        functools.partial(plane_kernel, width),
        out_shape=(jax.ShapeDtypeStruct((4, x.shape[2], 8 * width), x.dtype), jax.ShapeDtypeStruct(d.shape, d.dtype)),
        in_specs=[VMEM, VMEM], out_specs=(VMEM, VMEM), scratch_shapes=semaphores(8),
        compiler_params=pltpu.CompilerParams(collective_id=collective_id, has_side_effects=True, vmem_limit_bytes=24 << 20),
    )(x, d)


TILE = 512


def final_kernel(dx_ref, ring_ref, near_ref, far_ref, dw_ref, o_ref, x_ref, sum_ref, gw_ref, gwo_ref,
                 parts, full, x_buf, x_sem, local_sem, *sems):
    me = lax.axis_index('tp')
    z, c, core = me // 8, lax.rem(me // 2, 4), lax.rem(me, 2)
    partner = me + 1 - 2 * core
    greet([line_peer(me, k) for k in range(1, 4)] + [ring_peer(me, k) for k in range(1, 4)] + [partner])
    sums = [send(dx_ref.at[line_peer(me, k) // 8], parts.at[k - 1], sems, k - 1, line_peer(me, k)) for k in (2, 1, 3)]
    planes = [lax.rem(z + 3, 4), lax.rem(z + 1, 4), lax.rem(z + 2, 4)]
    lines = [near_ref.at[0], near_ref.at[1], far_ref]

    def slot(plane, column):
        return plane * 8 + column * 2 + core

    rounds, shared, local = [], [], []
    for r in range(3):
        for k in range(1, 4):
            rounds.append(send(lines[r], full.at[slot(planes[r], c)], sems, 3 + r * 3 + k - 1, ring_peer(me, k)))
    for r in range(3):
        shared.append(send(lines[r], full.at[slot(planes[r], c)], sems, 12 + r, partner))
        local.append(pltpu.make_async_copy(lines[r], full.at[slot(planes[r], c)], local_sem.at[r]))
    for j in range(4):
        shared.append(send(ring_ref.at[j], full.at[slot(z, j)], sems, 15 + j, partner))
        local.append(pltpu.make_async_copy(ring_ref.at[j], full.at[slot(z, j)], local_sem.at[3 + j]))
    for copy in local:
        copy.start()

    tiles = x_ref.shape[1] // TILE

    def columns(j):
        return pl.ds(pl.multiple_of(j * TILE, TILE), TILE)

    def fetch(j, b):
        return pltpu.make_async_copy(x_ref.at[:, columns(j)], x_buf.at[b], x_sem.at[b])

    fetch(0, 0).start()

    def weights(j, carry):
        b = lax.rem(j, 2)

        @pl.when(j + 1 < tiles)
        def _():
            fetch(j + 1, 1 - b).start()

        fetch(j, b).wait()
        gw_ref[:, columns(j)] = nn(dw_ref[...], x_buf[b]).astype(gw_ref.dtype)
        return carry

    lax.fori_loop(0, tiles, weights, 0)
    for r in range(3):
        for k in range(1, 4):
            rounds[r * 3 + k - 1].wait()
            block = full.at[slot(planes[r], lax.rem(c + 4 - k, 4))]
            shared.append(send(block, block, sems, 19 + r * 3 + k - 1, partner))
    for copy in sums:
        copy.wait()

    def add(i, carry):
        rows = pl.ds(pl.multiple_of(i * 8, 8), 8)
        sum_ref[rows, :] = (dx_ref[z, rows, :] + parts[0, rows, :]) + (parts[1, rows, :] + parts[2, rows, :])
        return carry

    lax.fori_loop(0, sum_ref.shape[0] // 8, add, 0)
    for copy in local:
        copy.wait()
    for copy in shared:
        copy.wait()

    def out_weights(j, carry):
        d = full[:, :, columns(j)]
        gwo_ref[:, columns(j)] = nn(o_ref[...], d.reshape(o_ref.shape[1], TILE)).astype(gwo_ref.dtype)
        return carry

    lax.fori_loop(0, tiles, out_weights, 0)


def final(dx_part, d_ring, d_near, d_far, dw_rows, o_rows, x_full, collective_id):
    count, rows, model_dim = dx_part.shape
    seq_len = x_full.shape[0]
    anywhere = pl.BlockSpec(memory_space=pl.ANY)
    return pl.pallas_call(
        final_kernel,
        out_shape=(jax.ShapeDtypeStruct((rows, model_dim), jnp.float32),
                   jax.ShapeDtypeStruct((dw_rows.shape[0], model_dim), jnp.bfloat16),
                   jax.ShapeDtypeStruct((o_rows.shape[0], model_dim), jnp.bfloat16)),
        in_specs=[VMEM, anywhere, anywhere, anywhere, VMEM, VMEM, anywhere], out_specs=(VMEM, VMEM, VMEM),
        scratch_shapes=[pltpu.VMEM((count - 1, rows, model_dim), jnp.float32),
                        pltpu.VMEM((seq_len // rows, rows, model_dim), jnp.bfloat16),
                        pltpu.VMEM((2, seq_len, TILE), jnp.bfloat16),
                        pltpu.SemaphoreType.DMA((2,)), pltpu.SemaphoreType.DMA((7,))] + semaphores(28),
        compiler_params=pltpu.CompilerParams(collective_id=collective_id, has_side_effects=True, vmem_limit_bytes=60 << 20),
    )(dx_part, d_ring, d_near, d_far, dw_rows, o_rows, x_full)


def nt(a, b):
    return lax.dot_general(a, b, (((1,), (1,)), ((), ())), preferred_element_type=jnp.float32)


def tn(a, b):
    return lax.dot_general(a, b, (((0,), (0,)), ((), ())), preferred_element_type=jnp.float32)


def nn(a, b):
    return lax.dot_general(a, b, (((1,), (0,)), ((), ())), preferred_element_type=jnp.float32)


def fold_rows(values, op):
    return op(values.reshape(values.shape[0] // 8, 8, values.shape[1]), axis=0)


def block_rows(j):
    return pl.ds(pl.multiple_of(j * BLOCK, BLOCK), BLOCK)


def diagonal_mask():
    keys = lax.broadcasted_iota(jnp.int32, (BLOCK, BLOCK), 0)
    queries = lax.broadcasted_iota(jnp.int32, (BLOCK, BLOCK), 1)
    return keys <= queries


def attention_kernel(q_ref, k_ref, v_ref, o_ref, max_ref, inv_ref, s_scr, acc_scr):
    i = pl.program_id(0)
    q_blk = q_ref[...]

    def score(j, top):
        s = nt(k_ref[block_rows(j), :], q_blk) * (ATTN_SCALE * LOG2E)
        s_scr[block_rows(j), :] = s
        return jnp.maximum(top, fold_rows(s, jnp.max))

    s = jnp.where(diagonal_mask(), nt(k_ref[block_rows(i), :], q_blk) * (ATTN_SCALE * LOG2E), -1e30)
    s_scr[block_rows(i), :] = s
    top = lax.fori_loop(0, i, score, fold_rows(s, jnp.max))
    top = jnp.max(top, axis=0, keepdims=True)

    def weigh(j, total):
        p = jnp.exp2(s_scr[block_rows(j), :] - top)
        s_scr[block_rows(j), :] = p
        return total + fold_rows(p, jnp.sum)

    total = lax.fori_loop(0, i + 1, weigh, jnp.zeros((8, BLOCK), jnp.float32))
    inv = 1.0 / jnp.sum(total, axis=0, keepdims=True)
    max_ref[...] = top
    inv_ref[...] = inv
    acc_scr[...] = jnp.zeros_like(acc_scr)

    def gather(j, carry):
        p = (s_scr[block_rows(j), :] * inv).astype(jnp.bfloat16)
        acc_scr[...] += tn(v_ref[block_rows(j), :], p)
        return carry

    lax.fori_loop(0, i + 1, gather, 0)
    o_ref[...] = acc_scr[...].T.astype(jnp.bfloat16)


def attention(q, k, v):
    seq_len = q.shape[0]
    steps = seq_len // BLOCK
    rows = pl.BlockSpec((BLOCK, HEAD_SIZE), lambda i: (i, 0))
    whole = pl.BlockSpec((seq_len, HEAD_SIZE), lambda i: (0, 0))
    line = pl.BlockSpec((1, BLOCK), lambda i: (0, i))
    return pl.pallas_call(
        attention_kernel,
        grid=(steps,),
        out_shape=(jax.ShapeDtypeStruct((seq_len, HEAD_SIZE), jnp.bfloat16),
                   jax.ShapeDtypeStruct((1, seq_len), jnp.float32),
                   jax.ShapeDtypeStruct((1, seq_len), jnp.float32)),
        in_specs=[rows, whole, whole], out_specs=(rows, line, line),
        scratch_shapes=[pltpu.VMEM((seq_len, BLOCK), jnp.float32), pltpu.VMEM((HEAD_SIZE, BLOCK), jnp.float32)],
        compiler_params=pltpu.CompilerParams(dimension_semantics=("arbitrary",), vmem_limit_bytes=40 << 20),
        cost_estimate=pl.CostEstimate(flops=8 * seq_len * seq_len * HEAD_SIZE, bytes_accessed=8 * seq_len * HEAD_SIZE, transcendentals=0),
    )(q, k, v)


def attention_grad_kernel(q_ref, k_ref, v_ref, do_ref, max_ref, inv_ref, dq_ref, dk_ref, dv_ref, p_scr, dp_scr, dq_scr, dk_scr, dv_scr):
    i = pl.program_id(0)
    q_blk, do_blk = q_ref[...], do_ref[...]
    top, inv = max_ref[...], inv_ref[...]

    @pl.when(i == 0)
    def _():
        dk_scr[...] = jnp.zeros_like(dk_scr)
        dv_scr[...] = jnp.zeros_like(dv_scr)

    def scores(j, mask, delta):
        rows = block_rows(j)
        s = nt(k_ref[rows, :], q_blk) * (ATTN_SCALE * LOG2E)
        if mask is not None:
            s = jnp.where(mask, s, -1e30)
        p = jnp.exp2(s - top) * inv
        dp = nt(v_ref[rows, :], do_blk)
        p_scr[rows, :] = p
        dp_scr[rows, :] = dp
        dv_scr[rows, :] += nn(p.astype(jnp.bfloat16), do_blk)
        return delta + fold_rows(p * dp, jnp.sum)

    delta = scores(i, diagonal_mask(), jnp.zeros((8, BLOCK), jnp.float32))
    delta = lax.fori_loop(0, i, lambda j, d: scores(j, None, d), delta)
    delta = jnp.sum(delta, axis=0, keepdims=True)
    dq_scr[...] = jnp.zeros_like(dq_scr)

    def grads(j, carry):
        rows = block_rows(j)
        ds = (p_scr[rows, :] * (dp_scr[rows, :] - delta) * ATTN_SCALE).astype(jnp.bfloat16)
        dk_scr[rows, :] += nn(ds, q_blk)
        dq_scr[...] += tn(k_ref[rows, :], ds)
        return carry

    lax.fori_loop(0, i + 1, grads, 0)
    dq_ref[...] = dq_scr[...].T

    @pl.when(i == pl.num_programs(0) - 1)
    def _():
        dk_ref[...] = dk_scr[...]
        dv_ref[...] = dv_scr[...].astype(jnp.bfloat16)


def attention_grad(q, k, v, do, top, inv):
    seq_len = q.shape[0]
    steps = seq_len // BLOCK
    rows = pl.BlockSpec((BLOCK, HEAD_SIZE), lambda i: (i, 0))
    whole = pl.BlockSpec((seq_len, HEAD_SIZE), lambda i: (0, 0))
    line = pl.BlockSpec((1, BLOCK), lambda i: (0, i))
    full = (seq_len, HEAD_SIZE)
    return pl.pallas_call(
        attention_grad_kernel,
        grid=(steps,),
        out_shape=(jax.ShapeDtypeStruct(full, jnp.float32), jax.ShapeDtypeStruct(full, jnp.float32), jax.ShapeDtypeStruct(full, jnp.bfloat16)),
        in_specs=[rows, whole, whole, rows, line, line], out_specs=(rows, whole, whole),
        scratch_shapes=[pltpu.VMEM((seq_len, BLOCK), jnp.float32), pltpu.VMEM((seq_len, BLOCK), jnp.float32),
                        pltpu.VMEM((HEAD_SIZE, BLOCK), jnp.float32), pltpu.VMEM(full, jnp.float32), pltpu.VMEM(full, jnp.float32)],
        compiler_params=pltpu.CompilerParams(dimension_semantics=("arbitrary",), vmem_limit_bytes=48 << 20),
        cost_estimate=pl.CostEstimate(flops=20 * seq_len * seq_len * HEAD_SIZE, bytes_accessed=20 * seq_len * HEAD_SIZE, transcendentals=0),
    )(q, k, v, do, top, inv)


COLUMN_GROUPS = [[z * 8 + c * 2 + core for z in range(4) for core in range(2)] for c in range(4)]
PLANE_GROUPS = [[z * 8 + p for p in range(8)] for z in range(4)]


def after_kernel(value_ref, *refs):
    refs[-1][...] = value_ref[...]


def after(value, *others):
    anywhere = pl.BlockSpec(memory_space=pl.ANY)
    return pl.pallas_call(
        after_kernel,
        out_shape=jax.ShapeDtypeStruct(value.shape, value.dtype),
        in_specs=[VMEM] + [anywhere] * len(others), out_specs=VMEM,
        compiler_params=pltpu.CompilerParams(vmem_limit_bytes=8 << 20),
        cost_estimate=pl.CostEstimate(flops=value.size, bytes_accessed=4 * value.size, transcendentals=0),
    )(value, *others)


def lane_rows(values):
    return values.reshape(-1, 128)


def local_block(x_loc, wq_loc, wk_loc, wv_loc, wo_loc, gq_loc, gk_loc, g_attn, dy_loc):
    x_loc, dy_loc = x_loc[0], dy_loc[0]
    rows, model_dim = x_loc.shape
    bf16, f32 = jnp.bfloat16, jnp.float32
    x_full = lax.all_gather(x_loc, 'tp', axis=0, tiled=True)
    seq_len = x_full.shape[0]
    wo_col = lax.all_gather(after(wo_loc, x_full), 'tp', axis=0, tiled=True, axis_index_groups=COLUMN_GROUPS)
    w_rows = jnp.concatenate([wq_loc.T, wk_loc.T, wv_loc.T], axis=0)

    cos_t, sin_t = rope_tables(seq_len)
    q_raw = nn(x_full, wq_loc)
    k_raw = nn(x_full, wk_loc)
    v_head = nn(x_full, wv_loc).astype(bf16)
    stats = jnp.concatenate([lane_rows(jnp.sum(q_raw * q_raw, axis=-1)), lane_rows(jnp.sum(k_raw * k_raw, axis=-1))])
    sq_sums = all_sum(stats, 1).reshape(2, seq_len)
    inv_rms = lax.rsqrt(sq_sums / model_dim + NORM_EPS)[..., None]
    q_unit = q_raw * inv_rms[0]
    k_unit = k_raw * inv_rms[1]
    gq_f, gk_f = gq_loc.astype(f32), gk_loc.astype(f32)
    q_rot = rotate(q_unit * gq_f, cos_t, sin_t).astype(bf16)
    k_rot = rotate(k_unit * gk_f, cos_t, sin_t).astype(bf16)
    o_head, top, inv = attention(q_rot, k_rot, v_head)

    o_col = exchange(
        o_head.reshape(4, 4, 2, rows, HEAD_SIZE), (4, rows, 8 * HEAD_SIZE), column_peer, 8,
        lambda ref, d: ref.at[d // 8, :, lax.rem(d, 2)],
        lambda ref, d: ref.at[:, :, pl.ds(pl.multiple_of(column_of(d)[0] * HEAD_SIZE, HEAD_SIZE), HEAD_SIZE)], 2)
    a_part = nn(o_col.reshape(4 * rows, 8 * HEAD_SIZE), wo_col)
    attn_loc = reduce_scatter(a_part.reshape(4, rows, model_dim), ring_peer, lambda d: lax.rem(d // 2, 4), 3)

    post_rms = lax.rsqrt(jnp.mean(attn_loc * attn_loc, axis=-1, keepdims=True) + NORM_EPS)
    normed = attn_loc * post_rms
    ga_f = g_attn.astype(f32)
    dy_f = dy_loc.astype(f32)
    y_loc = (x_loc.astype(f32) + normed * ga_f).astype(bf16)
    ga_part = jnp.sum(dy_f * normed, axis=0)
    g_normed = dy_f * ga_f
    d_attn = (post_rms * (g_normed - normed * jnp.mean(g_normed * normed, axis=-1, keepdims=True))).astype(bf16)

    d_ring, d_near = spread(d_attn, 4)
    w_plane = lax.all_gather(after(w_rows, d_ring), 'tp', axis=0, tiled=True, axis_index_groups=PLANE_GROUPS)
    d_col = nt(d_ring.reshape(4 * rows, model_dim), wo_col).astype(bf16)
    d_head = exchange(
        d_col.reshape(4, rows, 8 * HEAD_SIZE), (4, 4, 2, rows, HEAD_SIZE), column_peer, 8,
        lambda ref, d: ref.at[:, :, pl.ds(pl.multiple_of(column_of(d)[0] * HEAD_SIZE, HEAD_SIZE), HEAD_SIZE)],
        lambda ref, d: ref.at[d // 8, :, lax.rem(d, 2)], 5).reshape(seq_len, HEAD_SIZE)

    dq_rot, dk_rot, d_value = attention_grad(q_rot, k_rot, v_head, d_head, top, inv)
    dq_hat = rotate_back(dq_rot, cos_t, sin_t)
    dk_hat = rotate_back(dk_rot, cos_t, sin_t)
    grad_gq = jnp.sum(dq_hat * q_unit, axis=0)
    grad_gk = jnp.sum(dk_hat * k_unit, axis=0)
    dq_unit = dq_hat * gq_f
    dk_unit = dk_hat * gk_f
    sums = jnp.concatenate([lane_rows(jnp.sum(dq_unit * q_unit, axis=-1)), lane_rows(jnp.sum(dk_unit * k_unit, axis=-1)), lane_rows(ga_part)])
    sums = all_sum(sums, 6)
    dots_rows = 2 * seq_len // 128
    unit_dots = sums[:dots_rows].reshape(2, seq_len)[..., None] / model_dim
    grad_ga = sums[dots_rows:].reshape(model_dim)
    dq_raw = (inv_rms[0] * (dq_unit - q_unit * unit_dots[0])).astype(bf16)
    dk_raw = (inv_rms[1] * (dk_unit - k_unit * unit_dots[1])).astype(bf16)
    d_qkv = jnp.concatenate([dq_raw, dk_raw, d_value], axis=1)

    width = 3 * HEAD_SIZE
    d_plane, d_far = plane_exchange(d_qkv.reshape(4, 8, rows, width), d_attn, 7)
    dx_part = nn(d_plane.reshape(4 * rows, 8 * width), w_plane)
    dx_loc, grad_w, grad_wo = final(dx_part.reshape(4, rows, model_dim), d_ring, d_near, d_far, d_qkv.T, o_head.T, x_full, 8)
    grad_x = (dx_loc + dy_f).astype(bf16)
    grad_wq, grad_wk, grad_wv = [grad_w[i * HEAD_SIZE:(i + 1) * HEAD_SIZE].T for i in range(3)]
    return (y_loc[None], grad_x[None], grad_wq, grad_wk, grad_wv, grad_wo,
            grad_gq.astype(bf16), grad_gk.astype(bf16), grad_ga.astype(bf16))


def solution(mesh):
    act_spec = P(None, 'tp', None)
    col_spec = P(None, 'tp')
    row_spec = P('tp', None)
    vec_spec = P('tp')
    in_specs = (act_spec, col_spec, col_spec, col_spec, row_spec, vec_spec, vec_spec, P(), act_spec)
    out_specs = (act_spec, act_spec, col_spec, col_spec, col_spec, row_spec, vec_spec, vec_spec, P())
    return jax.shard_map(local_block, mesh=mesh, in_specs=in_specs, out_specs=out_specs, check_vma=False)
```

time: 1600 us -> 739 us (0.46)
  the two profiles are of different devices: /device:TPU:0 before, /device:TPU:11 now
where the time goes in v1:
time: 739 us; the launch traced here: 738 us
  Pallas kernels  426 us (58%)
  waiting for transfers between devices  169 us (23%)
  matrix products  68.1 us (9%)
  local copies, waits for them, and re-layouts  41.1 us (6%)
  other arithmetic  20.7 us (3%)
  between operations  14.3 us (2%)
    all_gather x1, waiting for transfers between devices, local_block(): x_full = lax.all_gather(x_loc, 'tp', axis=0, tiled=True)  157 us
    pallas_call x1, Pallas kernels, final(): pl.pallas_call(final_kernel, out_shape=(jax.ShapeDtypeStruct((rows, model...  150 us
    pallas_call x1, Pallas kernels, reduce_scatter(): pl.pallas_call(functools.partial(reduce_kernel, peer_of, count, rank_of),...  70.7 us
    dot_general x5, matrix products, nn(): lax.dot_general(a, b, (((1,), (0,)), ((), ())), preferred_element_type=jn...  62 us
    pallas_call x1, Pallas kernels, plane_exchange(): pl.pallas_call(functools.partial(plane_kernel, width), out_shape=(jax.Sha...  54.9 us
    pallas_call x2, Pallas kernels, exchange(): pl.pallas_call(functools.partial(exchange_kernel, peer_of, count, source,...  42.3 us
    pallas_call x1, Pallas kernels, spread(): pl.pallas_call(spread_kernel, out_shape=(jax.ShapeDtypeStruct((4,) + x.sh...  37.5 us
    pallas_call x2, Pallas kernels, all_sum(): pl.pallas_call(all_sum_kernel, out_shape=jax.ShapeDtypeStruct(x.shape, x....  30.4 us
  transfers between devices with their start and end apart: 3, of which 2 were waited for; matrix products, arithmetic and copies ran while one was open for 11% of the time, Pallas kernels for 22%

profile of v1, /device:TPU:11, one launch (start us, length us, event | category | flops | bytes accessed | tf_op | source)
XLA Modules:
  0.0 738.5 jit_solution(8560941951862122763)
XLA Ops:
  7.2 0.7 all-gather.9.cloned.1.call-update
  8.0 156.6 %all-gather.9.cloned.1.call-done = bf16[1,3072,4096]{2,1,0:T(8,128)(2,1)} async-done(((bf16[1,96,4096]{2,1,0:T(8,128)(2,1)}), bf16[1,3072,4096]{2,1,0:T(8,128)(2,1)}) %all-gather.9.cloned.1.call-update) | async-done | bytes 25165840 | tf_op jit(solution)/shard_map/all_gather | solution.py:506
  164.6 8.2 %copy-done = bf16[1,3072,4096]{2,1,0:T(8,128)(2,1)S(1)} copy-done((bf16[1,3072,4096]{2,1,0:T(8,128)(2,1)S(1)}, bf16[1,3072,4096]{2,1,0:T(8,128)(2,1)}, u32[]{:S(2)}) %copy-start) | copy-done | bytes 25165848
  172.7 1.2 copy-done.8
  174.0 1.0 shard_map.163
  175.0 0.0 all-gather.7.cloned.1.call-start
  175.2 1.1 copy-done.24
  176.2 1.3 copy.45
  177.5 1.3 copy.46
  178.9 2.4 copy.47
  181.2 3.0 pad_maximum_fusion.value_ref
  184.2 13.2 %multiply_reduce_fusion.6 = (f32[3072]{0:T(1024)S(1)}, f32[3072,128]{0,1:T(8,128)S(1)}) fusion(bf16[4096,128]{1,0:T(8,128)(2,1)S(1)} %copy-done.24, bf16[1,3072,4096]{2,1,0:T(8,128)(2,1)} %all-gather.9.cloned.1.call-done), kind=kOutput, calls=%fused_computation.29 | convolution fusion | flops 3222008832 | bytes 27799552 | tf_op jit(solution)/shard_map/dot_general | solution.py:347
  197.5 14.0 %multiply_reduce_fusion.5 = (f32[3072]{0:T(1024)S(1)}, f32[3072,128]{0,1:T(8,128)S(1)}) fusion(bf16[4096,128]{1,0:T(8,128)(2,1)} %param.11, bf16[1,3072,4096]{2,1,0:T(8,128)(2,1)} %all-gather.9.cloned.1.call-done), kind=kOutput, calls=%fused_computation.28 | convolution fusion | flops 3222008832 | bytes 27799552 | tf_op jit(solution)/shard_map/dot_general | solution.py:347
  211.6 14.4 %shard_map.160 = f32[48,128]{1,0:T(8,128)S(1)} custom-call(f32[48,128]{1,0:T(8,128)S(1)} %pad_maximum_fusion.7.x_ref), custom_call_target="tpu_custom_call" | custom-call | tf_op jit(solution)/shard_map/pallas_call | solution.py:170
  226.1 0.3 multiply_multiply_fusion
  226.4 0.3 multiply_multiply_fusion.1
  226.7 3.5 subtract_convert_fusion
  230.2 0.1 pad_maximum_fusion.5
  230.3 0.4 copy.36.k_ref
  230.7 0.1 pad_maximum_fusion.4
  230.7 0.4 copy.35.q_ref
  231.1 1.1 copy-done.30
  232.2 12.0 %convolution_convert_fusion.v_ref = bf16[3072,128]{1,0:T(8,128)(2,1)S(1)} fusion(bf16[4096,128]{1,0:T(8,128)(2,1)S(1)} %copy-done.30, bf16[1,3072,4096]{2,1,0:T(8,128)(2,1)} %all-gather.9.cloned.1.call-done), kind=kOutput, calls=%fused_computation.4 | convolution fusion | flops 3221618688 | bytes 27000832 | tf_op jit(solution)/shard_map/dot_general | solution.py:347
  244.2 15.5 %shard_map.161 = (bf16[3072,128]{1,0:T(8,128)(2,1)S(1)}, f32[1,3072]{1,0:T(1,128)S(1)}, f32[1,3072]{1,0:T(1,128)S(1)}) custom-call(bf16[3072,128]{1,0:T(8,128)(2,1)S(1)} %copy.35.q_ref, bf16[3072,128]{1,0:T(8,128)(2,1)S(1)} %copy.36.k_ref, bf16[3072,128]{1,0:T(8,128)(2,1)S(1)} %convolution_convert_fusion.v_ref), custom_call_target="tpu_custom_call" | custom-call | flops 9663676416 | bytes 3145728 | tf_op jit(solution)/shard_map/pallas_call | solution.py:404
  259.7 19.7 %shard_map.162 = bf16[4,96,1024]{2,1,0:T(8,128)(2,1)S(1)} custom-call(bf16[4,4,2,96,128]{4,3,2,1,0:T(8,128)(2,1)S(1)} %bitcast.73), custom_call_target="tpu_custom_call" | custom-call | tf_op jit(solution)/shard_map/pallas_call | solution.py:85
  279.4 0.9 copy-done.6
  280.3 5.8 fusion.2.x_ref
  286.1 70.7 %shard_map.164 = f32[96,4096]{1,0:T(8,128)S(1)} custom-call(f32[4,96,4096]{2,1,0:T(8,128)S(1)} %fusion.2.x_ref), custom_call_target="tpu_custom_call" | custom-call | tf_op jit(solution)/shard_map/pallas_call | solution.py:122
  356.9 0.2 multiply_reduce_fusion.4
  357.1 0.9 copy-done.21
  358.0 0.6 fusion.9
  358.7 1.5 fusion.8
  360.1 37.5 %shard_map.165 = (bf16[4,96,4096]{2,1,0:T(8,128)(2,1)S(1)}, bf16[2,96,4096]{2,1,0:T(8,128)(2,1)S(1)}) custom-call(bf16[96,4096]{1,0:T(8,128)(2,1)S(1)} %get-tuple-element.64.x_ref.d_ref), custom_call_target="tpu_custom_call" | custom-call | tf_op jit(solution)/shard_map/pallas_call | solution.py:210
  397.7 1.2 copy-done.7
  398.9 0.2 shard_map.170
  399.1 1.8 copy-done.2
  401.0 2.3 copy.48
  403.3 6.0 convolution_convert_fusion.1
  409.4 22.6 %shard_map.166 = bf16[4,4,2,96,128]{4,3,2,1,0:T(8,128)(2,1)S(1)} custom-call(bf16[4,96,1024]{2,1,0:T(8,128)(2,1)S(1)} %bitcast.75), custom_call_target="tpu_custom_call" | custom-call | tf_op jit(solution)/shard_map/pallas_call | solution.py:85
  432.0 23.1 %shard_map.167 = (f32[3072,128]{1,0:T(8,128)S(1)}, f32[3072,128]{1,0:T(8,128)}, bf16[3072,128]{1,0:T(8,128)(2,1)S(1)}) custom-call(bf16[3072,128]{1,0:T(8,128)(2,1)S(1)} %copy-done.12, bf16[3072,128]{1,0:T(8,128)(2,1)S(1)} %copy-done.10, bf16[3072,128]{1,0:T(8,128)(2,1)S(1)} %copy-done.16, bf16[3072,128]{1,0:T(8,128)(2,1)S(1)} %bitcast.74, ...), custom_call_target="tpu_custom_call" | custom-call | flops 24159191040 | bytes 7864320 | tf_op jit(solution)/shard_map/pallas_call | solution.py:467
  455.1 1.6 copy.39
  456.7 1.2 copy.43
  457.9 2.0 copy.41
  459.9 3.5 multiply_add_fusion.1
  463.4 1.7 multiply_reduce_fusion
  465.1 15.9 %shard_map.168 = f32[80,128]{1,0:T(8,128)S(1)} custom-call(f32[80,128]{1,0:T(8,128)S(1)} %pad_maximum_fusion.6.x_ref), custom_call_target="tpu_custom_call" | custom-call | tf_op jit(solution)/shard_map/pallas_call | solution.py:170
  481.1 0.4 multiply_convert_fusion
  481.4 0.3 multiply_convert_fusion.1
  481.8 0.8 copy-done.27
  482.5 2.7 fusion.22
  485.3 3.1 copy.44
  488.4 54.9 %shard_map.169 = (bf16[4,96,3072]{2,1,0:T(8,128)(2,1)S(1)}, bf16[96,4096]{1,0:T(8,128)(2,1)S(1)}) custom-call(bf16[4,8,96,384]{3,2,1,0:T(8,128)(2,1)S(1)} %bitcast.72, bf16[96,4096]{1,0:T(8,128)(2,1)S(1)} %copy-done.5), custom_call_target="tpu_custom_call" | custom-call | tf_op jit(solution)/shard_map/pallas_call | solution.py:234
  543.3 0.9 copy-done.13
  544.1 1.5 copy-done.14
  545.6 0.6 fusion.16
  546.2 11.2 %all-gather.7.cloned.1.call-done = bf16[3072,4096]{1,0:T(8,128)(2,1)} async-done(((bf16[384,4096]{1,0:T(8,128)(2,1)}), bf16[3072,4096]{1,0:T(8,128)(2,1)}) %all-gather.7.cloned.1.call-update) | async-done | bytes 25165840 | tf_op jit(solution)/shard_map/all_gather | solution.py:542
  557.4 16.9 %fusion.dx_ref = f32[4,96,4096]{2,1,0:T(8,128)} fusion(bf16[4,96,3072]{2,1,0:T(8,128)(2,1)} %copy-done.14, bf16[3072,4096]{1,0:T(8,128)(2,1)} %all-gather.7.cloned.1.call-done), kind=kOutput, calls=%fused_computation | convolution fusion | flops 9663676416 | bytes 33816576 | tf_op jit(solution)/shard_map/dot_general | solution.py:347
  574.3 149.9 %shard_map.171 = (f32[96,4096]{1,0:T(8,128)}, bf16[384,4096]{1,0:T(8,128)(2,1)}, bf16[128,4096]{1,0:T(8,128)(2,1)}) custom-call(f32[4,96,4096]{2,1,0:T(8,128)} %fusion.dx_ref, bf16[4,96,4096]{2,1,0:T(8,128)(2,1)} %copy-done.1, bf16[2,96,4096]{2,1,0:T(8,128)(2,1)} %copy-done.7, bf16[96,4096]{1,0:T(8,128)(2,1)} %copy-done.13, ...), custom_call_target="tpu_custom_call" | custom-call | tf_op jit(solution)/shard_map/pallas_call | solution.py:324
  724.3 2.6 fusion.13
  726.8 0.2 slice_bitcast_fusion
  727.1 1.3 copy.51
  728.4 1.3 copy.50
  729.7 1.3 copy.49
  731.0 1.0 copy.53
  (76 shorter events, 0.3 us)
Async XLA Ops:
  7.2 157.4 %all-gather.9.cloned.1.call-start = ((), (), s32[]{:S(2)}) async-start(), calls=%async_computation.2 | async-start | bytes 25952256 | tf_op jit(solution)/shard_map/all_gather | solution.py:506
  7.9 272.4 %all-gather.5.cloned.1.call-start = ((), (), s32[]{:S(2)}) async-start(), calls=%async_computation | async-start | bytes 9437184 | tf_op jit(solution)/shard_map/all_gather | solution.py:508
  164.6 8.2 %copy-start = (bf16[1,3072,4096]{2,1,0:T(8,128)(2,1)S(1)}, bf16[1,3072,4096]{2,1,0:T(8,128)(2,1)}, u32[]{:S(2)}) copy-start(bf16[1,3072,4096]{2,1,0:T(8,128)(2,1)} %all-gather.9.cloned.1.call-done) | copy-start | bytes 75497472
  172.7 1.2 copy-start.8
  174.0 1.1 copy-start.33
  174.0 1.1 copy-start.34
  174.0 1.2 copy-start.32
  175.0 1.2 copy-start.24
  175.0 2.5 copy-start.25
  175.0 382.4 %all-gather.7.cloned.1.call-start = ((), (), s32[]{:S(2)}) async-start(), calls=%async_computation.1 | async-start | bytes 28311552 | tf_op jit(solution)/shard_map/all_gather | solution.py:542
  178.8 2.4 copy-start.26
  197.5 28.9 %copy-start.17 = (f32[3072,128]{0,1:T(8,128)}, f32[3072,128]{0,1:T(8,128)S(1)}, u32[]{:S(2)}) copy-start(f32[3072,128]{0,1:T(8,128)S(1)} %get-tuple-element.85) | copy-start | bytes 4718596
  211.5 14.8 %copy-start.19 = (f32[3072,128]{0,1:T(8,128)}, f32[3072,128]{0,1:T(8,128)S(1)}, u32[]{:S(2)}) copy-start(f32[3072,128]{0,1:T(8,128)S(1)} %get-tuple-element.83) | copy-start | bytes 4718596
  230.6 13.5 %copy-start.9 = (bf16[3072,128]{1,0:T(8,128)(2,1)}, bf16[3072,128]{1,0:T(8,128)(2,1)S(1)}, u32[]{:S(2)}) copy-start(bf16[3072,128]{1,0:T(8,128)(2,1)S(1)} %copy.36.k_ref) | copy-start | bytes 2359300
  230.7 1.5 copy-start.30
  232.2 12.0 %copy-start.11 = (bf16[3072,128]{1,0:T(8,128)(2,1)}, bf16[3072,128]{1,0:T(8,128)(2,1)S(1)}, u32[]{:S(2)}) copy-start(bf16[3072,128]{1,0:T(8,128)(2,1)S(1)} %copy.35.q_ref) | copy-start | bytes 2359300
  244.2 15.5 %copy-start.15 = (bf16[3072,128]{1,0:T(8,128)(2,1)}, bf16[3072,128]{1,0:T(8,128)(2,1)S(1)}, u32[]{:S(2)}) copy-start(bf16[3072,128]{1,0:T(8,128)(2,1)S(1)} %convolution_convert_fusion.v_ref) | copy-start | bytes 2359300
  279.4 0.9 copy-start.6
  356.9 1.1 copy-start.21
  357.1 1.5 copy-start.29
  358.7 40.3 %copy-start.3 = (bf16[384,4096]{1,0:T(8,128)(2,1)S(1)}, bf16[384,4096]{1,0:T(8,128)(2,1)}, u32[]{:S(2)}) copy-start(bf16[384,4096]{1,0:T(8,128)(2,1)} %pad_maximum_fusion.value_ref) | copy-start | bytes 9437188
  360.1 37.6 %copy-start.4 = (bf16[96,4096]{1,0:T(8,128)(2,1)}, bf16[96,4096]{1,0:T(8,128)(2,1)S(1)}, u32[]{:S(2)}) copy-start(bf16[96,4096]{1,0:T(8,128)(2,1)S(1)} %get-tuple-element.64.x_ref.d_ref) | copy-start | bytes 2359300
  397.7 1.2 copy-start.7
  398.9 4.4 copy-start.1
  399.1 1.8 copy-start.2
  403.3 28.7 %copy-start.16 = (bf16[3072,128]{1,0:T(8,128)(2,1)S(1)}, bf16[3072,128]{1,0:T(8,128)(2,1)}, u32[]{:S(2)}) copy-start(bf16[3072,128]{1,0:T(8,128)(2,1)} %copy-done.15) | copy-start | bytes 2359300
  409.4 22.6 %copy-start.10 = (bf16[3072,128]{1,0:T(8,128)(2,1)S(1)}, bf16[3072,128]{1,0:T(8,128)(2,1)}, u32[]{:S(2)}) copy-start(bf16[3072,128]{1,0:T(8,128)(2,1)} %copy-done.9) | copy-start | bytes 2359300
  409.4 22.6 %copy-start.12 = (bf16[3072,128]{1,0:T(8,128)(2,1)S(1)}, bf16[3072,128]{1,0:T(8,128)(2,1)}, u32[]{:S(2)}) copy-start(bf16[3072,128]{1,0:T(8,128)(2,1)} %copy-done.11) | copy-start | bytes 2359300
  457.9 2.0 copy-start.23
  459.9 3.5 copy-start.18
  459.9 3.5 copy-start.20
  481.4 1.1 copy-start.27
  485.3 3.1 copy-start.5
  543.3 0.9 copy-start.13
  544.1 1.5 copy-start.14
  574.3 149.9 %copy-start.22 = (bf16[1,96,4096]{2,1,0:T(8,128)(2,1)S(1)}, bf16[1,96,4096]{2,1,0:T(8,128)(2,1)}, u32[]{:S(2)}) copy-start(bf16[1,96,4096]{2,1,0:T(8,128)(2,1)} %param.17) | copy-start | bytes 2359300
  724.2 2.6 copy-start.28
  729.7 1.3 copy-start.31
Sparse Core Ops, SparseCore 0:
  10.8 153.6 all-gather.8
  175.2 80.3 all-gather.4
  401.1 156.2 all-gather.6

commit v2 on v1

v2 whole, which is shorter than its diff:
```python
import functools

import jax
import jax.numpy as jnp
from jax import lax
from jax.experimental import pallas as pl
from jax.experimental.pallas import tpu as pltpu
from jax.sharding import PartitionSpec as P

HEAD_SIZE = 128
ROPE_THETA = 500000.0
NORM_EPS = 1e-6
LOG2E = 1.4426950408889634
ATTN_SCALE = HEAD_SIZE ** -0.5
MESH = pl.DeviceIdType.MESH
VMEM = pl.BlockSpec(memory_space=pltpu.VMEM)
BLOCK = 512


def rope_tables(seq_len):
    half_dim = HEAD_SIZE // 2
    inv_freq = 1.0 / (ROPE_THETA ** (jnp.arange(half_dim, dtype=jnp.float32) / half_dim))
    angles = jnp.arange(seq_len, dtype=jnp.float32)[:, None] * inv_freq[None, :]
    return jnp.cos(angles), jnp.sin(angles)


def rotate(values, cos_t, sin_t):
    lower_half, upper_half = jnp.split(values, 2, axis=-1)
    return jnp.concatenate([lower_half * cos_t - upper_half * sin_t, upper_half * cos_t + lower_half * sin_t], axis=-1)


def rotate_back(values, cos_t, sin_t):
    lower_half, upper_half = jnp.split(values, 2, axis=-1)
    return jnp.concatenate([lower_half * cos_t + upper_half * sin_t, upper_half * cos_t - lower_half * sin_t], axis=-1)


SEMAPHORES = 72
DEPTH = 1024
CHUNKS = 4
TILE = 512
ANY = pl.BlockSpec(memory_space=pl.ANY)


def position(d):
    return d // 8, d // 2 % 4, d % 2


def member_of(d):
    z, _, core = position(d)
    return z * 2 + core


def column_peer(me, k):
    member = (member_of(me) + k) % 8
    return member // 2 * 8 + position(me)[1] * 2 + member % 2


def plane_peer(me, k):
    return me - me % 8 + (me + k) % 8


def ring_peer(me, k):
    z, c, core = position(me)
    return z * 8 + (c + k) % 4 * 2 + core


def line_peer(me, k):
    return (me + k * 8) % 32


def ring_steps(c, core):
    step_x, step_y = 1 - c % 2 * 2, 2 - c // 2 * 4
    step1 = step_x * (1 - core) + step_y * core
    return step1, step_x + step_y - step1


def greet(peers):
    barrier = pltpu.get_barrier_semaphore()
    for peer in peers:
        pl.semaphore_signal(barrier, inc=1, device_id=(peer,), device_id_type=MESH)
    pl.semaphore_wait(barrier, len(peers))


def remote(src, dst, sems, slot, peer):
    return pltpu.make_async_remote_copy(
        src_ref=src, dst_ref=dst, send_sem=sems[0].at[slot], recv_sem=sems[1].at[slot], device_id=(peer,), device_id_type=MESH)


class Copies:
    def __init__(self, sems):
        self.sems, self.used = sems, 0

    def send(self, src, dst, peer):
        copy = remote(src, dst, self.sems, self.used, peer)
        copy.start()
        self.used += 1
        return copy

    def local(self, src, dst):
        copy = pltpu.make_async_copy(src, dst, self.sems[2].at[self.used])
        copy.start()
        self.used += 1
        return copy


def wait_all(copies):
    for copy in copies:
        copy.wait()


def call(kernel, out_shape, operands, in_specs, out_specs, scratch, collective_id, mib):
    return pl.pallas_call(
        kernel, out_shape=out_shape, in_specs=in_specs, out_specs=out_specs,
        scratch_shapes=list(scratch) + [pltpu.SemaphoreType.DMA((SEMAPHORES,))] * 3,
        compiler_params=pltpu.CompilerParams(collective_id=collective_id, has_side_effects=True, vmem_limit_bytes=mib << 20),
    )(*operands)


def shape(dims, dtype):
    return jax.ShapeDtypeStruct(tuple(dims), dtype)


def part(index, size):
    return pl.ds(pl.multiple_of(index * size, size), size)


def add_rows(ref, other, start, count):
    def add(i, carry):
        rows = part(start // 8 + i, 8)
        ref[rows, :] = ref[rows, :] + other[rows, :]
        return carry

    lax.fori_loop(0, count // 8, add, 0)


def exchange_kernel(peer_of, count, source, target, x_ref, out_ref, *sems):
    me, copies = lax.axis_index('tp'), Copies(sems)
    peers = [peer_of(me, k) for k in range(1, count)]
    greet(peers)
    started = [copies.send(source(x_ref, peer), target(out_ref, me), peer) for peer in peers]
    target(out_ref, me)[...] = source(x_ref, me)[...]
    wait_all(started)


def exchange(x, out_shape, peer_of, count, source, target, collective_id):
    kernel = functools.partial(exchange_kernel, peer_of, count, source, target)
    return call(kernel, shape(out_shape, x.dtype), (x,), [VMEM], VMEM, [], collective_id, 24)


def all_sum_kernel(x_ref, out_ref, plane, middle, line, *sems):
    me, copies = lax.axis_index('tp'), Copies(sems)
    z, mine = me // 8, me % 8
    plane_peers = [plane_peer(me, k) for k in range(1, 8)]
    line_peers = [line_peer(me, k) for k in range(1, 4)]
    greet(plane_peers + line_peers)
    started = [copies.send(x_ref, plane.at[mine], peer) for peer in plane_peers]
    plane[mine] = x_ref[...]
    wait_all(started)
    total = plane[0]
    for k in range(1, 8):
        total = total + plane[k]
    middle[...] = total
    line[z] = total
    wait_all([copies.send(middle, line.at[z], peer) for peer in line_peers])
    out_ref[...] = (line[0] + line[1]) + (line[2] + line[3])


def all_sum(x, collective_id):
    scratch = [pltpu.VMEM((8,) + x.shape, x.dtype), pltpu.VMEM(x.shape, x.dtype), pltpu.VMEM((4,) + x.shape, x.dtype)]
    return call(all_sum_kernel, shape(x.shape, x.dtype), (x,), [VMEM], VMEM, scratch, collective_id, 8)


def ring_sum_kernel(x_ref, out_ref, passing, direct, last, *sems):
    me, copies = lax.axis_index('tp'), Copies(sems)
    _, c, core = position(me)
    step1, step2 = ring_steps(c, core)
    first, second = me + step1 * 2, me + step2 * 2
    greet([first, second])
    chunk = out_ref.shape[0] // CHUNKS
    pieces = [pl.ds(i * chunk, chunk) for i in range(CHUNKS)]
    hops = [copies.send(x_ref.at[c + step1 + step2, p, :], passing.at[p, :], first) for p in pieces]
    sums = [copies.send(x_ref.at[c + step1], direct, first)]
    for i, p in enumerate(pieces):
        hops[i].wait()
        add_rows(passing, x_ref.at[c + step2], i * chunk, chunk)
        sums.append(copies.send(passing.at[p, :], last.at[p, :], second))
    wait_all(sums)

    def add(i, carry):
        rows = part(i, 8)
        out_ref[rows, :] = (x_ref[c, rows, :] + direct[rows, :]) + last[rows, :]
        return carry

    lax.fori_loop(0, out_ref.shape[0] // 8, add, 0)


def ring_sum(x, collective_id):
    dims = x.shape[1:]
    return call(ring_sum_kernel, shape(dims, x.dtype), (x,), [VMEM], VMEM, [pltpu.VMEM(dims, x.dtype)] * 3, collective_id, 32)


def spread_kernel(x_ref, ring_ref, near_ref, *sems):
    me, copies = lax.axis_index('tp'), Copies(sems)
    ring = [ring_peer(me, k) for k in range(1, 4)]
    line = [line_peer(me, k) for k in (1, 3)]
    greet(ring + line)
    mine = position(me)[1]
    started = [copies.send(x_ref, ring_ref.at[mine], peer) for peer in ring]
    started += [copies.send(x_ref, near_ref.at[i], peer) for i, peer in enumerate(line)]
    ring_ref[mine] = x_ref[...]
    wait_all(started)


def spread(x, collective_id):
    out = (shape((4,) + x.shape, x.dtype), shape((2,) + x.shape, x.dtype))
    return call(spread_kernel, out, (x,), [VMEM], (VMEM, VMEM), [], collective_id, 24)


def plane_kernel(qk_ref, v_ref, near_ref, out_qk, out_v, far_ref, *sems):
    me, copies = lax.axis_index('tp'), Copies(sems)
    peers = [plane_peer(me, k) for k in range(1, 8)]
    up, down = line_peer(me, 1), line_peer(me, 3)
    greet(peers + [up, down])
    mine = me % 8
    started = [copies.send(near_ref.at[0], far_ref, up)]
    for src, dst in ((qk_ref, out_qk), (v_ref, out_v)):
        columns = part(mine, src.shape[-1])
        started += [copies.send(src.at[:, peer % 8], dst.at[:, :, columns], peer) for peer in peers]
        dst[:, :, columns] = src[:, mine]
    wait_all(started)


def plane_exchange(qk, v, near, collective_id):
    outs = tuple(shape((4, a.shape[2], 8 * a.shape[3]), a.dtype) for a in (qk, v)) + (shape(near.shape[1:], near.dtype),)
    return call(plane_kernel, outs, (qk, v, near), [VMEM, VMEM, ANY], (VMEM, VMEM, VMEM), [], collective_id, 24)


def final_kernel(dqk_ref, dv_ref, wqk_ref, wv_ref, ring_ref, near_ref, far_ref, dw_ref, o_ref, x_ref, sum_ref, gw_ref, gwo_ref,
                 dx, above, below, passing, full, buf, tile_sem, line_send, line_recv, *sems):
    me, copies = lax.axis_index('tp'), Copies(sems)
    z, c, core = position(me)
    partner = me + 1 - core * 2
    up, down = line_peer(me, 1), line_peer(me, 3)
    z_up, z_far, z_down = up // 8, line_peer(me, 2) // 8, down // 8
    ring = [ring_peer(me, k) for k in range(1, 4)]
    greet([up, down, partner] + ring)
    tiles = x_ref.shape[1] // TILE
    depth = dqk_ref.shape[1]
    line_sems = (line_send, line_recv)

    def fetch_w(j, b):
        return [pltpu.make_async_copy(wqk_ref.at[:, part(j, TILE)], buf.at[b, pl.ds(0, depth), :], tile_sem.at[0, b]),
                pltpu.make_async_copy(wv_ref.at[:, part(j, TILE)], buf.at[b, pl.ds(depth, dv_ref.shape[1]), :], tile_sem.at[1, b])]

    def fetch_x(j, b):
        return [pltpu.make_async_copy(x_ref.at[:, part(j, TILE)], buf.at[b], tile_sem.at[0, b])]

    for copy in fetch_w(0, 0):
        copy.start()
    planes, lines = [z_down, z_up, z_far], [near_ref.at[0], near_ref.at[1], far_ref]

    def slot(plane, column):
        return full.at[plane * 8 + column * 2 + core]

    rounds, shared, local = [], [], []
    for plane, block in zip(planes, lines):
        rounds += [copies.send(block, slot(plane, c), peer) for peer in ring]
    held = [(block, slot(plane, c)) for plane, block in zip(planes, lines)]
    held += [(ring_ref.at[column], slot(z, column)) for column in range(4)]
    for block, place in held:
        shared.append(copies.send(block, place, partner))
        local.append(copies.local(block, place))

    def hop(j):
        return remote(dx.at[z_far, :, part(j, TILE)], passing.at[:, part(j, TILE)], line_sems, j, up)

    def direct(j):
        return remote(dx.at[z_down, :, part(j, TILE)], above.at[:, part(j, TILE)], line_sems, tiles + j, down)

    def onward(j):
        return remote(passing.at[:, part(j, TILE)], below.at[:, part(j, TILE)], line_sems, tiles * 2 + j, up)

    def input_grad(j, carry):
        b = j % 2

        @pl.when(j + 1 < tiles)
        def _():
            for copy in fetch_w(j + 1, 1 - b):
                copy.start()

        wait_all(fetch_w(j, b))
        values = nn(dqk_ref[...], buf[b, :depth, :]) + nn(dv_ref[...], buf[b, depth:, :])
        dx[:, :, part(j, TILE)] = values.reshape(dx.shape[0], dx.shape[1], TILE)

        @pl.when(j > 0)
        def _():
            hop(j - 1).start()
            direct(j - 1).start()

        return carry

    lax.fori_loop(0, tiles, input_grad, 0)
    for copy in fetch_x(0, 0):
        copy.start()

    def weight_grad(j, carry):
        b = j % 2

        @pl.when(j + 1 < tiles)
        def _():
            for copy in fetch_x(j + 1, 1 - b):
                copy.start()

        wait_all(fetch_x(j, b))

        @pl.when(j == 0)
        def _():
            hop(tiles - 1).start()
            direct(tiles - 1).start()

        hop(j).wait()
        passing[:, part(j, TILE)] = passing[:, part(j, TILE)] + dx[z_up, :, part(j, TILE)]
        gw_ref[:, part(j, TILE)] = nn(dw_ref[...], buf[b]).astype(gw_ref.dtype)
        onward(j).start()
        return carry

    lax.fori_loop(0, tiles, weight_grad, 0)
    for i, copy in enumerate(rounds):
        copy.wait()
        block = slot(planes[i // 3], (c + 3 - i % 3) % 4)
        shared.append(copies.send(block, block, partner))

    def finish(j, carry):
        direct(j).wait()
        onward(j).wait()
        tile = part(j, TILE)
        sum_ref[:, tile] = (dx[z, :, tile] + above[:, tile]) + below[:, tile]
        return carry

    lax.fori_loop(0, tiles, finish, 0)
    wait_all(local + shared)

    def out_grad(j, carry):
        d = full[:, :, part(j, TILE)]
        gwo_ref[:, part(j, TILE)] = nn(o_ref[...], d.reshape(o_ref.shape[1], TILE)).astype(gwo_ref.dtype)
        return carry

    lax.fori_loop(0, tiles, out_grad, 0)


def final(dqk, dv, wqk, wv, d_ring, d_near, d_far, dw_rows, o_rows, x_full, collective_id):
    rows, model_dim = d_far.shape
    seq_len = x_full.shape[0]
    bf16, f32 = d_far.dtype, jnp.float32
    block = pltpu.VMEM((rows, model_dim), f32)
    scratch = [pltpu.VMEM((dqk.shape[0] // rows, rows, model_dim), f32), block, block, block,
               pltpu.VMEM((seq_len // rows, rows, model_dim), bf16), pltpu.VMEM((2, seq_len, TILE), bf16), pltpu.SemaphoreType.DMA((2, 2)),
               pltpu.SemaphoreType.DMA((SEMAPHORES,)), pltpu.SemaphoreType.DMA((SEMAPHORES,))]
    outs = (shape(d_far.shape, f32), shape((dw_rows.shape[0], model_dim), bf16), shape((o_rows.shape[0], model_dim), bf16))
    return call(final_kernel, outs, (dqk, dv, wqk, wv, d_ring, d_near, d_far, dw_rows, o_rows, x_full),
                [VMEM, VMEM, ANY, ANY, ANY, ANY, ANY, VMEM, VMEM, ANY], (VMEM, VMEM, VMEM),
                scratch, collective_id, 60)


def gather_kernel(x_ref, wq_ref, wk_ref, wv_ref, wo_ref, out_ref, q_ref, k_ref, v_ref, col_ref,
                  full, weights, total, *sems):
    me, copies = lax.axis_index('tp'), Copies(sems)
    z, c, core = position(me)
    partner = me + 1 - core * 2
    step1, step2 = ring_steps(c, core)
    first, second = me + step1 * 2, me + step2 * 2
    up, far, down = [line_peer(me, k) for k in range(1, 4)]
    planes = [z, down // 8, up // 8, far // 8]
    direct, corner = (0, 1, 3, 5), (2, 4, 6, 7)

    def slot(plane, column):
        return full.at[plane * 8 + column * 2 + core]

    own = copies.local(x_ref, slot(z, c))
    loads = [copies.local(ref, weights.at[:, pl.ds(i * HEAD_SIZE, HEAD_SIZE)]) for i, ref in enumerate((wq_ref, wk_ref, wv_ref))]
    greet([up, down, first, second, partner])
    own.wait()
    line = {i: copies.send(slot(z, c), slot(z, c), peer) for i, peer in ((1, up), (2, down))}
    to_first, to_second, to_partner, stores = {}, {}, {}, []

    def forward(s, column, index, slot_of):
        block = slot(planes[s], column)
        if index is not None:
            to_second[index] = copies.send(block, block, second)
        to_partner[slot_of] = copies.send(block, block, partner)

    def pass_on(s):
        block = slot(planes[s], c)
        to_first[s] = copies.send(block, block, first)
        forward(s, c, direct[s], s)

    def from_line(s):
        line[s].wait()
        pass_on(s)

    head, head_line, head_partner = (lambda plane: col_ref.at[plane * 2 + core]), {}, []

    def head_from_line(s):
        head_line[s].wait()
        block = head(planes[s])
        if s == 1:
            head_line[3] = copies.send(block, block, up)
        head_partner.append(copies.send(block, block, partner))

    def from_first(s):
        to_first[s].wait()
        forward(s, c + step1, corner[s], 4 + s)

    def from_second(i):
        to_second[i].wait()
        if i in direct:
            forward(direct.index(i), c + step2, None, 8 + i)
        else:
            forward(corner.index(i), c + step2 + step1, None, 8 + i)

    def multiply(s, column, slot_of):
        to_partner[slot_of].wait()
        pair = planes[s] * 4 + column
        blocks = pl.ds(pair * 2, 2)
        stores.append(copies.local(full.at[blocks], out_ref.at[blocks]))
        rows = part(pair, total.shape[0])
        total[...] = jnp.zeros_like(total)

        def chunk(i, carry):
            depth = part(i, DEPTH)
            a = full[blocks, :, depth].reshape(rows.size, DEPTH)
            total[...] += nn(a, weights[depth, :])
            return carry

        lax.fori_loop(0, weights.shape[0] // DEPTH, chunk, 0)
        q_ref[rows, :] = total[:, :HEAD_SIZE]
        k_ref[rows, :] = total[:, HEAD_SIZE:2 * HEAD_SIZE]
        v_ref[rows, :] = total[:, 2 * HEAD_SIZE:].astype(v_ref.dtype)

    def multiply_own(s):
        multiply(s, c, s)

    def multiply_sides(s):
        multiply(s, c + step1, 8 + direct[s])
        multiply(s, c + step2, 4 + s)

    def multiply_corner(s):
        multiply(s, c + step1 + step2, 8 + corner[s])

    pass_on(0)
    from_line(1)
    line[3] = copies.send(slot(planes[1], c), slot(planes[1], c), up)
    own_head = copies.local(wo_ref, head(z))
    head_line[1] = copies.send(wo_ref, head(z), up)
    head_line[2] = copies.send(wo_ref, head(z), down)
    head_partner.append(copies.send(wo_ref, head(z), partner))
    from_first(0)
    wait_all(loads)
    multiply_own(0)
    from_second(0)
    from_line(2)
    from_first(1)
    multiply_own(1)
    from_second(1)
    from_first(2)
    from_line(3)
    multiply_own(2)
    from_second(2)
    head_from_line(1)
    multiply_sides(0)
    from_first(3)
    multiply_own(3)
    from_second(3)
    multiply_sides(1)
    from_second(4)
    multiply_corner(0)
    from_second(5)
    multiply_sides(2)
    head_from_line(2)
    from_second(6)
    multiply_sides(3)
    multiply_corner(1)
    from_second(7)
    multiply_corner(2)
    multiply_corner(3)
    head_from_line(3)
    wait_all(stores + [own_head] + head_partner)


def gather(x, wq, wk, wv, wo, devices, collective_id):
    rows, model_dim = x.shape
    f32 = jnp.float32
    head = (devices * rows, HEAD_SIZE)
    outs = (shape((devices, rows, model_dim), x.dtype), shape(head, f32), shape(head, f32), shape(head, x.dtype),
            shape((8,) + wo.shape, wo.dtype))
    width = 3 * HEAD_SIZE
    scratch = [pltpu.VMEM((devices, rows, model_dim), x.dtype), pltpu.VMEM((model_dim, width), x.dtype), pltpu.VMEM((2 * rows, width), f32)]
    return call(gather_kernel, outs, (x, wq, wk, wv, wo), [ANY] * 5, (ANY, VMEM, VMEM, VMEM, ANY), scratch, collective_id, 44)


def nt(a, b):
    return lax.dot_general(a, b, (((1,), (1,)), ((), ())), preferred_element_type=jnp.float32)


def tn(a, b):
    return lax.dot_general(a, b, (((0,), (0,)), ((), ())), preferred_element_type=jnp.float32)


def nn(a, b):
    return lax.dot_general(a, b, (((1,), (0,)), ((), ())), preferred_element_type=jnp.float32)


def fold_rows(values, op):
    return op(values.reshape(values.shape[0] // 8, 8, values.shape[1]), axis=0)


def block_rows(j):
    return pl.ds(pl.multiple_of(j * BLOCK, BLOCK), BLOCK)


def diagonal_mask():
    keys = lax.broadcasted_iota(jnp.int32, (BLOCK, BLOCK), 0)
    queries = lax.broadcasted_iota(jnp.int32, (BLOCK, BLOCK), 1)
    return keys <= queries


def attention_kernel(q_ref, k_ref, v_ref, o_ref, max_ref, inv_ref, s_scr, acc_scr):
    i = pl.program_id(0)
    q_blk = q_ref[...]

    def score(j, top):
        s = nt(k_ref[block_rows(j), :], q_blk) * (ATTN_SCALE * LOG2E)
        s_scr[block_rows(j), :] = s
        return jnp.maximum(top, fold_rows(s, jnp.max))

    s = jnp.where(diagonal_mask(), nt(k_ref[block_rows(i), :], q_blk) * (ATTN_SCALE * LOG2E), -1e30)
    s_scr[block_rows(i), :] = s
    top = lax.fori_loop(0, i, score, fold_rows(s, jnp.max))
    top = jnp.max(top, axis=0, keepdims=True)

    def weigh(j, total):
        p = jnp.exp2(s_scr[block_rows(j), :] - top)
        s_scr[block_rows(j), :] = p
        return total + fold_rows(p, jnp.sum)

    total = lax.fori_loop(0, i + 1, weigh, jnp.zeros((8, BLOCK), jnp.float32))
    inv = 1.0 / jnp.sum(total, axis=0, keepdims=True)
    max_ref[...] = top
    inv_ref[...] = inv
    acc_scr[...] = jnp.zeros_like(acc_scr)

    def gather(j, carry):
        p = (s_scr[block_rows(j), :] * inv).astype(jnp.bfloat16)
        acc_scr[...] += tn(v_ref[block_rows(j), :], p)
        return carry

    lax.fori_loop(0, i + 1, gather, 0)
    o_ref[...] = acc_scr[...].T.astype(jnp.bfloat16)


def attention(q, k, v):
    seq_len = q.shape[0]
    steps = seq_len // BLOCK
    rows = pl.BlockSpec((BLOCK, HEAD_SIZE), lambda i: (i, 0))
    whole = pl.BlockSpec((seq_len, HEAD_SIZE), lambda i: (0, 0))
    line = pl.BlockSpec((1, BLOCK), lambda i: (0, i))
    return pl.pallas_call(
        attention_kernel,
        grid=(steps,),
        out_shape=(jax.ShapeDtypeStruct((seq_len, HEAD_SIZE), jnp.bfloat16),
                   jax.ShapeDtypeStruct((1, seq_len), jnp.float32),
                   jax.ShapeDtypeStruct((1, seq_len), jnp.float32)),
        in_specs=[rows, whole, whole], out_specs=(rows, line, line),
        scratch_shapes=[pltpu.VMEM((seq_len, BLOCK), jnp.float32), pltpu.VMEM((HEAD_SIZE, BLOCK), jnp.float32)],
        compiler_params=pltpu.CompilerParams(dimension_semantics=("arbitrary",), vmem_limit_bytes=40 << 20),
        cost_estimate=pl.CostEstimate(flops=8 * seq_len * seq_len * HEAD_SIZE, bytes_accessed=8 * seq_len * HEAD_SIZE, transcendentals=0),
    )(q, k, v)


def attention_grad_kernel(q_ref, k_ref, v_ref, do_ref, max_ref, inv_ref, dq_ref, dk_ref, dv_ref, p_scr, dp_scr, dq_scr, dk_scr, dv_scr):
    i = pl.program_id(0)
    q_blk, do_blk = q_ref[...], do_ref[...]
    top, inv = max_ref[...], inv_ref[...]

    @pl.when(i == 0)
    def _():
        dk_scr[...] = jnp.zeros_like(dk_scr)
        dv_scr[...] = jnp.zeros_like(dv_scr)

    def scores(j, mask, delta):
        rows = block_rows(j)
        s = nt(k_ref[rows, :], q_blk) * (ATTN_SCALE * LOG2E)
        if mask is not None:
            s = jnp.where(mask, s, -1e30)
        p = jnp.exp2(s - top) * inv
        dp = nt(v_ref[rows, :], do_blk)
        p_scr[rows, :] = p
        dp_scr[rows, :] = dp
        dv_scr[rows, :] += nn(p.astype(jnp.bfloat16), do_blk)
        return delta + fold_rows(p * dp, jnp.sum)

    delta = scores(i, diagonal_mask(), jnp.zeros((8, BLOCK), jnp.float32))
    delta = lax.fori_loop(0, i, lambda j, d: scores(j, None, d), delta)
    delta = jnp.sum(delta, axis=0, keepdims=True)
    dq_scr[...] = jnp.zeros_like(dq_scr)

    def grads(j, carry):
        rows = block_rows(j)
        ds = (p_scr[rows, :] * (dp_scr[rows, :] - delta) * ATTN_SCALE).astype(jnp.bfloat16)
        dk_scr[rows, :] += nn(ds, q_blk)
        dq_scr[...] += tn(k_ref[rows, :], ds)
        return carry

    lax.fori_loop(0, i + 1, grads, 0)
    dq_ref[...] = dq_scr[...].T

    @pl.when(i == pl.num_programs(0) - 1)
    def _():
        dk_ref[...] = dk_scr[...]
        dv_ref[...] = dv_scr[...].astype(jnp.bfloat16)


def attention_grad(q, k, v, do, top, inv):
    seq_len = q.shape[0]
    steps = seq_len // BLOCK
    rows = pl.BlockSpec((BLOCK, HEAD_SIZE), lambda i: (i, 0))
    whole = pl.BlockSpec((seq_len, HEAD_SIZE), lambda i: (0, 0))
    line = pl.BlockSpec((1, BLOCK), lambda i: (0, i))
    full = (seq_len, HEAD_SIZE)
    return pl.pallas_call(
        attention_grad_kernel,
        grid=(steps,),
        out_shape=(jax.ShapeDtypeStruct(full, jnp.float32), jax.ShapeDtypeStruct(full, jnp.float32), jax.ShapeDtypeStruct(full, jnp.bfloat16)),
        in_specs=[rows, whole, whole, rows, line, line], out_specs=(rows, whole, whole),
        scratch_shapes=[pltpu.VMEM((seq_len, BLOCK), jnp.float32), pltpu.VMEM((seq_len, BLOCK), jnp.float32),
                        pltpu.VMEM((HEAD_SIZE, BLOCK), jnp.float32), pltpu.VMEM(full, jnp.float32), pltpu.VMEM(full, jnp.float32)],
        compiler_params=pltpu.CompilerParams(dimension_semantics=("arbitrary",), vmem_limit_bytes=48 << 20),
        cost_estimate=pl.CostEstimate(flops=20 * seq_len * seq_len * HEAD_SIZE, bytes_accessed=20 * seq_len * HEAD_SIZE, transcendentals=0),
    )(q, k, v, do, top, inv)


COLUMN_GROUPS = [[z * 8 + c * 2 + core for z in range(4) for core in range(2)] for c in range(4)]
PLANE_GROUPS = [[z * 8 + p for p in range(8)] for z in range(4)]


def after_kernel(value_ref, *refs):
    refs[-1][...] = value_ref[...]


def after(value, *others):
    anywhere = pl.BlockSpec(memory_space=pl.ANY)
    return pl.pallas_call(
        after_kernel,
        out_shape=jax.ShapeDtypeStruct(value.shape, value.dtype),
        in_specs=[VMEM] + [anywhere] * len(others), out_specs=VMEM,
        compiler_params=pltpu.CompilerParams(vmem_limit_bytes=8 << 20),
        cost_estimate=pl.CostEstimate(flops=value.size, bytes_accessed=4 * value.size, transcendentals=0),
    )(value, *others)


def lane_rows(values):
    return values.reshape(-1, 128)


def local_block(x_loc, wq_loc, wk_loc, wv_loc, wo_loc, gq_loc, gk_loc, g_attn, dy_loc):
    x_loc, dy_loc = x_loc[0], dy_loc[0]
    rows, model_dim = x_loc.shape
    bf16, f32 = jnp.bfloat16, jnp.float32
    x_blocks, q_raw, k_raw, v_head, wo_blocks = gather(x_loc, wq_loc, wk_loc, wv_loc, wo_loc, 32, 9)
    wo_col = wo_blocks.reshape(8 * HEAD_SIZE, model_dim)
    x_full = x_blocks.reshape(32 * rows, model_dim)
    seq_len = x_full.shape[0]
    wv_plane = lax.all_gather(after(wv_loc.T, q_raw[:8]), 'tp', axis=0, tiled=True, axis_index_groups=PLANE_GROUPS)
    cos_t, sin_t = rope_tables(seq_len)
    stats = jnp.concatenate([lane_rows(jnp.sum(q_raw * q_raw, axis=-1)), lane_rows(jnp.sum(k_raw * k_raw, axis=-1))])
    sq_sums = all_sum(stats, 1).reshape(2, seq_len)
    inv_rms = lax.rsqrt(sq_sums / model_dim + NORM_EPS)[..., None]
    q_unit = q_raw * inv_rms[0]
    k_unit = k_raw * inv_rms[1]
    gq_f, gk_f = gq_loc.astype(f32), gk_loc.astype(f32)
    q_rot = rotate(q_unit * gq_f, cos_t, sin_t).astype(bf16)
    k_rot = rotate(k_unit * gk_f, cos_t, sin_t).astype(bf16)
    o_head, top, inv = attention(q_rot, k_rot, v_head)

    o_col = exchange(
        o_head.reshape(4, 4, 2, rows, HEAD_SIZE), (4, rows, 8 * HEAD_SIZE), column_peer, 8,
        lambda ref, d: ref.at[d // 8, :, d % 2],
        lambda ref, d: ref.at[:, :, part(member_of(d), HEAD_SIZE)], 2)
    a_part = nn(o_col.reshape(4 * rows, 8 * HEAD_SIZE), wo_col)
    attn_loc = ring_sum(a_part.reshape(4, rows, model_dim), 3)

    post_rms = lax.rsqrt(jnp.mean(attn_loc * attn_loc, axis=-1, keepdims=True) + NORM_EPS)
    normed = attn_loc * post_rms
    ga_f = g_attn.astype(f32)
    dy_f = dy_loc.astype(f32)
    y_loc = (x_loc.astype(f32) + normed * ga_f).astype(bf16)
    ga_part = jnp.sum(dy_f * normed, axis=0)
    g_normed = dy_f * ga_f
    d_attn = (post_rms * (g_normed - normed * jnp.mean(g_normed * normed, axis=-1, keepdims=True))).astype(bf16)

    d_ring, d_near = spread(d_attn, 4)
    wqk_plane = lax.all_gather(after(jnp.concatenate([wq_loc.T, wk_loc.T], axis=0), d_ring), 'tp', axis=0, tiled=True, axis_index_groups=PLANE_GROUPS)
    d_col = nt(d_ring.reshape(4 * rows, model_dim), wo_col).astype(bf16)
    d_head = exchange(
        d_col.reshape(4, rows, 8 * HEAD_SIZE), (4, 4, 2, rows, HEAD_SIZE), column_peer, 8,
        lambda ref, d: ref.at[:, :, part(member_of(d), HEAD_SIZE)],
        lambda ref, d: ref.at[d // 8, :, d % 2], 5).reshape(seq_len, HEAD_SIZE)

    dq_rot, dk_rot, d_value = attention_grad(q_rot, k_rot, v_head, d_head, top, inv)
    dq_hat = rotate_back(dq_rot, cos_t, sin_t)
    dk_hat = rotate_back(dk_rot, cos_t, sin_t)
    grad_gq = jnp.sum(dq_hat * q_unit, axis=0)
    grad_gk = jnp.sum(dk_hat * k_unit, axis=0)
    dq_unit = dq_hat * gq_f
    dk_unit = dk_hat * gk_f
    sums = jnp.concatenate([lane_rows(jnp.sum(dq_unit * q_unit, axis=-1)), lane_rows(jnp.sum(dk_unit * k_unit, axis=-1)), lane_rows(ga_part)])
    sums = all_sum(sums, 6)
    dots_rows = 2 * seq_len // 128
    unit_dots = sums[:dots_rows].reshape(2, seq_len)[..., None] / model_dim
    grad_ga = sums[dots_rows:].reshape(model_dim)
    dq_raw = (inv_rms[0] * (dq_unit - q_unit * unit_dots[0])).astype(bf16)
    dk_raw = (inv_rms[1] * (dk_unit - k_unit * unit_dots[1])).astype(bf16)
    d_qk = jnp.concatenate([dq_raw, dk_raw], axis=1)
    dw_rows = jnp.concatenate([dq_raw.T, dk_raw.T, d_value.T], axis=0)

    dqk_plane, dv_plane, d_far = plane_exchange(
        d_qk.reshape(4, 8, rows, 2 * HEAD_SIZE), d_value.reshape(4, 8, rows, HEAD_SIZE), d_near, 7)
    dx_loc, grad_w, grad_wo = final(
        dqk_plane.reshape(4 * rows, 16 * HEAD_SIZE), dv_plane.reshape(4 * rows, 8 * HEAD_SIZE), wqk_plane, wv_plane,
        d_ring, d_near, d_far, dw_rows, o_head.T, x_full, 8)
    grad_x = (dx_loc + dy_f).astype(bf16)
    grad_wq, grad_wk, grad_wv = [grad_w[i * HEAD_SIZE:(i + 1) * HEAD_SIZE].T for i in range(3)]
    return (y_loc[None], grad_x[None], grad_wq, grad_wk, grad_wv, grad_wo,
            grad_gq.astype(bf16), grad_gk.astype(bf16), grad_ga.astype(bf16))


def solution(mesh):
    act_spec = P(None, 'tp', None)
    col_spec = P(None, 'tp')
    row_spec = P('tp', None)
    vec_spec = P('tp')
    in_specs = (act_spec, col_spec, col_spec, col_spec, row_spec, vec_spec, vec_spec, P(), act_spec)
    out_specs = (act_spec, act_spec, col_spec, col_spec, col_spec, row_spec, vec_spec, vec_spec, P())
    return jax.shard_map(local_block, mesh=mesh, in_specs=in_specs, out_specs=out_specs, check_vma=False)
```

time: 739 us -> 589 us (0.80)
  the two profiles are of different devices: /device:TPU:11 before, /device:TPU:0 now
where the time goes in v2:
time: 589 us; the launch traced here: 588 us
  Pallas kernels  497 us (84%)
  local copies, waits for them, and re-layouts  44 us (7%)
  other arithmetic  22.3 us (4%)
  between operations  14.7 us (2%)
  matrix products  9.45 us (2%)
    pallas_call x9, Pallas kernels, call(): pl.pallas_call(kernel, out_shape=out_shape, in_specs=in_specs, out_specs=...  459 us
    unnamed x113, local copies, waits for them, and re-layouts  30.2 us
    pallas_call x1, Pallas kernels, attention_grad(): pl.pallas_call(attention_grad_kernel, grid=(steps,), out_shape=(jax.Shape...  23 us
    pallas_call x1, Pallas kernels, attention(): pl.pallas_call(attention_kernel, grid=(steps,), out_shape=(jax.ShapeDtype...  15.5 us
  transfers between devices with their start and end apart: 2, of which 0 were waited for; matrix products, arithmetic and copies ran while one was open for 8% of the time, Pallas kernels for 41%

profile of v2, /device:TPU:0, one launch (start us, length us, event | category | flops | bytes accessed | tf_op | source)
XLA Modules:
  0.0 588.2 jit_solution(5555468536036934076)
XLA Ops:
  7.2 2.3 copy.50
  9.5 1.2 copy-done.4
  10.7 1.2 copy-done.5
  11.9 1.2 copy-done.6
  13.2 1.1 copy-done.10
  14.3 1.2 copy-done.15
  15.5 130.5 %shard_map.160 = (bf16[32,96,4096]{2,1,0:T(8,128)(2,1)}, f32[3072,128]{1,0:T(8,128)S(1)}, f32[3072,128]{1,0:T(8,128)S(1)}, bf16[3072,128]{1,0:T(8,128)(2,1)S(1)}, bf16[8,128,4096]{2,1,0:T(8,128)(2,1)}) custom-call(bf16[96,4096]{1,0:T(8,128)(2,1)S(1)} %bitcast.60, bf16[4096,128]{1,0:T(8,128)(2,1)S(1)} %copy-done.5, bf16[4096,128]{1,0:T(8,128)(2,1)S(1)} %copy-done.6, ...), custom_call_target="tpu_custom_call" | custom-call | tf_op jit(solution)/shard_map/pallas_call | solution.py:112
  146.0 0.9 copy-done.22
  147.0 1.0 copy-done.7
  148.2 2.3 copy.48
  150.5 2.3 copy.49
  152.7 1.7 copy.37
  154.4 0.6 convert_element_type.51
  155.0 1.7 copy.38
  156.7 0.9 multiply_reduce_fusion.5
  157.6 13.8 %shard_map.161 = f32[48,128]{1,0:T(8,128)S(1)} custom-call(f32[48,128]{1,0:T(8,128)S(1)} %pad_maximum_fusion.8.x_ref), custom_call_target="tpu_custom_call" | custom-call | tf_op jit(solution)/shard_map/pallas_call | solution.py:112
  171.6 0.3 multiply_multiply_fusion
  171.9 0.2 copy-done.41
  172.1 0.8 copy-done.25
  173.0 0.3 multiply_multiply_fusion.1
  173.3 4.1 subtract_convert_fusion
  177.5 0.4 copy.40.k_ref
  177.9 1.4 pad_maximum_fusion.5
  179.2 0.4 copy.39.q_ref
  179.7 15.5 %shard_map.162 = (bf16[3072,128]{1,0:T(8,128)(2,1)S(1)}, f32[1,3072]{1,0:T(1,128)S(1)}, f32[1,3072]{1,0:T(1,128)S(1)}) custom-call(bf16[3072,128]{1,0:T(8,128)(2,1)S(1)} %copy.39.q_ref, bf16[3072,128]{1,0:T(8,128)(2,1)S(1)} %copy.40.k_ref, bf16[3072,128]{1,0:T(8,128)(2,1)S(1)} %copy-done.23), custom_call_target="tpu_custom_call" | custom-call | flops 9663676416 | bytes 3145728 | tf_op jit(solution)/shard_map/pallas_call | solution.py:567
  195.2 18.5 %shard_map.163 = bf16[4,96,1024]{2,1,0:T(8,128)(2,1)S(1)} custom-call(bf16[4,4,2,96,128]{4,3,2,1,0:T(8,128)(2,1)S(1)} %bitcast.59), custom_call_target="tpu_custom_call" | custom-call | tf_op jit(solution)/shard_map/pallas_call | solution.py:112
  213.7 3.4 fusion.12.x_ref
  217.1 57.0 %shard_map.164 = f32[96,4096]{1,0:T(8,128)S(1)} custom-call(f32[4,96,4096]{2,1,0:T(8,128)S(1)} %fusion.12.x_ref), custom_call_target="tpu_custom_call" | custom-call | tf_op jit(solution)/shard_map/pallas_call | solution.py:112
  274.4 0.9 copy-done.33
  275.3 0.6 fusion.5
  276.0 1.5 fusion.4
  277.5 44.0 %shard_map.165 = (bf16[4,96,4096]{2,1,0:T(8,128)(2,1)S(1)}, bf16[2,96,4096]{2,1,0:T(8,128)(2,1)S(1)}) custom-call(bf16[96,4096]{1,0:T(8,128)(2,1)S(1)} %get-tuple-element.74.x_ref), custom_call_target="tpu_custom_call" | custom-call | tf_op jit(solution)/shard_map/pallas_call | solution.py:112
  321.4 1.1 copy-done.2
  323.0 1.6 copy-done.1
  324.6 2.3 copy.52
  326.9 6.0 %convolution_convert_fusion = bf16[384,1024]{1,0:T(8,128)(2,1)S(1)} fusion(bf16[384,4096]{1,0:T(8,128)(2,1)S(1)} %bitcast.56, bf16[1024,4096]{1,0:T(8,128)(2,1)} %bitcast.78), kind=kOutput, calls=%fused_computation.25 | convolution fusion | flops 3221618688 | bytes 12320768 | tf_op jit(solution)/shard_map/dot_general | solution.py:502
  333.0 18.6 %shard_map.166 = bf16[4,4,2,96,128]{4,3,2,1,0:T(8,128)(2,1)S(1)} custom-call(bf16[4,96,1024]{2,1,0:T(8,128)(2,1)S(1)} %bitcast.65), custom_call_target="tpu_custom_call" | custom-call | tf_op jit(solution)/shard_map/pallas_call | solution.py:112
  351.6 23.0 %shard_map.167 = (f32[3072,128]{1,0:T(8,128)S(1)}, f32[3072,128]{1,0:T(8,128)}, bf16[3072,128]{1,0:T(8,128)(2,1)S(1)}) custom-call(bf16[3072,128]{1,0:T(8,128)(2,1)S(1)} %copy-done.21, bf16[3072,128]{1,0:T(8,128)(2,1)S(1)} %copy-done.19, bf16[3072,128]{1,0:T(8,128)(2,1)S(1)} %copy-done.24, bf16[3072,128]{1,0:T(8,128)(2,1)S(1)} %bitcast.64, ...), custom_call_target="tpu_custom_call" | custom-call | flops 24159191040 | bytes 7864320 | tf_op jit(solution)/shard_map/pallas_call | solution.py:630
  374.7 1.7 copy.43
  376.3 1.2 copy.51
  377.5 2.0 copy.45
  379.5 3.8 multiply_add_fusion.1
  383.3 1.2 multiply_reduce_fusion.1
  384.7 1.1 multiply_reduce_fusion
  385.9 20.7 %shard_map.168 = f32[80,128]{1,0:T(8,128)S(1)} custom-call(f32[80,128]{1,0:T(8,128)S(1)} %pad_maximum_fusion.7.x_ref), custom_call_target="tpu_custom_call" | custom-call | tf_op jit(solution)/shard_map/pallas_call | solution.py:112
  406.5 0.4 multiply_convert_fusion
  406.9 0.4 multiply_convert_fusion.1
  407.3 0.5 copy-done.29
  407.8 0.9 copy-done.31
  408.7 1.2 pad_maximum_fusion.4
  410.0 1.8 copy.47
  411.8 1.1 copy-done.13
  413.0 31.5 %shard_map.169 = (bf16[4,96,2048]{2,1,0:T(8,128)(2,1)S(1)}, bf16[4,96,1024]{2,1,0:T(8,128)(2,1)S(1)}, bf16[96,4096]{1,0:T(8,128)(2,1)S(1)}) custom-call(bf16[4,8,96,256]{3,2,1,0:T(8,128)(2,1)S(1)} %bitcast.57, bf16[4,8,96,128]{3,2,1,0:T(8,128)(2,1)S(1)} %bitcast.61, bf16[2,96,4096]{2,1,0:T(8,128)(2,1)S(1)} %copy-done.3), custom_call_target="tpu_custom_call" | custom-call | tf_op jit(solution)/shard_map/pallas_call | solution.py:112
  444.5 1.1 copy-done.14
  445.6 0.9 copy-done.16
  446.5 0.9 copy-done.17
  447.4 0.6 fusion.11
  448.0 1.6 pad_maximum_fusion.dw_ref
  449.5 124.1 %shard_map.172 = (f32[96,4096]{1,0:T(8,128)}, bf16[384,4096]{1,0:T(8,128)(2,1)}, bf16[128,4096]{1,0:T(8,128)(2,1)}) custom-call(bf16[384,2048]{1,0:T(8,128)(2,1)} %bitcast.62, bf16[384,1024]{1,0:T(8,128)(2,1)} %bitcast.63, bf16[2048,4096]{1,0:T(8,128)(2,1)} %all-gather.3.cloned.1.call-done.wqk_ref, bf16[1024,4096]{1,0:T(8,128)(2,1)} %all-gather.5.cloned.1.call-done.wv_ref, ...), custom_call_target="tpu_custom_call" | custom-call | tf_op jit(solution)/shard_map/pallas_call | solution.py:112
  573.7 2.6 fusion.8
  576.5 1.3 copy.55
  577.8 1.3 copy.54
  579.1 1.3 copy.53
  580.4 1.0 copy.57
  (113 shorter events, 1.7 us)
Async XLA Ops:
  7.2 442.3 %all-gather.5.cloned.1.call-start = ((), (), s32[]{:S(2)}) async-start(), calls=%async_computation.1 | async-start | bytes 9437184 | tf_op jit(solution)/shard_map/all_gather | solution.py:673
  9.5 1.2 copy-start.4
  10.7 1.2 copy-start.5
  11.9 1.2 copy-start.6
  13.2 1.1 copy-start.10
  14.3 1.2 copy-start.15
  15.5 131.4 %copy-start.8 = (bf16[4096,128]{0,1:T(8,128)(2,1)S(1)}, bf16[4096,128]{0,1:T(8,128)(2,1)}, u32[]{:S(2)}) copy-start(bf16[4096,128]{0,1:T(8,128)(2,1)} %copy.50) | copy-start | bytes 3145732
  146.0 0.9 copy-start.22
  147.0 1.0 copy-start.7
  148.0 301.6 %all-gather.3.cloned.1.call-start = ((), (), s32[]{:S(2)}) async-start(), calls=%async_computation | async-start | bytes 18874368 | tf_op jit(solution)/shard_map/all_gather | solution.py:702
  152.7 1.7 copy-start.49
  152.7 1.7 copy-start.50
  152.7 1.7 copy-start.44
  154.4 17.1 %copy-start.45 = (f32[128]{0:T(128)}, f32[128]{0:T(128)S(1)}, u32[]{:S(2)}) copy-start(f32[128]{0:T(128)S(1)} %convert_element_type.50) | copy-start | bytes 1540
  156.7 14.8 %copy-start.27 = (f32[3072,128]{0,1:T(8,128)S(1)}, f32[3072,128]{0,1:T(8,128)}, u32[]{:S(2)}) copy-start(f32[3072,128]{0,1:T(8,128)} %copy.38) | copy-start | bytes 4718596
  171.5 1.8 copy-start.47
  171.5 0.6 copy-start.41
  171.5 1.4 copy-start.25
  177.9 1.8 copy-start.18
  177.9 1.8 copy-start.23
  179.6 15.6 %copy-start.20 = (bf16[3072,128]{1,0:T(8,128)(2,1)}, bf16[3072,128]{1,0:T(8,128)(2,1)S(1)}, u32[]{:S(2)}) copy-start(bf16[3072,128]{1,0:T(8,128)(2,1)S(1)} %copy.39.q_ref) | copy-start | bytes 2359300
  179.6 34.1 %slice-start = ((s8[8388608]{0:T(1024)(128)(4,1)}), s8[4194304]{0:T(1024)(128)(4,1)S(1)}, s32[]{:S(2)}) async-start(s8[8388608]{0:T(1024)(128)(4,1)} %bitcast.79), calls=%async_computation.2 | async-start | bytes 8388608
  179.7 34.0 %slice-start.1 = ((s8[8388608]{0:T(1024)(128)(4,1)}), s8[4194304]{0:T(1024)(128)(4,1)S(1)}, s32[]{:S(2)}) async-start(s8[8388608]{0:T(1024)(128)(4,1)} %bitcast.79), calls=%async_computation.3 | async-start | bytes 8388608
  195.2 21.9 %copy-start.9 = (bf16[3072,128]{1,0:T(8,128)(2,1)}, bf16[3072,128]{1,0:T(8,128)(2,1)S(1)}, u32[]{:S(2)}) copy-start(bf16[3072,128]{1,0:T(8,128)(2,1)S(1)} %get-tuple-element.31) | copy-start | bytes 2359300
  274.2 1.1 copy-start.33
  274.2 1.1 copy-start.43
  274.4 1.5 copy-start.11
  276.0 46.6 %copy-start.36 = (bf16[4096,128]{0,1:T(8,128)(2,1)S(1)}, bf16[4096,128]{0,1:T(8,128)(2,1)}, u32[]{:S(2)}) copy-start(bf16[4096,128]{0,1:T(8,128)(2,1)} %copy.48) | copy-start | bytes 3145732
  276.0 46.6 %copy-start.37 = (bf16[4096,128]{0,1:T(8,128)(2,1)S(1)}, bf16[4096,128]{0,1:T(8,128)(2,1)}, u32[]{:S(2)}) copy-start(bf16[4096,128]{0,1:T(8,128)(2,1)} %copy.49) | copy-start | bytes 3145732
  321.4 1.1 copy-start.2
  322.6 4.3 copy-start
  322.9 1.6 copy-start.1
  326.9 24.7 %copy-start.24 = (bf16[3072,128]{1,0:T(8,128)(2,1)S(1)}, bf16[3072,128]{1,0:T(8,128)(2,1)}, u32[]{:S(2)}) copy-start(bf16[3072,128]{1,0:T(8,128)(2,1)} %copy-done.22) | copy-start | bytes 2359300
  332.9 18.7 %copy-start.19 = (bf16[3072,128]{1,0:T(8,128)(2,1)S(1)}, bf16[3072,128]{1,0:T(8,128)(2,1)}, u32[]{:S(2)}) copy-start(bf16[3072,128]{1,0:T(8,128)(2,1)} %copy-done.18) | copy-start | bytes 2359300
  333.0 18.7 %copy-start.21 = (bf16[3072,128]{1,0:T(8,128)(2,1)S(1)}, bf16[3072,128]{1,0:T(8,128)(2,1)}, u32[]{:S(2)}) copy-start(bf16[3072,128]{1,0:T(8,128)(2,1)} %copy-done.20) | copy-start | bytes 2359300
  374.7 1.7 copy-start.12
  377.5 2.0 copy-start.35
  377.5 2.0 copy-start.48
  379.5 3.8 copy-start.26
  383.3 1.4 copy-start.28
  383.3 1.4 copy-start.42
  383.3 1.4 copy-start.46
  406.9 0.9 copy-start.29
  407.8 0.9 copy-start.31
  410.0 1.9 copy-start.3
  411.8 1.1 copy-start.13
  413.0 35.0 %copy-start.30 = (bf16[3072,128]{0,1:T(8,128)(2,1)S(1)}, bf16[3072,128]{0,1:T(8,128)(2,1)}, u32[]{:S(2)}) copy-start(bf16[3072,128]{0,1:T(8,128)(2,1)} %copy-done.29) | copy-start | bytes 2359300
  413.0 35.0 %copy-start.32 = (bf16[3072,128]{0,1:T(8,128)(2,1)S(1)}, bf16[3072,128]{0,1:T(8,128)(2,1)}, u32[]{:S(2)}) copy-start(bf16[3072,128]{0,1:T(8,128)(2,1)} %copy-done.31) | copy-start | bytes 2359300
  413.0 35.0 %copy-start.38 = (bf16[3072,128]{0,1:T(8,128)(2,1)S(1)}, bf16[3072,128]{0,1:T(8,128)(2,1)}, u32[]{:S(2)}) copy-start(bf16[3072,128]{0,1:T(8,128)(2,1)} %copy.51) | copy-start | bytes 2359300
  444.5 1.1 copy-start.14
  445.6 0.9 copy-start.16
  446.5 0.9 copy-start.17
  449.5 124.1 %copy-start.34 = (bf16[1,96,4096]{2,1,0:T(8,128)(2,1)S(1)}, bf16[1,96,4096]{2,1,0:T(8,128)(2,1)}, u32[]{:S(2)}) copy-start(bf16[1,96,4096]{2,1,0:T(8,128)(2,1)} %param.17) | copy-start | bytes 2359300
  573.7 2.6 copy-start.39
  579.1 1.3 copy-start.40
Sparse Core Ops, SparseCore 0:
  148.1 55.4 all-gather.4
  324.7 93.0 all-gather.2

commit v3 on v2

--- a/solution.py
+++ b/solution.py
@@ -20,18 +20,17 @@
 def rope_tables(seq_len):
     half_dim = HEAD_SIZE // 2
     inv_freq = 1.0 / (ROPE_THETA ** (jnp.arange(half_dim, dtype=jnp.float32) / half_dim))
-    angles = jnp.arange(seq_len, dtype=jnp.float32)[:, None] * inv_freq[None, :]
+    angles = inv_freq[:, None] * jnp.arange(seq_len, dtype=jnp.float32)[None, :]
     return jnp.cos(angles), jnp.sin(angles)
 
 
 def rotate(values, cos_t, sin_t):
-    lower_half, upper_half = jnp.split(values, 2, axis=-1)
-    return jnp.concatenate([lower_half * cos_t - upper_half * sin_t, upper_half * cos_t + lower_half * sin_t], axis=-1)
+    lower_half, upper_half = jnp.split(values, 2, axis=0)
+    return jnp.concatenate([lower_half * cos_t - upper_half * sin_t, upper_half * cos_t + lower_half * sin_t], axis=0)
 
 
 def rotate_back(values, cos_t, sin_t):
-    lower_half, upper_half = jnp.split(values, 2, axis=-1)
-    return jnp.concatenate([lower_half * cos_t + upper_half * sin_t, upper_half * cos_t - lower_half * sin_t], axis=-1)
+    return rotate(values, cos_t, -sin_t)
 
 
 SEMAPHORES = 72
@@ -199,43 +198,48 @@
     return call(ring_sum_kernel, shape(dims, x.dtype), (x,), [VMEM], VMEM, [pltpu.VMEM(dims, x.dtype)] * 3, collective_id, 32)
 
 
-def spread_kernel(x_ref, ring_ref, near_ref, *sems):
+def spread_kernel(x_ref, w_ref, ring_ref, below_ref, w_out, *sems):
     me, copies = lax.axis_index('tp'), Copies(sems)
-    ring = [ring_peer(me, k) for k in range(1, 4)]
-    line = [line_peer(me, k) for k in (1, 3)]
-    greet(ring + line)
-    mine = position(me)[1]
-    started = [copies.send(x_ref, ring_ref.at[mine], peer) for peer in ring]
-    started += [copies.send(x_ref, near_ref.at[i], peer) for i, peer in enumerate(line)]
-    ring_ref[mine] = x_ref[...]
-    wait_all(started)
-
-
-def spread(x, collective_id):
-    out = (shape((4,) + x.shape, x.dtype), shape((2,) + x.shape, x.dtype))
-    return call(spread_kernel, out, (x,), [VMEM], (VMEM, VMEM), [], collective_id, 24)
-
-
-def plane_kernel(qk_ref, v_ref, near_ref, out_qk, out_v, far_ref, *sems):
+    _, c, core = position(me)
+    step1, step2 = ring_steps(c, core)
+    first, second = me + step1 * 2, me + step2 * 2
+    up, down = line_peer(me, 1), line_peer(me, 3)
+    greet([first, second, up, down])
+    forth = copies.send(x_ref, ring_ref.at[c], first)
+    started = [copies.send(x_ref, ring_ref.at[c], second), copies.send(x_ref, below_ref, up)]
+    held = copies.local(w_ref, w_out)
+    ring_ref[c] = x_ref[...]
+    forth.wait()
+    block = ring_ref.at[c + step1]
+    wait_all(started + [copies.send(block, block, second), held])
+
+
+def spread(x, w, collective_id):
+    outs = (shape((4,) + x.shape, x.dtype), shape(x.shape, x.dtype), shape(w.shape, w.dtype))
+    return call(spread_kernel, outs, (x, w), [VMEM, ANY], (VMEM, ANY, ANY), [], collective_id, 24)
+
+
+def plane_kernel(qk_ref, v_ref, below_ref, d_ref, out_qk, out_v, far_ref, above_ref, *sems):
     me, copies = lax.axis_index('tp'), Copies(sems)
     peers = [plane_peer(me, k) for k in range(1, 8)]
     up, down = line_peer(me, 1), line_peer(me, 3)
     greet(peers + [up, down])
     mine = me % 8
-    started = [copies.send(near_ref.at[0], far_ref, up)]
+    started = [copies.send(below_ref, far_ref, up), copies.send(d_ref, above_ref, down)]
     for src, dst in ((qk_ref, out_qk), (v_ref, out_v)):
         columns = part(mine, src.shape[-1])
         started += [copies.send(src.at[:, peer % 8], dst.at[:, :, columns], peer) for peer in peers]
-        dst[:, :, columns] = src[:, mine]
+        started.append(copies.local(src.at[:, mine], dst.at[:, :, columns]))
     wait_all(started)
 
 
-def plane_exchange(qk, v, near, collective_id):
-    outs = tuple(shape((4, a.shape[2], 8 * a.shape[3]), a.dtype) for a in (qk, v)) + (shape(near.shape[1:], near.dtype),)
-    return call(plane_kernel, outs, (qk, v, near), [VMEM, VMEM, ANY], (VMEM, VMEM, VMEM), [], collective_id, 24)
-
-
-def final_kernel(dqk_ref, dv_ref, wqk_ref, wv_ref, ring_ref, near_ref, far_ref, dw_ref, o_ref, x_ref, sum_ref, gw_ref, gwo_ref,
+def plane_exchange(qk, v, below, d, collective_id):
+    outs = tuple(shape((4, a.shape[2], 8 * a.shape[3]), a.dtype) for a in (qk, v)) + (shape(below.shape, below.dtype),) * 2
+    return call(plane_kernel, outs, (qk, v, below, d), [VMEM, VMEM, ANY, ANY], (ANY,) * 4, [], collective_id, 24)
+
+
+def final_kernel(dqk_ref, dv_ref, wqk_ref, wv_ref, ring_ref, below_ref, above_ref, far_ref, dw_ref, o_ref, dy_ref, x_ref,
+                 gx_ref, gwq_ref, gwk_ref, gwv_ref, gwo_ref,
                  dx, above, below, passing, full, buf, tile_sem, line_send, line_recv, *sems):
     me, copies = lax.axis_index('tp'), Copies(sems)
     z, c, core = position(me)
@@ -257,7 +261,7 @@
 
     for copy in fetch_w(0, 0):
         copy.start()
-    planes, lines = [z_down, z_up, z_far], [near_ref.at[0], near_ref.at[1], far_ref]
+    planes, lines = [z_down, z_up, z_far], [below_ref, above_ref, far_ref]
 
     def slot(plane, column):
         return full.at[plane * 8 + column * 2 + core]
@@ -320,7 +324,9 @@
 
         hop(j).wait()
         passing[:, part(j, TILE)] = passing[:, part(j, TILE)] + dx[z_up, :, part(j, TILE)]
-        gw_ref[:, part(j, TILE)] = nn(dw_ref[...], buf[b]).astype(gw_ref.dtype)
+        values = nn(dw_ref[...], buf[b]).T
+        for i, ref in enumerate((gwq_ref, gwk_ref, gwv_ref)):
+            ref[part(j, TILE), :] = values[:, i * HEAD_SIZE:(i + 1) * HEAD_SIZE].astype(ref.dtype)
         onward(j).start()
         return carry
 
@@ -334,7 +340,8 @@
         direct(j).wait()
         onward(j).wait()
         tile = part(j, TILE)
-        sum_ref[:, tile] = (dx[z, :, tile] + above[:, tile]) + below[:, tile]
+        total = (dx[z, :, tile] + above[:, tile]) + below[:, tile]
+        gx_ref[:, tile] = (total + dy_ref[:, tile].astype(jnp.float32)).astype(gx_ref.dtype)
         return carry
 
     lax.fori_loop(0, tiles, finish, 0)
@@ -348,7 +355,7 @@
     lax.fori_loop(0, tiles, out_grad, 0)
 
 
-def final(dqk, dv, wqk, wv, d_ring, d_near, d_far, dw_rows, o_rows, x_full, collective_id):
+def final(dqk, dv, wqk, wv, d_ring, d_below, d_above, d_far, dw_rows, o_rows, dy, x_full, collective_id):
     rows, model_dim = d_far.shape
     seq_len = x_full.shape[0]
     bf16, f32 = d_far.dtype, jnp.float32
@@ -356,14 +363,14 @@
     scratch = [pltpu.VMEM((dqk.shape[0] // rows, rows, model_dim), f32), block, block, block,
                pltpu.VMEM((seq_len // rows, rows, model_dim), bf16), pltpu.VMEM((2, seq_len, TILE), bf16), pltpu.SemaphoreType.DMA((2, 2)),
                pltpu.SemaphoreType.DMA((SEMAPHORES,)), pltpu.SemaphoreType.DMA((SEMAPHORES,))]
-    outs = (shape(d_far.shape, f32), shape((dw_rows.shape[0], model_dim), bf16), shape((o_rows.shape[0], model_dim), bf16))
-    return call(final_kernel, outs, (dqk, dv, wqk, wv, d_ring, d_near, d_far, dw_rows, o_rows, x_full),
-                [VMEM, VMEM, ANY, ANY, ANY, ANY, ANY, VMEM, VMEM, ANY], (VMEM, VMEM, VMEM),
+    outs = (shape(dy.shape, bf16),) + (shape((model_dim, HEAD_SIZE), bf16),) * 3 + (shape((o_rows.shape[0], model_dim), bf16),)
+    return call(final_kernel, outs, (dqk, dv, wqk, wv, d_ring, d_below, d_above, d_far, dw_rows, o_rows, dy, x_full),
+                [VMEM] * 2 + [ANY] * 6 + [VMEM] * 3 + [ANY], (VMEM,) * 5,
                 scratch, collective_id, 60)
 
 
-def gather_kernel(x_ref, wq_ref, wk_ref, wv_ref, wo_ref, out_ref, q_ref, k_ref, v_ref, col_ref,
-                  full, weights, total, *sems):
+def gather_kernel(x_ref, wq_ref, wk_ref, wv_ref, wo_ref, out_ref, q_ref, k_ref, v_ref, col_ref, wqk_rows, wv_rows,
+                  full, weights, rows_scr, qk_scr, total, *sems):
     me, copies = lax.axis_index('tp'), Copies(sems)
     z, c, core = position(me)
     partner = me + 1 - core * 2
@@ -433,8 +440,7 @@
             return carry
 
         lax.fori_loop(0, weights.shape[0] // DEPTH, chunk, 0)
-        q_ref[rows, :] = total[:, :HEAD_SIZE]
-        k_ref[rows, :] = total[:, HEAD_SIZE:2 * HEAD_SIZE]
+        qk_scr[rows, :] = total[:, :2 * HEAD_SIZE]
         v_ref[rows, :] = total[:, 2 * HEAD_SIZE:].astype(v_ref.dtype)
 
     def multiply_own(s):
@@ -457,6 +463,12 @@
     from_first(0)
     wait_all(loads)
     multiply_own(0)
+
+    def transpose(i, carry):
+        rows_scr[:, part(i, TILE)] = weights[part(i, TILE), :].T
+        return carry
+
+    lax.fori_loop(0, weights.shape[0] // TILE, transpose, 0)
     from_second(0)
     from_line(2)
     from_first(1)
@@ -464,6 +476,8 @@
     from_second(1)
     from_first(2)
     from_line(3)
+    stores.append(copies.local(rows_scr.at[pl.ds(0, 2 * HEAD_SIZE), :], wqk_rows))
+    stores.append(copies.local(rows_scr.at[pl.ds(2 * HEAD_SIZE, HEAD_SIZE), :], wv_rows))
     multiply_own(2)
     from_second(2)
     head_from_line(1)
@@ -483,6 +497,14 @@
     from_second(7)
     multiply_corner(2)
     multiply_corner(3)
+
+    def turn(i, carry):
+        values = qk_scr[part(i, TILE), :].T
+        q_ref[:, part(i, TILE)] = values[:HEAD_SIZE]
+        k_ref[:, part(i, TILE)] = values[HEAD_SIZE:]
+        return carry
+
+    lax.fori_loop(0, qk_scr.shape[0] // TILE, turn, 0)
     head_from_line(3)
     wait_all(stores + [own_head] + head_partner)
 
@@ -491,11 +513,12 @@
     rows, model_dim = x.shape
     f32 = jnp.float32
     head = (devices * rows, HEAD_SIZE)
-    outs = (shape((devices, rows, model_dim), x.dtype), shape(head, f32), shape(head, f32), shape(head, x.dtype),
-            shape((8,) + wo.shape, wo.dtype))
+    outs = (shape((devices, rows, model_dim), x.dtype), shape(head[::-1], f32), shape(head[::-1], f32), shape(head, x.dtype),
+            shape((8,) + wo.shape, wo.dtype), shape((2 * HEAD_SIZE, model_dim), x.dtype), shape((HEAD_SIZE, model_dim), x.dtype))
     width = 3 * HEAD_SIZE
-    scratch = [pltpu.VMEM((devices, rows, model_dim), x.dtype), pltpu.VMEM((model_dim, width), x.dtype), pltpu.VMEM((2 * rows, width), f32)]
-    return call(gather_kernel, outs, (x, wq, wk, wv, wo), [ANY] * 5, (ANY, VMEM, VMEM, VMEM, ANY), scratch, collective_id, 44)
+    scratch = [pltpu.VMEM((devices, rows, model_dim), x.dtype), pltpu.VMEM((model_dim, width), x.dtype),
+               pltpu.VMEM((width, model_dim), x.dtype), pltpu.VMEM((devices * rows, 2 * HEAD_SIZE), f32), pltpu.VMEM((2 * rows, width), f32)]
+    return call(gather_kernel, outs, (x, wq, wk, wv, wo), [ANY] * 5, (ANY, VMEM, VMEM, VMEM, ANY, ANY, ANY), scratch, collective_id, 62)
 
 
 def nt(a, b):
@@ -524,16 +547,16 @@
     return keys <= queries
 
 
-def attention_kernel(q_ref, k_ref, v_ref, o_ref, max_ref, inv_ref, s_scr, acc_scr):
+def attention_kernel(q_ref, k_ref, v_ref, o_ref, ot_ref, max_ref, inv_ref, s_scr, acc_scr):
     i = pl.program_id(0)
     q_blk = q_ref[...]
 
     def score(j, top):
-        s = nt(k_ref[block_rows(j), :], q_blk) * (ATTN_SCALE * LOG2E)
+        s = tn(k_ref[:, block_rows(j)], q_blk) * (ATTN_SCALE * LOG2E)
         s_scr[block_rows(j), :] = s
         return jnp.maximum(top, fold_rows(s, jnp.max))
 
-    s = jnp.where(diagonal_mask(), nt(k_ref[block_rows(i), :], q_blk) * (ATTN_SCALE * LOG2E), -1e30)
+    s = jnp.where(diagonal_mask(), tn(k_ref[:, block_rows(i)], q_blk) * (ATTN_SCALE * LOG2E), -1e30)
     s_scr[block_rows(i), :] = s
     top = lax.fori_loop(0, i, score, fold_rows(s, jnp.max))
     top = jnp.max(top, axis=0, keepdims=True)
@@ -556,28 +579,32 @@
 
     lax.fori_loop(0, i + 1, gather, 0)
     o_ref[...] = acc_scr[...].T.astype(jnp.bfloat16)
+    ot_ref[...] = acc_scr[...].astype(jnp.bfloat16)
 
 
 def attention(q, k, v):
-    seq_len = q.shape[0]
+    seq_len = v.shape[0]
     steps = seq_len // BLOCK
     rows = pl.BlockSpec((BLOCK, HEAD_SIZE), lambda i: (i, 0))
     whole = pl.BlockSpec((seq_len, HEAD_SIZE), lambda i: (0, 0))
     line = pl.BlockSpec((1, BLOCK), lambda i: (0, i))
+    columns = pl.BlockSpec((HEAD_SIZE, BLOCK), lambda i: (0, i))
+    wide = pl.BlockSpec((HEAD_SIZE, seq_len), lambda i: (0, 0))
     return pl.pallas_call(
         attention_kernel,
         grid=(steps,),
         out_shape=(jax.ShapeDtypeStruct((seq_len, HEAD_SIZE), jnp.bfloat16),
+                   jax.ShapeDtypeStruct((HEAD_SIZE, seq_len), jnp.bfloat16),
                    jax.ShapeDtypeStruct((1, seq_len), jnp.float32),
                    jax.ShapeDtypeStruct((1, seq_len), jnp.float32)),
-        in_specs=[rows, whole, whole], out_specs=(rows, line, line),
+        in_specs=[columns, wide, whole], out_specs=(rows, columns, line, line),
         scratch_shapes=[pltpu.VMEM((seq_len, BLOCK), jnp.float32), pltpu.VMEM((HEAD_SIZE, BLOCK), jnp.float32)],
         compiler_params=pltpu.CompilerParams(dimension_semantics=("arbitrary",), vmem_limit_bytes=40 << 20),
         cost_estimate=pl.CostEstimate(flops=8 * seq_len * seq_len * HEAD_SIZE, bytes_accessed=8 * seq_len * HEAD_SIZE, transcendentals=0),
     )(q, k, v)
 
 
-def attention_grad_kernel(q_ref, k_ref, v_ref, do_ref, max_ref, inv_ref, dq_ref, dk_ref, dv_ref, p_scr, dp_scr, dq_scr, dk_scr, dv_scr):
+def attention_grad_kernel(q_ref, k_ref, v_ref, do_ref, max_ref, inv_ref, dq_ref, dk_ref, dv_ref, dvt_ref, p_scr, dp_scr, dq_scr, dk_scr, dv_scr):
     i = pl.program_id(0)
     q_blk, do_blk = q_ref[...], do_ref[...]
     top, inv = max_ref[...], inv_ref[...]
@@ -589,7 +616,7 @@
 
     def scores(j, mask, delta):
         rows = block_rows(j)
-        s = nt(k_ref[rows, :], q_blk) * (ATTN_SCALE * LOG2E)
+        s = tn(k_ref[:, rows], q_blk) * (ATTN_SCALE * LOG2E)
         if mask is not None:
             s = jnp.where(mask, s, -1e30)
         p = jnp.exp2(s - top) * inv
@@ -607,33 +634,41 @@
     def grads(j, carry):
         rows = block_rows(j)
         ds = (p_scr[rows, :] * (dp_scr[rows, :] - delta) * ATTN_SCALE).astype(jnp.bfloat16)
-        dk_scr[rows, :] += nn(ds, q_blk)
-        dq_scr[...] += tn(k_ref[rows, :], ds)
+        dk_scr[:, rows] += nt(q_blk, ds)
+        dq_scr[...] += nn(k_ref[:, rows], ds)
         return carry
 
     lax.fori_loop(0, i + 1, grads, 0)
-    dq_ref[...] = dq_scr[...].T
+    dq_ref[...] = dq_scr[...]
 
     @pl.when(i == pl.num_programs(0) - 1)
     def _():
         dk_ref[...] = dk_scr[...]
         dv_ref[...] = dv_scr[...].astype(jnp.bfloat16)
 
+        def turn(j, carry):
+            dvt_ref[:, block_rows(j)] = dv_scr[block_rows(j), :].T.astype(jnp.bfloat16)
+            return carry
+
+        lax.fori_loop(0, pl.num_programs(0), turn, 0)
+
 
 def attention_grad(q, k, v, do, top, inv):
-    seq_len = q.shape[0]
+    seq_len = v.shape[0]
     steps = seq_len // BLOCK
     rows = pl.BlockSpec((BLOCK, HEAD_SIZE), lambda i: (i, 0))
     whole = pl.BlockSpec((seq_len, HEAD_SIZE), lambda i: (0, 0))
     line = pl.BlockSpec((1, BLOCK), lambda i: (0, i))
-    full = (seq_len, HEAD_SIZE)
+    columns = pl.BlockSpec((HEAD_SIZE, BLOCK), lambda i: (0, i))
+    wide = pl.BlockSpec((HEAD_SIZE, seq_len), lambda i: (0, 0))
+    full, turned = (seq_len, HEAD_SIZE), (HEAD_SIZE, seq_len)
     return pl.pallas_call(
         attention_grad_kernel,
         grid=(steps,),
-        out_shape=(jax.ShapeDtypeStruct(full, jnp.float32), jax.ShapeDtypeStruct(full, jnp.float32), jax.ShapeDtypeStruct(full, jnp.bfloat16)),
-        in_specs=[rows, whole, whole, rows, line, line], out_specs=(rows, whole, whole),
+        out_shape=(shape(turned, jnp.float32), shape(turned, jnp.float32), shape(full, jnp.bfloat16), shape(turned, jnp.bfloat16)),
+        in_specs=[columns, wide, whole, rows, line, line], out_specs=(columns, wide, whole, wide),
         scratch_shapes=[pltpu.VMEM((seq_len, BLOCK), jnp.float32), pltpu.VMEM((seq_len, BLOCK), jnp.float32),
-                        pltpu.VMEM((HEAD_SIZE, BLOCK), jnp.float32), pltpu.VMEM(full, jnp.float32), pltpu.VMEM(full, jnp.float32)],
+                        pltpu.VMEM((HEAD_SIZE, BLOCK), jnp.float32), pltpu.VMEM(turned, jnp.float32), pltpu.VMEM(full, jnp.float32)],
         compiler_params=pltpu.CompilerParams(dimension_semantics=("arbitrary",), vmem_limit_bytes=48 << 20),
         cost_estimate=pl.CostEstimate(flops=20 * seq_len * seq_len * HEAD_SIZE, bytes_accessed=20 * seq_len * HEAD_SIZE, transcendentals=0),
     )(q, k, v, do, top, inv)
@@ -641,21 +676,6 @@
 
 COLUMN_GROUPS = [[z * 8 + c * 2 + core for z in range(4) for core in range(2)] for c in range(4)]
 PLANE_GROUPS = [[z * 8 + p for p in range(8)] for z in range(4)]
-
-
-def after_kernel(value_ref, *refs):
-    refs[-1][...] = value_ref[...]
-
-
-def after(value, *others):
-    anywhere = pl.BlockSpec(memory_space=pl.ANY)
-    return pl.pallas_call(
-        after_kernel,
-        out_shape=jax.ShapeDtypeStruct(value.shape, value.dtype),
-        in_specs=[VMEM] + [anywhere] * len(others), out_specs=VMEM,
-        compiler_params=pltpu.CompilerParams(vmem_limit_bytes=8 << 20),
-        cost_estimate=pl.CostEstimate(flops=value.size, bytes_accessed=4 * value.size, transcendentals=0),
-    )(value, *others)
 
 
 def lane_rows(values):
@@ -666,21 +686,21 @@
     x_loc, dy_loc = x_loc[0], dy_loc[0]
     rows, model_dim = x_loc.shape
     bf16, f32 = jnp.bfloat16, jnp.float32
-    x_blocks, q_raw, k_raw, v_head, wo_blocks = gather(x_loc, wq_loc, wk_loc, wv_loc, wo_loc, 32, 9)
+    x_blocks, q_raw, k_raw, v_head, wo_blocks, wqk_rows, wv_rows = gather(x_loc, wq_loc, wk_loc, wv_loc, wo_loc, 32, 9)
     wo_col = wo_blocks.reshape(8 * HEAD_SIZE, model_dim)
     x_full = x_blocks.reshape(32 * rows, model_dim)
     seq_len = x_full.shape[0]
-    wv_plane = lax.all_gather(after(wv_loc.T, q_raw[:8]), 'tp', axis=0, tiled=True, axis_index_groups=PLANE_GROUPS)
+    wv_plane = lax.all_gather(wv_rows, 'tp', axis=0, tiled=True, axis_index_groups=PLANE_GROUPS)
     cos_t, sin_t = rope_tables(seq_len)
-    stats = jnp.concatenate([lane_rows(jnp.sum(q_raw * q_raw, axis=-1)), lane_rows(jnp.sum(k_raw * k_raw, axis=-1))])
+    stats = jnp.concatenate([lane_rows(jnp.sum(q_raw * q_raw, axis=0)), lane_rows(jnp.sum(k_raw * k_raw, axis=0))])
     sq_sums = all_sum(stats, 1).reshape(2, seq_len)
-    inv_rms = lax.rsqrt(sq_sums / model_dim + NORM_EPS)[..., None]
+    inv_rms = lax.rsqrt(sq_sums / model_dim + NORM_EPS)[:, None, :]
     q_unit = q_raw * inv_rms[0]
     k_unit = k_raw * inv_rms[1]
-    gq_f, gk_f = gq_loc.astype(f32), gk_loc.astype(f32)
+    gq_f, gk_f = gq_loc.astype(f32)[:, None], gk_loc.astype(f32)[:, None]
     q_rot = rotate(q_unit * gq_f, cos_t, sin_t).astype(bf16)
     k_rot = rotate(k_unit * gk_f, cos_t, sin_t).astype(bf16)
-    o_head, top, inv = attention(q_rot, k_rot, v_head)
+    o_head, o_rows, top, inv = attention(q_rot, k_rot, v_head)
 
     o_col = exchange(
         o_head.reshape(4, 4, 2, rows, HEAD_SIZE), (4, rows, 8 * HEAD_SIZE), column_peer, 8,
@@ -698,38 +718,37 @@
     g_normed = dy_f * ga_f
     d_attn = (post_rms * (g_normed - normed * jnp.mean(g_normed * normed, axis=-1, keepdims=True))).astype(bf16)
 
-    d_ring, d_near = spread(d_attn, 4)
-    wqk_plane = lax.all_gather(after(jnp.concatenate([wq_loc.T, wk_loc.T], axis=0), d_ring), 'tp', axis=0, tiled=True, axis_index_groups=PLANE_GROUPS)
+    d_ring, d_below, wqk_after = spread(d_attn, wqk_rows, 4)
+    wqk_plane = lax.all_gather(wqk_after, 'tp', axis=0, tiled=True, axis_index_groups=PLANE_GROUPS)
     d_col = nt(d_ring.reshape(4 * rows, model_dim), wo_col).astype(bf16)
     d_head = exchange(
         d_col.reshape(4, rows, 8 * HEAD_SIZE), (4, 4, 2, rows, HEAD_SIZE), column_peer, 8,
         lambda ref, d: ref.at[:, :, part(member_of(d), HEAD_SIZE)],
         lambda ref, d: ref.at[d // 8, :, d % 2], 5).reshape(seq_len, HEAD_SIZE)
 
-    dq_rot, dk_rot, d_value = attention_grad(q_rot, k_rot, v_head, d_head, top, inv)
+    dq_rot, dk_rot, d_value, d_value_rows = attention_grad(q_rot, k_rot, v_head, d_head, top, inv)
     dq_hat = rotate_back(dq_rot, cos_t, sin_t)
     dk_hat = rotate_back(dk_rot, cos_t, sin_t)
-    grad_gq = jnp.sum(dq_hat * q_unit, axis=0)
-    grad_gk = jnp.sum(dk_hat * k_unit, axis=0)
+    grad_gq = jnp.sum(dq_hat * q_unit, axis=1)
+    grad_gk = jnp.sum(dk_hat * k_unit, axis=1)
     dq_unit = dq_hat * gq_f
     dk_unit = dk_hat * gk_f
-    sums = jnp.concatenate([lane_rows(jnp.sum(dq_unit * q_unit, axis=-1)), lane_rows(jnp.sum(dk_unit * k_unit, axis=-1)), lane_rows(ga_part)])
+    sums = jnp.concatenate([lane_rows(jnp.sum(dq_unit * q_unit, axis=0)), lane_rows(jnp.sum(dk_unit * k_unit, axis=0)), lane_rows(ga_part)])
     sums = all_sum(sums, 6)
     dots_rows = 2 * seq_len // 128
-    unit_dots = sums[:dots_rows].reshape(2, seq_len)[..., None] / model_dim
+    unit_dots = sums[:dots_rows].reshape(2, seq_len)[:, None, :] / model_dim
     grad_ga = sums[dots_rows:].reshape(model_dim)
     dq_raw = (inv_rms[0] * (dq_unit - q_unit * unit_dots[0])).astype(bf16)
     dk_raw = (inv_rms[1] * (dk_unit - k_unit * unit_dots[1])).astype(bf16)
-    d_qk = jnp.concatenate([dq_raw, dk_raw], axis=1)
-    dw_rows = jnp.concatenate([dq_raw.T, dk_raw.T, d_value.T], axis=0)
-
-    dqk_plane, dv_plane, d_far = plane_exchange(
-        d_qk.reshape(4, 8, rows, 2 * HEAD_SIZE), d_value.reshape(4, 8, rows, HEAD_SIZE), d_near, 7)
-    dx_loc, grad_w, grad_wo = final(
+    dqk_rows = jnp.concatenate([dq_raw, dk_raw], axis=0)
+    d_qk = dqk_rows.T
+    dw_rows = jnp.concatenate([dqk_rows, d_value_rows], axis=0)
+
+    dqk_plane, dv_plane, d_far, d_above = plane_exchange(
+        d_qk.reshape(4, 8, rows, 2 * HEAD_SIZE), d_value.reshape(4, 8, rows, HEAD_SIZE), d_below, d_attn, 7)
+    grad_x, grad_wq, grad_wk, grad_wv, grad_wo = final(
         dqk_plane.reshape(4 * rows, 16 * HEAD_SIZE), dv_plane.reshape(4 * rows, 8 * HEAD_SIZE), wqk_plane, wv_plane,
-        d_ring, d_near, d_far, dw_rows, o_head.T, x_full, 8)
-    grad_x = (dx_loc + dy_f).astype(bf16)
-    grad_wq, grad_wk, grad_wv = [grad_w[i * HEAD_SIZE:(i + 1) * HEAD_SIZE].T for i in range(3)]
+        d_ring, d_below, d_above, d_far, dw_rows, o_rows, dy_loc, x_full, 8)
     return (y_loc[None], grad_x[None], grad_wq, grad_wk, grad_wv, grad_wo,
             grad_gq.astype(bf16), grad_gk.astype(bf16), grad_ga.astype(bf16))
 

time: 589 us -> 569 us (0.966)
  local copies, waits for them, and re-layouts: 44 us -> 21.3 us
    unnamed x113 -> x73, local copies, waits for them, and re-layouts: 30.2 us -> 19 us
    pallas_call x6 -> x0, local copies, waits for them, and re-layouts: 10.5 us -> none  [the longest x3 4.81 us: attention_grad(): pl.pallas_call(attention_grad_kernel, grid=(steps,), out_shape=(jax.Shape...]
    pallas_call x3 -> x1, Pallas kernels: 23.2 us -> 24.8 us  [attention_grad(): pl.pallas_call(attention_grad_kernel, grid=(steps,), out_shape=(shape(tur...]
  transfers between devices with their start and end apart: 2 -> 2, of which waited for: 0 -> 0; matrix products, arithmetic and copies ran while one was open for 8% -> 6% of each run, Pallas kernels for 41% -> 43%
where the time goes in v3:
time: 569 us
  Pallas kernels  502 us (88%)
  local copies, waits for them, and re-layouts  21.3 us (4%)
  other arithmetic  19.4 us (3%)
  between operations  14.6 us (3%)
  matrix products  11.5 us (2%)
    pallas_call x9, Pallas kernels, call(): pl.pallas_call(kernel, out_shape=out_shape, in_specs=in_specs, out_specs=...  461 us
    pallas_call x1, Pallas kernels, attention_grad(): pl.pallas_call(attention_grad_kernel, grid=(steps,), out_shape=(shape(tur...  24.8 us
    unnamed x73, local copies, waits for them, and re-layouts  19 us
    pallas_call x1, Pallas kernels, attention(): pl.pallas_call(attention_kernel, grid=(steps,), out_shape=(jax.ShapeDtype...  16.2 us
  transfers between devices with their start and end apart: 2, of which 0 were waited for; matrix products, arithmetic and copies ran while one was open for 6% of the time, Pallas kernels for 43%

profile of v3, /device:TPU:0, one launch (start us, length us, event | category | flops | bytes accessed | tf_op | source)
XLA Modules:
  0.0 568.8 jit_solution(16936316515863953144)
XLA Ops:
  7.2 0.0 all-gather.5.cloned.1.call-start
  7.2 131.9 %shard_map.160 = (bf16[32,96,4096]{2,1,0:T(8,128)(2,1)}, f32[128,3072]{1,0:T(8,128)}, f32[128,3072]{1,0:T(8,128)}, bf16[3072,128]{1,0:T(8,128)(2,1)}, bf16[8,128...) custom-call(bf16[96,4096]{1,0:T(8,128)(2,1)} %bitcast.52, bf16[4096,128]{1,0:T(8,128)(2,1)} %wq_ref.1, ...), custom_call_target="tpu_custom_call" | custom-call | tf_op jit(solution)/shard_map/pallas_call | solution.py:111
  139.1 0.0 all-gather.5.cloned.1.call-update
  139.2 0.0 all-gather.3.cloned.1.call-start
  139.2 0.0 copy-start.31
  139.3 1.7 multiply_reduce_fusion.5
  140.9 0.1 copy-done.15
  141.0 0.1 multiply_reduce_fusion.6
  141.2 12.4 %shard_map.161 = f32[48,128]{1,0:T(8,128)S(1)} custom-call(f32[48,128]{1,0:T(8,128)S(1)} %pad_maximum_fusion.6.x_ref), custom_call_target="tpu_custom_call" | custom-call | tf_op jit(solution)/shard_map/pallas_call | solution.py:111
  153.5 0.0 copy-done.31
  153.6 0.3 multiply_multiply_fusion
  153.9 0.3 multiply_multiply_fusion.1
  154.2 3.7 subtract_convert_fusion
  157.9 0.0 copy-start.13
  157.9 0.1 pad_maximum_fusion.3.q_ref
  158.0 0.1 pad_maximum_fusion.4.k_ref
  158.1 0.0 slice-start
  158.1 1.0 copy-done.13
  159.1 16.2 %shard_map.162 = (bf16[3072,128]{1,0:T(8,128)(2,1)S(1)}, bf16[128,3072]{1,0:T(8,128)(2,1)S(1)}, f32[1,3072]{1,0:T(1,128)S(1)}, f32[1,3072]{1,0:T(1,128)S(1)}) custom-call(bf16[128,3072]{1,0:T(8,128)(2,1)S(1)} %pad_maximum_fusion.3.q_ref, bf16[128,3072]{1,0:T(8,128)(2,1)S(1)} %pad_maximum_fusion.4.k_ref, bf16[3072,128]{1,0:T(8,128)(2,1)S(1)} %copy-done.13), custom_call_target="tpu_custom_call" | custom-call | flops 9663676416 | bytes 3145728 | tf_op jit(solution)/shard_map/pallas_call | solution.py:593
  175.3 18.1 %shard_map.163 = bf16[4,96,1024]{2,1,0:T(8,128)(2,1)S(1)} custom-call(bf16[4,4,2,96,128]{4,3,2,1,0:T(8,128)(2,1)S(1)} %bitcast.47), custom_call_target="tpu_custom_call" | custom-call | tf_op jit(solution)/shard_map/pallas_call | solution.py:111
  193.4 0.0 slice-done
  193.4 0.0 slice-done.1
  193.4 3.4 fusion.11.x_ref
  196.8 0.0 copy-start.29
  196.8 56.6 %shard_map.164 = f32[96,4096]{1,0:T(8,128)S(1)} custom-call(f32[4,96,4096]{2,1,0:T(8,128)S(1)} %fusion.11.x_ref), custom_call_target="tpu_custom_call" | custom-call | tf_op jit(solution)/shard_map/pallas_call | solution.py:111
  253.5 0.0 copy-start.19
  253.5 0.2 multiply_reduce_fusion.4
  253.7 0.9 copy-done.19
  254.6 0.6 fusion.5
  255.3 1.5 fusion.4
  256.7 0.2 copy-done.3
  256.9 37.7 %shard_map.165 = (bf16[4,96,4096]{2,1,0:T(8,128)(2,1)S(1)}, bf16[96,4096]{1,0:T(8,128)(2,1)S(1)}, bf16[256,4096]{1,0:T(8,128)(2,1)S(1)}) custom-call(bf16[96,4096]{1,0:T(8,128)(2,1)S(1)} %get-tuple-element.69.x_ref.d_ref, bf16[256,4096]{1,0:T(8,128)(2,1)S(1)} %copy-done.3), custom_call_target="tpu_custom_call" | custom-call | tf_op jit(solution)/shard_map/pallas_call | solution.py:111
  294.6 1.6 copy-done.1
  296.3 1.4 copy-done.2
  297.6 0.0 all-gather.3.cloned.1.call-update
  297.7 8.0 %convolution_convert_fusion = bf16[384,1024]{1,0:T(8,128)(2,1)S(1)} fusion(bf16[384,4096]{1,0:T(8,128)(2,1)} %bitcast.43, bf16[1024,4096]{1,0:T(8,128)(2,1)} %bitcast.59), kind=kOutput, calls=%fused_computation.22 | convolution fusion | flops 3221618688 | bytes 12320768 | tf_op jit(solution)/shard_map/dot_general | solution.py:525
  305.7 16.8 %shard_map.166 = bf16[4,4,2,96,128]{4,3,2,1,0:T(8,128)(2,1)S(1)} custom-call(bf16[4,96,1024]{2,1,0:T(8,128)(2,1)S(1)} %bitcast.48), custom_call_target="tpu_custom_call" | custom-call | tf_op jit(solution)/shard_map/pallas_call | solution.py:111
  322.5 24.8 %shard_map.167 = (f32[128,3072]{1,0:T(8,128)}, f32[128,3072]{1,0:T(8,128)}, bf16[3072,128]{1,0:T(8,128)(2,1)S(1)}, bf16[128,3072]{1,0:T(8,128)(2,1)S(1)}) custom-call(bf16[128,3072]{1,0:T(8,128)(2,1)S(1)} %pad_maximum_fusion.3.q_ref, bf16[128,3072]{1,0:T(8,128)(2,1)S(1)} %pad_maximum_fusion.4.k_ref, bf16[3072,128]{1,0:T(8,128)(2,1)S(1)} %copy-done.14, ...), custom_call_target="tpu_custom_call" | custom-call | flops 24159191040 | bytes 7864320 | tf_op jit(solution)/shard_map/pallas_call | solution.py:665
  347.4 5.7 multiply_subtract_fusion.1
  353.1 1.7 multiply_reduce_fusion
  354.8 20.6 %shard_map.168 = f32[80,128]{1,0:T(8,128)S(1)} custom-call(f32[80,128]{1,0:T(8,128)S(1)} %pad_maximum_fusion.5.x_ref), custom_call_target="tpu_custom_call" | custom-call | tf_op jit(solution)/shard_map/pallas_call | solution.py:111
  375.4 0.4 multiply_convert_fusion
  375.8 0.3 multiply_convert_fusion.1
  376.1 0.5 copy-done.20
  376.7 0.9 copy-done.22
  377.6 1.3 maximum_bitcast_fusion
  378.8 1.7 copy.19
  380.6 0.0 copy-start.12
  380.6 1.1 copy-done.12
  381.7 40.0 %shard_map.169 = (bf16[4,96,2048]{2,1,0:T(8,128)(2,1)S(1)}, bf16[4,96,1024]{2,1,0:T(8,128)(2,1)S(1)}, bf16[96,4096]{1,0:T(8,128)(2,1)S(1)}, bf16[96,4096]{1,0:T(8,128)(2,1)S(1)}) custom-call(bf16[4,8,96,256]{3,2,1,0:T(8,128)(2,1)S(1)} %bitcast.42, bf16[4,8,96,128]{3,2,1,0:T(8,128)(2,1)S(1)} %bitcast.49, bf16[96,4096]{1,0:T(8,128)(2,1)S(1)} %get-tuple-element.48.below_ref, ...), custom_call_target="tpu_custom_call" | custom-call | tf_op jit(solution)/shard_map/pallas_call | solution.py:111
  421.7 1.2 copy-done.4
  422.9 0.9 copy-done.6
  423.8 0.9 copy-done.7
  424.6 0.9 copy-done.8
  425.5 0.6 fusion.10
  426.1 1.6 pad_maximum_fusion.dw_ref
  427.7 126.9 %shard_map.170 = (bf16[96,4096]{1,0:T(8,128)(2,1)}, bf16[4096,128]{1,0:T(8,128)(2,1)}, bf16[4096,128]{1,0:T(8,128)(2,1)}, bf16[4096,128]{1,0:T(8,128)(2,1)}, bf16[128,4096]{1,0:T(8,128)(2,1)}) custom-call(bf16[384,2048]{1,0:T(8,128)(2,1)} %bitcast.44, bf16[384,1024]{1,0:T(8,128)(2,1)} %bitcast.45, bf16[2048,4096]{1,0:T(8,128)(2,1)} %all-gather.3.cloned.1.call-done.wqk_ref, ...), custom_call_target="tpu_custom_call" | custom-call | tf_op jit(solution)/shard_map/pallas_call | solution.py:111
  554.6 2.2 copy.25
  556.8 1.0 copy.26
  557.8 1.0 copy.27
  558.8 0.6 copy-done.26
  559.4 1.0 copy.28
  560.4 0.6 copy-done.25
  561.0 1.0 copy.29
  (59 shorter events, 0.2 us)
Async XLA Ops:
  7.2 420.5 %all-gather.5.cloned.1.call-start = ((), (), s32[]{:S(2)}) async-start(), calls=%async_computation.1 | async-start | bytes 9437184 | tf_op jit(solution)/shard_map/all_gather | solution.py:693
  7.2 132.0 %copy-start.30 = (bf16[128]{0:T(256)(128)(2,1)S(1)}, bf16[128]{0:T(256)(128)(2,1)}, u32[]{:S(2)}) copy-start(bf16[128]{0:T(256)(128)(2,1)} %param.15) | copy-start | bytes 772
  139.1 1.9 copy-start.15
  139.2 288.5 %all-gather.3.cloned.1.call-start = ((), (), s32[]{:S(2)}) async-start(), calls=%async_computation | async-start | bytes 18874368 | tf_op jit(solution)/shard_map/all_gather | solution.py:722
  139.2 14.3 %copy-start.31 = (bf16[128]{0:T(256)(128)(2,1)S(1)}, bf16[128]{0:T(256)(128)(2,1)}, u32[]{:S(2)}) copy-start(bf16[128]{0:T(256)(128)(2,1)} %param.14) | copy-start | bytes 772
  139.2 14.4 %copy-start.17 = (f32[128,3072]{1,0:T(8,128)S(1)}, f32[128,3072]{1,0:T(8,128)}, u32[]{:S(2)}) copy-start(f32[128,3072]{1,0:T(8,128)} %get-tuple-element.37) | copy-start | bytes 4718596
  157.9 1.1 copy-start.13
  158.1 35.3 %slice-start = ((s8[8388608]{0:T(1024)(128)(4,1)}), s8[4194304]{0:T(1024)(128)(4,1)S(1)}, s32[]{:S(2)}) async-start(s8[8388608]{0:T(1024)(128)(4,1)} %bitcast.60), calls=%async_computation.2 | async-start | bytes 8388608
  159.1 34.3 %slice-start.1 = ((s8[8388608]{0:T(1024)(128)(4,1)}), s8[4194304]{0:T(1024)(128)(4,1)S(1)}, s32[]{:S(2)}) async-start(s8[8388608]{0:T(1024)(128)(4,1)} %bitcast.60), calls=%async_computation.3 | async-start | bytes 8388608
  175.3 21.6 %copy-start.5 = (bf16[128,3072]{1,0:T(8,128)(2,1)}, bf16[128,3072]{1,0:T(8,128)(2,1)S(1)}, u32[]{:S(2)}) copy-start(bf16[128,3072]{1,0:T(8,128)(2,1)S(1)} %get-tuple-element.56.o_ref) | copy-start | bytes 2359300
  196.8 56.7 %copy-start.29 = (bf16[4096]{0:T(1024)(128)(2,1)S(1)}, bf16[4096]{0:T(1024)(128)(2,1)}, u32[]{:S(2)}) copy-start(bf16[4096]{0:T(1024)(128)(2,1)} %param.16) | copy-start | bytes 24580
  253.5 1.1 copy-start.19
  253.7 1.5 copy-start.24
  255.3 1.7 copy-start.3
  294.6 1.6 copy-start.1
  296.3 1.4 copy-start.2
  297.6 82.9 %copy-start = (bf16[96,4096]{1,0:T(8,128)(2,1)}, bf16[96,4096]{1,0:T(8,128)(2,1)S(1)}, u32[]{:S(2)}) copy-start(bf16[96,4096]{1,0:T(8,128)(2,1)S(1)} %get-tuple-element.48.below_ref) | copy-start | bytes 2359300
  305.7 16.8 %copy-start.14 = (bf16[3072,128]{1,0:T(8,128)(2,1)S(1)}, bf16[3072,128]{1,0:T(8,128)(2,1)}, u32[]{:S(2)}) copy-start(bf16[3072,128]{1,0:T(8,128)(2,1)} %get-tuple-element.38.v_ref) | copy-start | bytes 2359300
  347.4 5.7 %copy-start.9 = (bf16[128,3072]{1,0:T(8,128)(2,1)}, bf16[128,3072]{1,0:T(8,128)(2,1)S(1)}, u32[]{:S(2)}) copy-start(bf16[128,3072]{1,0:T(8,128)(2,1)S(1)} %get-tuple-element.55) | copy-start | bytes 2359300
  347.4 5.7 %copy-start.11 = (bf16[3072,128]{1,0:T(8,128)(2,1)}, bf16[3072,128]{1,0:T(8,128)(2,1)S(1)}, u32[]{:S(2)}) copy-start(bf16[3072,128]{1,0:T(8,128)(2,1)S(1)} %get-tuple-element.47) | copy-start | bytes 2359300
  347.4 5.7 %copy-start.16 = (f32[128,3072]{1,0:T(8,128)S(1)}, f32[128,3072]{1,0:T(8,128)}, u32[]{:S(2)}) copy-start(f32[128,3072]{1,0:T(8,128)} %get-tuple-element.36) | copy-start | bytes 4718596
  347.4 5.7 %copy-start.18 = (f32[128,3072]{1,0:T(8,128)S(1)}, f32[128,3072]{1,0:T(8,128)}, u32[]{:S(2)}) copy-start(f32[128,3072]{1,0:T(8,128)} %get-tuple-element.37) | copy-start | bytes 4718596
  375.8 0.9 copy-start.20
  376.7 0.9 copy-start.22
  380.6 1.1 copy-start.12
  381.7 44.4 %copy-start.10 = (bf16[128,3072]{1,0:T(8,128)(2,1)S(1)}, bf16[128,3072]{1,0:T(8,128)(2,1)}, u32[]{:S(2)}) copy-start(bf16[128,3072]{1,0:T(8,128)(2,1)} %copy-done.9) | copy-start | bytes 2359300
  381.7 44.4 %copy-start.21 = (bf16[128,3072]{1,0:T(8,128)(2,1)S(1)}, bf16[128,3072]{1,0:T(8,128)(2,1)}, u32[]{:S(2)}) copy-start(bf16[128,3072]{1,0:T(8,128)(2,1)} %copy-done.20) | copy-start | bytes 2359300
  381.7 44.4 %copy-start.23 = (bf16[128,3072]{1,0:T(8,128)(2,1)S(1)}, bf16[128,3072]{1,0:T(8,128)(2,1)}, u32[]{:S(2)}) copy-start(bf16[128,3072]{1,0:T(8,128)(2,1)} %copy-done.22) | copy-start | bytes 2359300
  421.7 1.2 copy-start.4
  422.9 0.9 copy-start.6
  423.7 0.9 copy-start.7
  424.6 0.9 copy-start.8
  554.6 2.2 copy-start.28
  554.6 3.2 copy-start.27
  557.8 1.6 copy-start.26
  559.4 1.6 copy-start.25
Sparse Core Ops, SparseCore 0:
  139.3 53.4 all-gather.4
  297.8 90.6 all-gather.2

commit v4 on v3

--- a/solution.py
+++ b/solution.py
@@ -56,11 +56,6 @@
 
 def plane_peer(me, k):
     return me - me % 8 + (me + k) % 8
-
-
-def ring_peer(me, k):
-    z, c, core = position(me)
-    return z * 8 + (c + k) % 4 * 2 + core
 
 
 def line_peer(me, k):
@@ -198,7 +193,7 @@
     return call(ring_sum_kernel, shape(dims, x.dtype), (x,), [VMEM], VMEM, [pltpu.VMEM(dims, x.dtype)] * 3, collective_id, 32)
 
 
-def spread_kernel(x_ref, w_ref, ring_ref, below_ref, w_out, *sems):
+def spread_kernel(x_ref, w_ref, ring_ref, below_ref, above_ref, w_out, *sems):
     me, copies = lax.axis_index('tp'), Copies(sems)
     _, c, core = position(me)
     step1, step2 = ring_steps(c, core)
@@ -206,7 +201,8 @@
     up, down = line_peer(me, 1), line_peer(me, 3)
     greet([first, second, up, down])
     forth = copies.send(x_ref, ring_ref.at[c], first)
-    started = [copies.send(x_ref, ring_ref.at[c], second), copies.send(x_ref, below_ref, up)]
+    started = [copies.send(x_ref, ring_ref.at[c], second), copies.send(x_ref, below_ref, up),
+               copies.send(x_ref.at[pl.ds(0, above_ref.shape[0]), :], above_ref, down)]
     held = copies.local(w_ref, w_out)
     ring_ref[c] = x_ref[...]
     forth.wait()
@@ -215,8 +211,9 @@
 
 
 def spread(x, w, collective_id):
-    outs = (shape((4,) + x.shape, x.dtype), shape(x.shape, x.dtype), shape(w.shape, w.dtype))
-    return call(spread_kernel, outs, (x, w), [VMEM, ANY], (VMEM, ANY, ANY), [], collective_id, 24)
+    half = shape((x.shape[0] // 2, x.shape[1]), x.dtype)
+    outs = (shape((4,) + x.shape, x.dtype), shape(x.shape, x.dtype), half, shape(w.shape, w.dtype))
+    return call(spread_kernel, outs, (x, w), [VMEM, ANY], (VMEM, ANY, ANY, ANY), [], collective_id, 24)
 
 
 def plane_kernel(qk_ref, v_ref, below_ref, d_ref, out_qk, out_v, far_ref, above_ref, *sems):
@@ -225,7 +222,7 @@
     up, down = line_peer(me, 1), line_peer(me, 3)
     greet(peers + [up, down])
     mine = me % 8
-    started = [copies.send(below_ref, far_ref, up), copies.send(d_ref, above_ref, down)]
+    started = [copies.send(below_ref, far_ref, up), copies.send(d_ref.at[pl.ds(above_ref.shape[0], above_ref.shape[0]), :], above_ref, down)]
     for src, dst in ((qk_ref, out_qk), (v_ref, out_v)):
         columns = part(mine, src.shape[-1])
         started += [copies.send(src.at[:, peer % 8], dst.at[:, :, columns], peer) for peer in peers]
@@ -234,11 +231,12 @@
 
 
 def plane_exchange(qk, v, below, d, collective_id):
-    outs = tuple(shape((4, a.shape[2], 8 * a.shape[3]), a.dtype) for a in (qk, v)) + (shape(below.shape, below.dtype),) * 2
-    return call(plane_kernel, outs, (qk, v, below, d), [VMEM, VMEM, ANY, ANY], (ANY,) * 4, [], collective_id, 24)
-
-
-def final_kernel(dqk_ref, dv_ref, wqk_ref, wv_ref, ring_ref, below_ref, above_ref, far_ref, dw_ref, o_ref, dy_ref, x_ref,
+    outs = tuple(shape((4, a.shape[2], 8 * a.shape[3]), a.dtype) for a in (qk, v)) + (
+        shape(below.shape, below.dtype), shape((d.shape[0] // 2, d.shape[1]), d.dtype))
+    return call(plane_kernel, outs, (qk, v, below, d), [VMEM, VMEM, ANY, ANY], (ANY,) * 4, [], collective_id, 62)
+
+
+def final_kernel(dqk_ref, dv_ref, wqk_ref, wv_ref, ring_ref, below_ref, top_ref, low_ref, far_ref, dwqk_ref, dwv_ref, o_ref, dy_ref, x_ref,
                  gx_ref, gwq_ref, gwk_ref, gwv_ref, gwo_ref,
                  dx, above, below, passing, full, buf, tile_sem, line_send, line_recv, *sems):
     me, copies = lax.axis_index('tp'), Copies(sems)
@@ -246,8 +244,9 @@
     partner = me + 1 - core * 2
     up, down = line_peer(me, 1), line_peer(me, 3)
     z_up, z_far, z_down = up // 8, line_peer(me, 2) // 8, down // 8
-    ring = [ring_peer(me, k) for k in range(1, 4)]
-    greet([up, down, partner] + ring)
+    step1, step2 = ring_steps(c, core)
+    first, second = me + step1 * 2, me + step2 * 2
+    greet([up, down, partner, first, second])
     tiles = x_ref.shape[1] // TILE
     depth = dqk_ref.shape[1]
     line_sems = (line_send, line_recv)
@@ -261,19 +260,27 @@
 
     for copy in fetch_w(0, 0):
         copy.start()
-    planes, lines = [z_down, z_up, z_far], [below_ref, above_ref, far_ref]
-
-    def slot(plane, column):
-        return full.at[plane * 8 + column * 2 + core]
-
-    rounds, shared, local = [], [], []
-    for plane, block in zip(planes, lines):
-        rounds += [copies.send(block, slot(plane, c), peer) for peer in ring]
-    held = [(block, slot(plane, c)) for plane, block in zip(planes, lines)]
-    held += [(ring_ref.at[column], slot(z, column)) for column in range(4)]
+    half = top_ref.shape[0]
+    whole = pl.ds(0, 2 * half)
+    pieces = [(z_down, whole, below_ref), (z_up, pl.ds(0, half), top_ref), (z_up, pl.ds(half, half), low_ref), (z_far, whole, far_ref)]
+
+    def spot(plane, column, rows):
+        return full.at[plane * 8 + column * 2 + core, rows, :]
+
+    to_first = [copies.send(block, spot(plane, c, rows), first) for plane, rows, block in pieces]
+    to_second = [copies.send(block, spot(plane, c, rows), second) for plane, rows, block in pieces]
+    to_corner, shared, local = [], [], []
+    held = [(block, spot(plane, c, rows)) for plane, rows, block in pieces]
+    held += [(ring_ref.at[column], spot(z, column, whole)) for column in range(4)]
     for block, place in held:
         shared.append(copies.send(block, place, partner))
         local.append(copies.local(block, place))
+
+    def pass_on(copy, plane, column, rows):
+        copy.wait()
+        block = spot(plane, column, rows)
+        shared.append(copies.send(block, block, partner))
+        return block
 
     def hop(j):
         return remote(dx.at[z_far, :, part(j, TILE)], passing.at[:, part(j, TILE)], line_sems, j, up)
@@ -324,17 +331,28 @@
 
         hop(j).wait()
         passing[:, part(j, TILE)] = passing[:, part(j, TILE)] + dx[z_up, :, part(j, TILE)]
-        values = nn(dw_ref[...], buf[b]).T
-        for i, ref in enumerate((gwq_ref, gwk_ref, gwv_ref)):
-            ref[part(j, TILE), :] = values[:, i * HEAD_SIZE:(i + 1) * HEAD_SIZE].astype(ref.dtype)
+        values = nn(dwqk_ref[...], buf[b]).T
+        gwq_ref[part(j, TILE), :] = values[:, :HEAD_SIZE].astype(gwq_ref.dtype)
+        gwk_ref[part(j, TILE), :] = values[:, HEAD_SIZE:].astype(gwk_ref.dtype)
+        gwv_ref[part(j, TILE), :] = nn(dwv_ref[...], buf[b]).T.astype(gwv_ref.dtype)
         onward(j).start()
         return carry
 
     lax.fori_loop(0, tiles, weight_grad, 0)
-    for i, copy in enumerate(rounds):
-        copy.wait()
-        block = slot(planes[i // 3], (c + 3 - i % 3) % 4)
-        shared.append(copies.send(block, block, partner))
+    for copy, (plane, rows, _) in zip(to_first, pieces):
+        block = pass_on(copy, plane, c + step1, rows)
+        to_corner.append(copies.send(block, block, second))
+    for column, arrivals in ((c + step2, to_second), (c + step1 + step2, to_corner)):
+        for copy, (plane, rows, _) in zip(arrivals, pieces):
+            pass_on(copy, plane, column, rows)
+    wait_all(local + shared)
+
+    def out_grad(j, carry):
+        d = full[:, :, part(j, TILE)]
+        gwo_ref[:, part(j, TILE)] = nn(o_ref[...], d.reshape(o_ref.shape[1], TILE)).astype(gwo_ref.dtype)
+        return carry
+
+    lax.fori_loop(0, tiles, out_grad, 0)
 
     def finish(j, carry):
         direct(j).wait()
@@ -345,17 +363,9 @@
         return carry
 
     lax.fori_loop(0, tiles, finish, 0)
-    wait_all(local + shared)
-
-    def out_grad(j, carry):
-        d = full[:, :, part(j, TILE)]
-        gwo_ref[:, part(j, TILE)] = nn(o_ref[...], d.reshape(o_ref.shape[1], TILE)).astype(gwo_ref.dtype)
-        return carry
-
-    lax.fori_loop(0, tiles, out_grad, 0)
-
-
-def final(dqk, dv, wqk, wv, d_ring, d_below, d_above, d_far, dw_rows, o_rows, dy, x_full, collective_id):
+
+
+def final(dqk, dv, wqk, wv, d_ring, d_below, d_top, d_low, d_far, dqk_rows, dv_rows, o_rows, dy, x_full, collective_id):
     rows, model_dim = d_far.shape
     seq_len = x_full.shape[0]
     bf16, f32 = d_far.dtype, jnp.float32
@@ -364,8 +374,8 @@
                pltpu.VMEM((seq_len // rows, rows, model_dim), bf16), pltpu.VMEM((2, seq_len, TILE), bf16), pltpu.SemaphoreType.DMA((2, 2)),
                pltpu.SemaphoreType.DMA((SEMAPHORES,)), pltpu.SemaphoreType.DMA((SEMAPHORES,))]
     outs = (shape(dy.shape, bf16),) + (shape((model_dim, HEAD_SIZE), bf16),) * 3 + (shape((o_rows.shape[0], model_dim), bf16),)
-    return call(final_kernel, outs, (dqk, dv, wqk, wv, d_ring, d_below, d_above, d_far, dw_rows, o_rows, dy, x_full),
-                [VMEM] * 2 + [ANY] * 6 + [VMEM] * 3 + [ANY], (VMEM,) * 5,
+    return call(final_kernel, outs, (dqk, dv, wqk, wv, d_ring, d_below, d_top, d_low, d_far, dqk_rows, dv_rows, o_rows, dy, x_full),
+                [VMEM] * 2 + [ANY] * 7 + [VMEM] * 4 + [ANY], (VMEM,) * 5,
                 scratch, collective_id, 60)
 
 
@@ -718,7 +728,7 @@
     g_normed = dy_f * ga_f
     d_attn = (post_rms * (g_normed - normed * jnp.mean(g_normed * normed, axis=-1, keepdims=True))).astype(bf16)
 
-    d_ring, d_below, wqk_after = spread(d_attn, wqk_rows, 4)
+    d_ring, d_below, d_top, wqk_after = spread(d_attn, wqk_rows, 4)
     wqk_plane = lax.all_gather(wqk_after, 'tp', axis=0, tiled=True, axis_index_groups=PLANE_GROUPS)
     d_col = nt(d_ring.reshape(4 * rows, model_dim), wo_col).astype(bf16)
     d_head = exchange(
@@ -742,13 +752,12 @@
     dk_raw = (inv_rms[1] * (dk_unit - k_unit * unit_dots[1])).astype(bf16)
     dqk_rows = jnp.concatenate([dq_raw, dk_raw], axis=0)
     d_qk = dqk_rows.T
-    dw_rows = jnp.concatenate([dqk_rows, d_value_rows], axis=0)
-
-    dqk_plane, dv_plane, d_far, d_above = plane_exchange(
+
+    dqk_plane, dv_plane, d_far, d_low = plane_exchange(
         d_qk.reshape(4, 8, rows, 2 * HEAD_SIZE), d_value.reshape(4, 8, rows, HEAD_SIZE), d_below, d_attn, 7)
     grad_x, grad_wq, grad_wk, grad_wv, grad_wo = final(
         dqk_plane.reshape(4 * rows, 16 * HEAD_SIZE), dv_plane.reshape(4 * rows, 8 * HEAD_SIZE), wqk_plane, wv_plane,
-        d_ring, d_below, d_above, d_far, dw_rows, o_rows, dy_loc, x_full, 8)
+        d_ring, d_below, d_top, d_low, d_far, dqk_rows, d_value_rows, o_rows, dy_loc, x_full, 8)
     return (y_loc[None], grad_x[None], grad_wq, grad_wk, grad_wv, grad_wo,
             grad_gq.astype(bf16), grad_gk.astype(bf16), grad_ga.astype(bf16))
 

time: 569 us -> 550 us (0.967)
  Pallas kernels: 502 us -> 491 us
  local copies, waits for them, and re-layouts: 21.3 us -> 15 us
    pallas_call x9, Pallas kernels: 461 us -> 449 us  [call(): pl.pallas_call(kernel, out_shape=out_shape, in_specs=in_specs, out_specs=...]
    unnamed x73 -> x53, local copies, waits for them, and re-layouts: 19 us -> 12.8 us
where the time goes in v4:
time: 550 us
  Pallas kernels  491 us (89%)
  other arithmetic  18.3 us (3%)
  local copies, waits for them, and re-layouts  15 us (3%)
  between operations  14.5 us (3%)
  matrix products  11.3 us (2%)
    pallas_call x9, Pallas kernels, call(): pl.pallas_call(kernel, out_shape=out_shape, in_specs=in_specs, out_specs=...  449 us
    pallas_call x1, Pallas kernels, attention_grad(): pl.pallas_call(attention_grad_kernel, grid=(steps,), out_shape=(shape(tur...  25.2 us
    pallas_call x1, Pallas kernels, attention(): pl.pallas_call(attention_kernel, grid=(steps,), out_shape=(jax.ShapeDtype...  16.1 us
    unnamed x53, local copies, waits for them, and re-layouts  12.8 us
  transfers between devices with their start and end apart: 2, of which 0 were waited for; matrix products, arithmetic and copies ran while one was open for 6% of the time, Pallas kernels for 43%

profile of v4, /device:TPU:0, one launch (start us, length us, event | category | flops | bytes accessed | tf_op | source)
XLA Modules:
  0.0 549.9 jit_solution(14166287914809340039)
XLA Ops:
  7.2 0.0 all-gather.5.cloned.1.call-start
  7.2 0.0 copy-start.20
  7.2 131.8 %shard_map.160 = (bf16[32,96,4096]{2,1,0:T(8,128)(2,1)}, f32[128,3072]{1,0:T(8,128)}, f32[128,3072]{1,0:T(8,128)}, bf16[3072,128]{1,0:T(8,128)(2,1)}, bf16[8,128...) custom-call(bf16[96,4096]{1,0:T(8,128)(2,1)} %bitcast.50, bf16[4096,128]{1,0:T(8,128)(2,1)} %wq_ref.1, ...), custom_call_target="tpu_custom_call" | custom-call | tf_op jit(solution)/shard_map/pallas_call | solution.py:106
  139.1 0.0 copy-start.9
  139.1 0.0 all-gather.5.cloned.1.call-update
  139.1 0.0 all-gather.3.cloned.1.call-start
  139.1 0.0 copy-done.20
  139.2 0.0 copy-start.21
  139.2 1.7 multiply_reduce_fusion.5
  140.9 0.1 copy-done.9
  140.9 0.1 multiply_reduce_fusion.6
  141.1 12.4 %shard_map.161 = f32[48,128]{1,0:T(8,128)S(1)} custom-call(f32[48,128]{1,0:T(8,128)S(1)} %pad_maximum_fusion.6.x_ref), custom_call_target="tpu_custom_call" | custom-call | tf_op jit(solution)/shard_map/pallas_call | solution.py:106
  153.6 0.3 multiply_multiply_fusion
  153.9 0.3 multiply_multiply_fusion.1
  154.2 3.7 subtract_convert_fusion
  157.9 0.1 pad_maximum_fusion.3.q_ref
  157.9 0.1 pad_maximum_fusion.4.k_ref
  158.0 0.0 slice-start
  158.0 1.0 copy-done.8
  159.0 16.1 %shard_map.162 = (bf16[3072,128]{1,0:T(8,128)(2,1)S(1)}, bf16[128,3072]{1,0:T(8,128)(2,1)S(1)}, f32[1,3072]{1,0:T(1,128)S(1)}, f32[1,3072]{1,0:T(1,128)S(1)}) custom-call(bf16[128,3072]{1,0:T(8,128)(2,1)S(1)} %pad_maximum_fusion.3.q_ref, bf16[128,3072]{1,0:T(8,128)(2,1)S(1)} %pad_maximum_fusion.4.k_ref, bf16[3072,128]{1,0:T(8,128)(2,1)S(1)} %copy-done.8), custom_call_target="tpu_custom_call" | custom-call | flops 9663676416 | bytes 3145728 | tf_op jit(solution)/shard_map/pallas_call | solution.py:603
  175.2 0.0 copy-start.4
  175.2 18.1 %shard_map.163 = bf16[4,96,1024]{2,1,0:T(8,128)(2,1)S(1)} custom-call(bf16[4,4,2,96,128]{4,3,2,1,0:T(8,128)(2,1)S(1)} %bitcast.44), custom_call_target="tpu_custom_call" | custom-call | tf_op jit(solution)/shard_map/pallas_call | solution.py:106
  193.3 0.0 slice-done
  193.3 0.0 slice-done.1
  193.3 3.5 fusion.12.x_ref
  196.8 0.0 copy-start.19
  196.8 56.6 %shard_map.164 = f32[96,4096]{1,0:T(8,128)S(1)} custom-call(f32[4,96,4096]{2,1,0:T(8,128)S(1)} %fusion.12.x_ref), custom_call_target="tpu_custom_call" | custom-call | tf_op jit(solution)/shard_map/pallas_call | solution.py:106
  253.5 0.0 copy-start.13
  253.5 0.2 multiply_reduce_fusion.4
  253.7 0.9 copy-done.13
  254.6 0.6 fusion.5
  255.3 0.0 copy-done.14
  255.3 0.0 copy-start.3
  255.3 1.5 fusion.4
  256.7 0.2 copy-done.3
  256.9 37.7 %shard_map.165 = (bf16[4,96,4096]{2,1,0:T(8,128)(2,1)S(1)}, bf16[96,4096]{1,0:T(8,128)(2,1)S(1)}, bf16[48,4096]{1,0:T(8,128)(2,1)S(1)}, bf16[256,4096]{1,0:T(8,128)(2,1)}) custom-call(bf16[96,4096]{1,0:T(8,128)(2,1)S(1)} %get-tuple-element.71.x_ref.d_ref, bf16[256,4096]{1,0:T(8,128)(2,1)S(1)} %copy-done.3), custom_call_target="tpu_custom_call" | custom-call | tf_op jit(solution)/shard_map/pallas_call | solution.py:106
  294.6 0.0 copy-start.1
  294.6 0.9 copy-done.1
  295.5 1.6 copy-done.2
  297.1 0.8 copy-done.7
  297.9 0.0 all-gather.3.cloned.1.call-update
  297.9 7.8 %convolution_convert_fusion = bf16[384,1024]{1,0:T(8,128)(2,1)S(1)} fusion(bf16[384,4096]{1,0:T(8,128)(2,1)} %bitcast.42, bf16[1024,4096]{1,0:T(8,128)(2,1)} %bitcast.59), kind=kOutput, calls=%fused_computation.21 | convolution fusion | flops 3221618688 | bytes 12320768 | tf_op jit(solution)/shard_map/dot_general | solution.py:535
  305.7 16.8 %shard_map.166 = bf16[4,4,2,96,128]{4,3,2,1,0:T(8,128)(2,1)S(1)} custom-call(bf16[4,96,1024]{2,1,0:T(8,128)(2,1)S(1)} %bitcast.45), custom_call_target="tpu_custom_call" | custom-call | tf_op jit(solution)/shard_map/pallas_call | solution.py:106
  322.5 25.2 %shard_map.167 = (f32[128,3072]{1,0:T(8,128)}, f32[128,3072]{1,0:T(8,128)}, bf16[3072,128]{1,0:T(8,128)(2,1)S(1)}, bf16[128,3072]{1,0:T(8,128)(2,1)S(1)}) custom-call(bf16[128,3072]{1,0:T(8,128)(2,1)S(1)} %pad_maximum_fusion.3.q_ref, bf16[128,3072]{1,0:T(8,128)(2,1)S(1)} %pad_maximum_fusion.4.k_ref, bf16[3072,128]{1,0:T(8,128)(2,1)S(1)} %copy-done.8, ...), custom_call_target="tpu_custom_call" | custom-call | flops 24159191040 | bytes 7864320 | tf_op jit(solution)/shard_map/pallas_call | solution.py:675
  347.7 5.7 %multiply_subtract_fusion.1 = (f32[64,3072]{1,0:T(8,128)S(1)}, f32[64,3072]{1,0:T(8,128)S(1)}, f32[64,3072]{1,0:T(8,128)S(1)}, f32[64,3072]{1,0:T(8,128)S(1)}) fusion(f32[128,3072]{1,0:T(8,128)} %get-tuple-element.46, f32[64]{0:T(128)S(1)} %negate_power_fusion, f32[128,3072]{1,0:T(8,128)} %get-tuple-element.47), kind=kLoop, calls=%fused_computation.30 | loop fusion | flops 2752512 | bytes 6291712 | tf_op jit(solution)/shard_map/sub | solution.py:29
  353.4 1.8 multiply_reduce_fusion
  355.3 20.6 %shard_map.168 = f32[80,128]{1,0:T(8,128)S(1)} custom-call(f32[80,128]{1,0:T(8,128)S(1)} %pad_maximum_fusion.5.x_ref), custom_call_target="tpu_custom_call" | custom-call | tf_op jit(solution)/shard_map/pallas_call | solution.py:106
  375.9 0.4 multiply_convert_fusion
  376.3 0.4 multiply_convert_fusion.1
  376.6 1.5 pad_maximum_fusion.2
  378.1 1.6 copy.19
  379.7 33.1 %shard_map.169 = (bf16[4,96,2048]{2,1,0:T(8,128)(2,1)}, bf16[4,96,1024]{2,1,0:T(8,128)(2,1)}, bf16[96,4096]{1,0:T(8,128)(2,1)}, bf16[48,4096]{1,0:T(8,128)(2,1)}) custom-call(bf16[4,8,96,256]{3,2,1,0:T(8,128)(2,1)} %bitcast.49, bf16[4,8,96,128]{3,2,1,0:T(8,128)(2,1)} %bitcast.46, bf16[96,4096]{1,0:T(8,128)(2,1)} %copy-done.1, bf16[96,4096]{1,0:T(8,128)(2,1)} %copy-done), custom_call_target="tpu_custom_call" | custom-call | tf_op jit(solution)/shard_map/pallas_call | solution.py:106
  412.9 0.6 fusion.10
  413.5 122.2 %shard_map.170 = (bf16[96,4096]{1,0:T(8,128)(2,1)}, bf16[4096,128]{1,0:T(8,128)(2,1)}, bf16[4096,128]{1,0:T(8,128)(2,1)}, bf16[4096,128]{1,0:T(8,128)(2,1)}, bf16[128,4096]{1,0:T(8,128)(2,1)}) custom-call(bf16[384,2048]{1,0:T(8,128)(2,1)} %bitcast.51, bf16[384,1024]{1,0:T(8,128)(2,1)} %bitcast.52, bf16[2048,4096]{1,0:T(8,128)(2,1)} %all-gather.3.cloned.1.call-done.wqk_ref, ...), custom_call_target="tpu_custom_call" | custom-call | tf_op jit(solution)/shard_map/pallas_call | solution.py:106
  535.7 0.0 copy-start.18
  535.7 0.0 copy-start.17
  535.7 2.2 copy.25
  537.9 0.0 copy-done.18
  537.9 1.0 copy.26
  538.9 1.0 copy.27
  539.9 0.6 copy-done.16
  540.5 1.0 copy.28
  541.5 0.6 copy-done.15
  542.1 1.0 copy.29
  (38 shorter events, 0.1 us)
Async XLA Ops:
  7.2 406.3 %all-gather.5.cloned.1.call-start = ((), (), s32[]{:S(2)}) async-start(), calls=%async_computation.1 | async-start | bytes 9437184 | tf_op jit(solution)/shard_map/all_gather | solution.py:703
  7.2 131.9 %copy-start.20 = (bf16[128]{0:T(256)(128)(2,1)S(1)}, bf16[128]{0:T(256)(128)(2,1)}, u32[]{:S(2)}) copy-start(bf16[128]{0:T(256)(128)(2,1)} %param.15) | copy-start | bytes 772
  139.1 1.9 copy-start.9
  139.1 274.4 %all-gather.3.cloned.1.call-start = ((), (), s32[]{:S(2)}) async-start(), calls=%async_computation | async-start | bytes 18874368 | tf_op jit(solution)/shard_map/all_gather | solution.py:732
  139.2 14.3 %copy-start.21 = (bf16[128]{0:T(256)(128)(2,1)S(1)}, bf16[128]{0:T(256)(128)(2,1)}, u32[]{:S(2)}) copy-start(bf16[128]{0:T(256)(128)(2,1)} %param.14) | copy-start | bytes 772
  139.2 14.4 %copy-start.11 = (f32[128,3072]{1,0:T(8,128)S(1)}, f32[128,3072]{1,0:T(8,128)}, u32[]{:S(2)}) copy-start(f32[128,3072]{1,0:T(8,128)} %get-tuple-element.38) | copy-start | bytes 4718596
  157.9 1.1 copy-start.8
  158.0 35.3 %slice-start = ((s8[8388608]{0:T(1024)(128)(4,1)}), s8[4194304]{0:T(1024)(128)(4,1)S(1)}, s32[]{:S(2)}) async-start(s8[8388608]{0:T(1024)(128)(4,1)} %bitcast.60), calls=%async_computation.2 | async-start | bytes 8388608
  159.0 34.3 %slice-start.1 = ((s8[8388608]{0:T(1024)(128)(4,1)}), s8[4194304]{0:T(1024)(128)(4,1)S(1)}, s32[]{:S(2)}) async-start(s8[8388608]{0:T(1024)(128)(4,1)} %bitcast.60), calls=%async_computation.3 | async-start | bytes 8388608
  175.2 21.6 %copy-start.4 = (bf16[128,3072]{1,0:T(8,128)(2,1)}, bf16[128,3072]{1,0:T(8,128)(2,1)S(1)}, u32[]{:S(2)}) copy-start(bf16[128,3072]{1,0:T(8,128)(2,1)S(1)} %get-tuple-element.58.o_ref) | copy-start | bytes 2359300
  196.8 56.7 %copy-start.19 = (bf16[4096]{0:T(1024)(128)(2,1)S(1)}, bf16[4096]{0:T(1024)(128)(2,1)}, u32[]{:S(2)}) copy-start(bf16[4096]{0:T(1024)(128)(2,1)} %param.16) | copy-start | bytes 24580
  253.5 1.1 copy-start.13
  253.7 1.6 copy-start.14
  255.3 1.6 copy-start.3
  256.7 41.2 %copy-start = (bf16[96,4096]{1,0:T(8,128)(2,1)}, bf16[96,4096]{1,0:T(8,128)(2,1)S(1)}, u32[]{:S(2)}) copy-start(bf16[96,4096]{1,0:T(8,128)(2,1)S(1)} %get-tuple-element.71.x_ref.d_ref) | copy-start | bytes 2359300
  294.6 0.9 copy-start.1
  295.5 1.6 copy-start.2
  297.1 0.8 copy-start.7
  347.7 5.7 %copy-start.5 = (bf16[128,3072]{1,0:T(8,128)(2,1)}, bf16[128,3072]{1,0:T(8,128)(2,1)S(1)}, u32[]{:S(2)}) copy-start(bf16[128,3072]{1,0:T(8,128)(2,1)S(1)} %get-tuple-element.57.dwv_ref) | copy-start | bytes 2359300
  347.7 5.7 %copy-start.6 = (bf16[3072,128]{1,0:T(8,128)(2,1)}, bf16[3072,128]{1,0:T(8,128)(2,1)S(1)}, u32[]{:S(2)}) copy-start(bf16[3072,128]{1,0:T(8,128)(2,1)S(1)} %get-tuple-element.48) | copy-start | bytes 2359300
  347.7 5.7 %copy-start.10 = (f32[128,3072]{1,0:T(8,128)S(1)}, f32[128,3072]{1,0:T(8,128)}, u32[]{:S(2)}) copy-start(f32[128,3072]{1,0:T(8,128)} %get-tuple-element.37) | copy-start | bytes 4718596
  347.7 5.7 %copy-start.12 = (f32[128,3072]{1,0:T(8,128)S(1)}, f32[128,3072]{1,0:T(8,128)}, u32[]{:S(2)}) copy-start(f32[128,3072]{1,0:T(8,128)} %get-tuple-element.38) | copy-start | bytes 4718596
  535.7 2.2 copy-start.18
  535.7 3.2 copy-start.17
  538.9 1.6 copy-start.16
  540.5 1.6 copy-start.15
Sparse Core Ops, SparseCore 0:
  139.2 53.4 all-gather.4
  298.0 90.6 all-gather.2

commit v5 on v4

--- a/solution.py
+++ b/solution.py
@@ -701,7 +701,7 @@
     x_full = x_blocks.reshape(32 * rows, model_dim)
     seq_len = x_full.shape[0]
     wv_plane = lax.all_gather(wv_rows, 'tp', axis=0, tiled=True, axis_index_groups=PLANE_GROUPS)
-    cos_t, sin_t = rope_tables(seq_len)
+    cos_t, sin_t = lax.optimization_barrier(rope_tables(seq_len))
     stats = jnp.concatenate([lane_rows(jnp.sum(q_raw * q_raw, axis=0)), lane_rows(jnp.sum(k_raw * k_raw, axis=0))])
     sq_sums = all_sum(stats, 1).reshape(2, seq_len)
     inv_rms = lax.rsqrt(sq_sums / model_dim + NORM_EPS)[:, None, :]

time: 550 us -> 547 us (level)
    unnamed x53 -> x61, local copies, waits for them, and re-layouts: 12.8 us -> 13 us
  transfers between devices with their start and end apart: 2 -> 2, of which waited for: 0 -> 0; matrix products, arithmetic and copies ran while one was open for 6% -> 5% of each run, Pallas kernels for 43% -> 44%
where the time goes in v5:
time: 547 us
  Pallas kernels  492 us (90%)
  local copies, waits for them, and re-layouts  15.2 us (3%)
  between operations  14.6 us (3%)
  other arithmetic  13.8 us (3%)
  matrix products  11.3 us (2%)
    pallas_call x9, Pallas kernels, call(): pl.pallas_call(kernel, out_shape=out_shape, in_specs=in_specs, out_specs=...  450 us
    pallas_call x1, Pallas kernels, attention_grad(): pl.pallas_call(attention_grad_kernel, grid=(steps,), out_shape=(shape(tur...  25.1 us
    pallas_call x1, Pallas kernels, attention(): pl.pallas_call(attention_kernel, grid=(steps,), out_shape=(jax.ShapeDtype...  16.2 us
    unnamed x61, local copies, waits for them, and re-layouts  13 us
  transfers between devices with their start and end apart: 2, of which 0 were waited for; matrix products, arithmetic and copies ran while one was open for 5% of the time, Pallas kernels for 44%

profile of v5, /device:TPU:0, one launch (start us, length us, event | category | flops | bytes accessed | tf_op | source)
XLA Modules:
  0.0 546.6 jit_solution(7911284598704126250)
XLA Ops:
  7.2 0.0 all-gather.5.cloned.1.call-start
  7.2 131.8 %shard_map.160 = (bf16[32,96,4096]{2,1,0:T(8,128)(2,1)}, f32[128,3072]{1,0:T(8,128)}, f32[128,3072]{1,0:T(8,128)}, bf16[3072,128]{1,0:T(8,128)(2,1)}, bf16[8,128...) custom-call(bf16[96,4096]{1,0:T(8,128)(2,1)} %bitcast.50, bf16[4096,128]{1,0:T(8,128)(2,1)} %wq_ref.1, ...), custom_call_target="tpu_custom_call" | custom-call | tf_op jit(solution)/shard_map/pallas_call | solution.py:106
  139.0 0.0 copy-start.24
  139.1 0.0 all-gather.5.cloned.1.call-update
  139.1 0.0 all-gather.3.cloned.1.call-start
  139.2 2.8 fusion.7
  142.0 0.0 copy-start.14
  142.0 0.0 copy-start.16
  142.0 0.0 copy-done.11
  142.0 0.0 copy-start.25
  142.0 0.1 multiply_reduce_fusion.5
  142.2 0.1 multiply_reduce_fusion.6
  142.3 12.4 %shard_map.161 = f32[48,128]{1,0:T(8,128)S(1)} custom-call(f32[48,128]{1,0:T(8,128)S(1)} %pad_maximum_fusion.6.x_ref), custom_call_target="tpu_custom_call" | custom-call | tf_op jit(solution)/shard_map/pallas_call | solution.py:106
  154.7 0.0 copy-done.25
  154.8 0.3 multiply_multiply_fusion
  155.1 0.3 multiply_multiply_fusion.1
  155.4 0.5 subtract_convert_fusion
  155.9 0.1 pad_maximum_fusion.3.q_ref
  156.0 0.1 pad_maximum_fusion.4.k_ref
  156.1 0.0 slice-start
  156.1 1.0 copy-done.8
  157.1 16.2 %shard_map.162 = (bf16[3072,128]{1,0:T(8,128)(2,1)S(1)}, bf16[128,3072]{1,0:T(8,128)(2,1)S(1)}, f32[1,3072]{1,0:T(1,128)S(1)}, f32[1,3072]{1,0:T(1,128)S(1)}) custom-call(bf16[128,3072]{1,0:T(8,128)(2,1)S(1)} %pad_maximum_fusion.3.q_ref, bf16[128,3072]{1,0:T(8,128)(2,1)S(1)} %pad_maximum_fusion.4.k_ref, bf16[3072,128]{1,0:T(8,128)(2,1)S(1)} %copy-done.8), custom_call_target="tpu_custom_call" | custom-call | flops 9663676416 | bytes 3145728 | tf_op jit(solution)/shard_map/pallas_call | solution.py:603
  173.3 18.1 %shard_map.163 = bf16[4,96,1024]{2,1,0:T(8,128)(2,1)S(1)} custom-call(bf16[4,4,2,96,128]{4,3,2,1,0:T(8,128)(2,1)S(1)} %bitcast.44), custom_call_target="tpu_custom_call" | custom-call | tf_op jit(solution)/shard_map/pallas_call | solution.py:106
  191.4 3.5 fusion.11.x_ref
  194.9 0.0 copy-start.23
  194.9 57.6 %shard_map.164 = f32[96,4096]{1,0:T(8,128)S(1)} custom-call(f32[4,96,4096]{2,1,0:T(8,128)S(1)} %fusion.11.x_ref), custom_call_target="tpu_custom_call" | custom-call | tf_op jit(solution)/shard_map/pallas_call | solution.py:106
  252.5 0.0 copy-start.13
  252.5 0.2 multiply_reduce_fusion.4
  252.7 0.9 copy-done.13
  253.6 0.6 fusion.5
  254.3 0.0 copy-start.3
  254.3 1.5 fusion.4
  255.8 0.1 copy-done.3
  255.9 37.7 %shard_map.165 = (bf16[4,96,4096]{2,1,0:T(8,128)(2,1)S(1)}, bf16[96,4096]{1,0:T(8,128)(2,1)S(1)}, bf16[48,4096]{1,0:T(8,128)(2,1)S(1)}, bf16[256,4096]{1,0:T(8,128)(2,1)}) custom-call(bf16[96,4096]{1,0:T(8,128)(2,1)S(1)} %get-tuple-element.83.x_ref.d_ref, bf16[256,4096]{1,0:T(8,128)(2,1)S(1)} %copy-done.3), custom_call_target="tpu_custom_call" | custom-call | tf_op jit(solution)/shard_map/pallas_call | solution.py:106
  293.6 0.0 copy-start.1
  293.6 0.9 copy-done.1
  294.5 1.7 copy-done.2
  296.1 0.7 copy-done.7
  296.9 0.0 all-gather.3.cloned.1.call-update
  296.9 7.8 %convolution_convert_fusion = bf16[384,1024]{1,0:T(8,128)(2,1)S(1)} fusion(bf16[384,4096]{1,0:T(8,128)(2,1)} %bitcast.42, bf16[1024,4096]{1,0:T(8,128)(2,1)} %bitcast.59), kind=kOutput, calls=%fused_computation.21 | convolution fusion | flops 3221618688 | bytes 12320768 | tf_op jit(solution)/shard_map/dot_general | solution.py:535
  304.7 16.8 %shard_map.166 = bf16[4,4,2,96,128]{4,3,2,1,0:T(8,128)(2,1)S(1)} custom-call(bf16[4,96,1024]{2,1,0:T(8,128)(2,1)S(1)} %bitcast.45), custom_call_target="tpu_custom_call" | custom-call | tf_op jit(solution)/shard_map/pallas_call | solution.py:106
  321.5 0.0 copy-start.15
  321.5 0.0 copy-start.17
  321.5 25.1 %shard_map.167 = (f32[128,3072]{1,0:T(8,128)}, f32[128,3072]{1,0:T(8,128)}, bf16[3072,128]{1,0:T(8,128)(2,1)S(1)}, bf16[128,3072]{1,0:T(8,128)(2,1)S(1)}) custom-call(bf16[128,3072]{1,0:T(8,128)(2,1)S(1)} %pad_maximum_fusion.3.q_ref, bf16[128,3072]{1,0:T(8,128)(2,1)S(1)} %pad_maximum_fusion.4.k_ref, bf16[3072,128]{1,0:T(8,128)(2,1)S(1)} %copy-done.8, ...), custom_call_target="tpu_custom_call" | custom-call | flops 24159191040 | bytes 7864320 | tf_op jit(solution)/shard_map/pallas_call | solution.py:675
  346.7 3.1 multiply_subtract_fusion.1
  349.8 0.3 copy-done.12
  350.0 1.8 multiply_reduce_fusion
  351.8 20.6 %shard_map.168 = f32[80,128]{1,0:T(8,128)S(1)} custom-call(f32[80,128]{1,0:T(8,128)S(1)} %pad_maximum_fusion.5.x_ref), custom_call_target="tpu_custom_call" | custom-call | tf_op jit(solution)/shard_map/pallas_call | solution.py:106
  372.4 0.4 multiply_convert_fusion
  372.8 0.4 multiply_convert_fusion.1
  373.2 1.5 pad_maximum_fusion.2
  374.7 1.6 copy.19
  376.3 34.4 %shard_map.169 = (bf16[4,96,2048]{2,1,0:T(8,128)(2,1)}, bf16[4,96,1024]{2,1,0:T(8,128)(2,1)}, bf16[96,4096]{1,0:T(8,128)(2,1)}, bf16[48,4096]{1,0:T(8,128)(2,1)}) custom-call(bf16[4,8,96,256]{3,2,1,0:T(8,128)(2,1)} %bitcast.49, bf16[4,8,96,128]{3,2,1,0:T(8,128)(2,1)} %bitcast.46, bf16[96,4096]{1,0:T(8,128)(2,1)} %copy-done.1, bf16[96,4096]{1,0:T(8,128)(2,1)} %copy-done), custom_call_target="tpu_custom_call" | custom-call | tf_op jit(solution)/shard_map/pallas_call | solution.py:106
  410.7 0.6 fusion.9
  411.3 121.0 %shard_map.170 = (bf16[96,4096]{1,0:T(8,128)(2,1)}, bf16[4096,128]{1,0:T(8,128)(2,1)}, bf16[4096,128]{1,0:T(8,128)(2,1)}, bf16[4096,128]{1,0:T(8,128)(2,1)}, bf16[128,4096]{1,0:T(8,128)(2,1)}) custom-call(bf16[384,2048]{1,0:T(8,128)(2,1)} %bitcast.51, bf16[384,1024]{1,0:T(8,128)(2,1)} %bitcast.52, bf16[2048,4096]{1,0:T(8,128)(2,1)} %all-gather.3.cloned.1.call-done.wqk_ref, ...), custom_call_target="tpu_custom_call" | custom-call | tf_op jit(solution)/shard_map/pallas_call | solution.py:106
  532.3 0.0 copy-start.22
  532.3 0.0 copy-start.21
  532.4 2.2 copy.25
  534.6 1.0 copy.26
  535.5 1.0 copy.27
  536.5 0.6 copy-done.20
  537.1 1.0 copy.28
  538.1 0.6 copy-done.19
  538.7 1.0 copy.29
  (47 shorter events, 0.1 us)
Async XLA Ops:
  7.2 404.1 %all-gather.5.cloned.1.call-start = ((), (), s32[]{:S(2)}) async-start(), calls=%async_computation.1 | async-start | bytes 9437184 | tf_op jit(solution)/shard_map/all_gather | solution.py:703
  139.0 3.0 copy-start.24
  139.1 3.0 copy-start.11
  139.1 272.2 %all-gather.3.cloned.1.call-start = ((), (), s32[]{:S(2)}) async-start(), calls=%async_computation | async-start | bytes 18874368 | tf_op jit(solution)/shard_map/all_gather | solution.py:732
  139.2 3.0 copy-start.9
  142.0 13.4 %copy-start.14 = (f32[64,3072]{1,0:T(8,128)}, f32[64,3072]{1,0:T(8,128)S(1)}, u32[]{:S(2)}) copy-start(f32[64,3072]{1,0:T(8,128)S(1)} %get-tuple-element.42) | copy-start | bytes 2359300
  142.0 13.4 %copy-start.16 = (f32[64,3072]{1,0:T(8,128)}, f32[64,3072]{1,0:T(8,128)S(1)}, u32[]{:S(2)}) copy-start(f32[64,3072]{1,0:T(8,128)S(1)} %get-tuple-element.41) | copy-start | bytes 2359300
  142.0 12.7 %copy-start.25 = (bf16[128]{0:T(256)(128)(2,1)S(1)}, bf16[128]{0:T(256)(128)(2,1)}, u32[]{:S(2)}) copy-start(bf16[128]{0:T(256)(128)(2,1)} %param.14) | copy-start | bytes 772
  155.9 1.1 copy-start.8
  156.1 35.3 %slice-start = ((s8[8388608]{0:T(1024)(128)(4,1)}), s8[4194304]{0:T(1024)(128)(4,1)S(1)}, s32[]{:S(2)}) async-start(s8[8388608]{0:T(1024)(128)(4,1)} %bitcast.60), calls=%async_computation.2 | async-start | bytes 8388608
  157.1 34.3 %slice-start.1 = ((s8[8388608]{0:T(1024)(128)(4,1)}), s8[4194304]{0:T(1024)(128)(4,1)S(1)}, s32[]{:S(2)}) async-start(s8[8388608]{0:T(1024)(128)(4,1)} %bitcast.60), calls=%async_computation.3 | async-start | bytes 8388608
  173.3 21.6 %copy-start.4 = (bf16[128,3072]{1,0:T(8,128)(2,1)}, bf16[128,3072]{1,0:T(8,128)(2,1)S(1)}, u32[]{:S(2)}) copy-start(bf16[128,3072]{1,0:T(8,128)(2,1)S(1)} %get-tuple-element.62.o_ref) | copy-start | bytes 2359300
  194.9 57.6 %copy-start.23 = (bf16[4096]{0:T(1024)(128)(2,1)S(1)}, bf16[4096]{0:T(1024)(128)(2,1)}, u32[]{:S(2)}) copy-start(bf16[4096]{0:T(1024)(128)(2,1)} %param.16) | copy-start | bytes 24580
  252.5 1.1 copy-start.13
  252.7 1.6 copy-start.18
  254.3 1.6 copy-start.3
  255.8 41.1 %copy-start = (bf16[96,4096]{1,0:T(8,128)(2,1)}, bf16[96,4096]{1,0:T(8,128)(2,1)S(1)}, u32[]{:S(2)}) copy-start(bf16[96,4096]{1,0:T(8,128)(2,1)S(1)} %get-tuple-element.83.x_ref.d_ref) | copy-start | bytes 2359300
  293.6 0.9 copy-start.1
  294.5 1.7 copy-start.2
  296.1 0.7 copy-start.7
  321.5 25.1 %copy-start.15 = (f32[64,3072]{1,0:T(8,128)S(1)}, f32[64,3072]{1,0:T(8,128)}, u32[]{:S(2)}) copy-start(f32[64,3072]{1,0:T(8,128)} %copy-done.14) | copy-start | bytes 2359300
  321.5 25.1 %copy-start.17 = (f32[64,3072]{1,0:T(8,128)S(1)}, f32[64,3072]{1,0:T(8,128)}, u32[]{:S(2)}) copy-start(f32[64,3072]{1,0:T(8,128)} %copy-done.16) | copy-start | bytes 2359300
  346.6 3.1 copy-start.5
  346.6 3.1 copy-start.6
  346.6 3.1 copy-start.10
  346.6 3.4 copy-start.12
  532.3 2.2 copy-start.22
  532.3 3.2 copy-start.21
  535.5 1.6 copy-start.20
  537.1 1.6 copy-start.19
Sparse Core Ops, SparseCore 0:
  139.2 53.3 all-gather.4
  297.0 101.2 all-gather.2
